TPU v7x, 32 devices: a whole 2x2x4 slice. The times are simulated.
32 devices in a mesh: pair: 2 (over core), dp: 16 (over z, y, x).
Axes of the slice: x: 2, y: 2, z: 4, core: 2. Of those that a mesh axis runs over, the one named last changes fastest.
Arguments:
- inputs: bfloat16 [2, 32, 512, 768], P('pair', 'dp'), may hold values from -6 to 6
- cotangent: bfloat16 [2, 32, 512, 768], P('pair', 'dp'), may hold values from -6 to 6
- span_lengths: int32 [2, 32, 4], P('pair', 'dp'), may hold values from 64 to 320, as said below
- pad_lengths: int32 [2, 32], P('pair', 'dp'), may hold values from 0 to 128, as said below
- pairing: int32 [2, 16, 8], P('pair', 'dp'), may hold values from 0 to 7, as said below
- owner_slot: int32 [108], replicated, may hold values from 0 to 111, as said below
- master: float32 [112, 256, 256], P('dp'), as said below
- first_moment: float32 [112, 256, 256], P('dp'), may hold values from -4 to 4
- second_moment: float32 [112, 256, 256], P('dp'), may hold values from 0.16 to 16
- left_basis: float32 [112, 256, 256], P('dp'), may hold values from -1 to 1
- right_basis: float32 [112, 256, 256], P('dp'), may hold values from -1 to 1
- vector_master: float32 [9216], replicated
- vector_first: float32 [9216], replicated, may hold values from -4 to 4
- vector_second: float32 [9216], replicated, may hold values from 0.16 to 16
Outputs:
- block_output: bfloat16 [2, 32, 512, 768], P('pair', 'dp')
- input_grad: float32 [2, 32, 512, 768], P('pair', 'dp')
- weight_grad: float32 [112, 256, 256], P('dp')
- new_master: float32 [112, 256, 256], P('dp')
- new_first: float32 [112, 256, 256], P('dp')
- new_second: float32 [112, 256, 256], P('dp')
- vector_grad: float32 [9216], replicated
- vector_state: float32 [3, 9216], replicated
Inputs may be any that keep to these rules, and one draw needn't show every extreme that they name: `span_lengths`: each row's spans come first in order and each has 64 tokens or more; the row's padding follows them; some span has exactly 320 tokens. `pad_lengths`: equals 512 minus the sum of the row's span lengths; some row has exactly 128, some row has none. For each dp index, pairing[0] is a permutation of the 8 spans of the partner device and pairing[1] is its inverse; spans are numbered row by row. `owner_slot`: distinct values; slot p belongs to dp index p // 7; every dp index holds at most 7 blocks and some hold exactly 7. `master`: slots that no block uses hold values that take part in no output but their own update.
All inputs are finite; a program needn't handle non-finite values.
Results may differ from a plain program's by a relative error of at most 0.012.
Values may be sent and summed in bfloat16 or wider, within the bound.
A program may use at most 256 MiB of HBM per device.

v0:
```python
import math

import jax
import jax.numpy as jnp
from jax import lax
from jax.sharding import PartitionSpec as P

D = 768
HEADS = 12
FF = 3072
SEGS = 4
STEP = 10


HIGHEST = lax.Precision.HIGHEST
BETA_ONE = 0.9
BETA_TWO = 0.95
ADAM_EPS = 1e-08
LR_MATRIX = 0.1
LR_VECTOR = 1.0
DECAY_RATE = 0.01
NORM_EPS = 1e-12
CLS_SCALE = 0.0625
CLS_WEIGHT = 4.0


def swapped(array, axis, stride):
    return lax.ppermute(array, axis, [(i, i ^ 1 << stride) for i in range(lax.axis_size(axis))])


def layer_norm(values, gain_vector, shift_vector):
    average = jnp.mean(values, axis=-1, keepdims=True)
    centered = values - average
    variance = jnp.mean(centered * centered, axis=-1, keepdims=True)
    return centered * lax.rsqrt(variance + NORM_EPS) * gain_vector + shift_vector


def gelu_exact(values):
    return jax.nn.gelu(values, approximate=False)


def split_vector(vector):
    pieces = [vector[index * D : (index + 1) * D] for index in range(8)]
    return tuple(pieces) + (vector[8 * D : 8 * D + FF],)


def tiled(stack, count_rows, count_cols):
    block_side = stack.shape[-1]
    return (
        stack.reshape(count_rows, count_cols, block_side, block_side)
        .transpose(0, 2, 1, 3)
        .reshape(count_rows * block_side, count_cols * block_side)
    )


def untiled(matrix, block_side):
    count_rows = matrix.shape[0] // block_side
    count_cols = matrix.shape[1] // block_side
    return (
        matrix.reshape(count_rows, block_side, count_cols, block_side)
        .transpose(0, 2, 1, 3)
        .reshape(count_rows * count_cols, block_side, block_side)
    )


def assemble(blocks):
    block_side = blocks.shape[-1]
    row_tiles = D // block_side
    wide_tiles = FF // block_side
    square = row_tiles * row_tiles
    wide_count = row_tiles * wide_tiles
    mats = [
        tiled(blocks[index * square : (index + 1) * square], row_tiles, row_tiles)
        for index in range(4)
    ]
    mats.append(tiled(blocks[4 * square : 4 * square + wide_count], row_tiles, wide_tiles))
    mats.append(
        tiled(blocks[4 * square + wide_count : 4 * square + 2 * wide_count], wide_tiles, row_tiles)
    )
    return tuple(mats)


def disassemble(mats, block_side):
    return jnp.concatenate([untiled(matrix, block_side) for matrix in mats], axis=0)


def soap_update(gradient, weight, moment_one, moment_two, left_basis, right_basis):
    rotated = jnp.matmul(
        jnp.matmul(jnp.swapaxes(left_basis, -1, -2), gradient, precision=HIGHEST),
        right_basis,
        precision=HIGHEST,
    )
    moment_one = BETA_ONE * moment_one + (1.0 - BETA_ONE) * rotated
    moment_two = BETA_TWO * moment_two + (1.0 - BETA_TWO) * rotated * rotated
    direction = (
        moment_one
        / (1.0 - BETA_ONE**STEP)
        / (jnp.sqrt(moment_two / (1.0 - BETA_TWO**STEP)) + ADAM_EPS)
    )
    restored = jnp.matmul(
        jnp.matmul(left_basis, direction, precision=HIGHEST),
        jnp.swapaxes(right_basis, -1, -2),
        precision=HIGHEST,
    )
    return (weight - LR_MATRIX * (restored + DECAY_RATE * weight), moment_one, moment_two)


def adam_update(gradient, weight, moment_one, moment_two):
    moment_one = BETA_ONE * moment_one + (1.0 - BETA_ONE) * gradient
    moment_two = BETA_TWO * moment_two + (1.0 - BETA_TWO) * gradient * gradient
    direction = (
        moment_one
        / (1.0 - BETA_ONE**STEP)
        / (jnp.sqrt(moment_two / (1.0 - BETA_TWO**STEP)) + ADAM_EPS)
    )
    return (weight - LR_VECTOR * direction, moment_one, moment_two)


def attend(query_row, key_row, segment_row):
    allowed = segment_row[:, None] == segment_row[None, :]
    logits = jnp.einsum("ihd,jhd->hij", query_row, key_row, preferred_element_type=jnp.float32)
    factor = 1.0 / math.sqrt(query_row.shape[-1])
    scores = jnp.where(allowed[None], logits * factor, -1e30)
    return (jax.nn.softmax(scores, axis=-1), allowed, factor)


def attend_forward(record):
    query_row, key_row, value_row, segment_row = record
    attn_probs, allowed, factor = attend(query_row, key_row, segment_row)
    return jnp.einsum(
        "hij,jhd->ihd",
        attn_probs.astype(jnp.bfloat16),
        value_row,
        preferred_element_type=jnp.float32,
    )


def attend_backward(record):
    query_row, key_row, value_row, segment_row, grad_row = record
    attn_probs, allowed, factor = attend(query_row, key_row, segment_row)
    probs_low = attn_probs.astype(jnp.bfloat16)
    grad_probs = jnp.einsum("ihd,jhd->hij", grad_row, value_row, preferred_element_type=jnp.float32)
    grad_value = jnp.einsum("hij,ihd->jhd", probs_low, grad_row, preferred_element_type=jnp.float32)
    grad_scores = attn_probs * (
        grad_probs - jnp.sum(attn_probs * grad_probs, axis=-1, keepdims=True)
    )
    grad_logits = jnp.where(allowed[None], grad_scores * factor, 0.0).astype(jnp.bfloat16)
    grad_query = jnp.einsum(
        "hij,jhd->ihd", grad_logits, key_row, preferred_element_type=jnp.float32
    )
    grad_key = jnp.einsum(
        "hij,ihd->jhd", grad_logits, query_row, preferred_element_type=jnp.float32
    )
    return (grad_query, grad_key, grad_value)


def per_device(
    inputs,
    cotangent,
    span_lengths,
    pad_lengths,
    pairing,
    owner_slot,
    master,
    first_moment,
    second_moment,
    left_basis,
    right_basis,
    vector_master,
    vector_first,
    vector_second,
):
    pair_count = lax.axis_size("pair")
    data_count = lax.axis_size("dp")
    grad_scale = 1.0 / (pair_count * data_count)
    block_side = master.shape[-1]
    gathered = lax.all_gather(master.astype(jnp.bfloat16), "dp", axis=0, tiled=True)
    w_query, w_key, w_value, w_output, w_inner, w_outer = assemble(
        jnp.take(gathered, owner_slot, axis=0)
    )
    (
        gain_one,
        shift_one,
        gain_two,
        shift_two,
        bias_query,
        bias_value,
        bias_output,
        bias_outer,
        bias_inner,
    ) = split_vector(vector_master)
    row_count = inputs.shape[1]
    seq_len = inputs.shape[2]
    token_count = row_count * seq_len
    heads_shape = (row_count, seq_len, HEADS, D // HEADS)
    flat_input = inputs.reshape(token_count, D)
    span_rows = span_lengths[0]
    pad_rows = pad_lengths[0]
    span_ends = jnp.cumsum(span_rows, axis=-1)
    span_starts = span_ends - span_rows
    positions = jnp.arange(seq_len, dtype=jnp.int32)
    inside = jnp.sum(
        (positions[None, :, None] >= span_ends[:, None, :-1]).astype(jnp.int32), axis=-1
    )
    segment_id = jnp.where(positions[None, :] >= seq_len - pad_rows[:, None], SEGS, inside)
    query_rows = (
        (jnp.dot(flat_input, w_query, preferred_element_type=jnp.float32) + bias_query)
        .astype(jnp.bfloat16)
        .reshape(heads_shape)
    )
    key_rows = (
        jnp.dot(flat_input, w_key, preferred_element_type=jnp.float32)
        .astype(jnp.bfloat16)
        .reshape(heads_shape)
    )
    value_rows = (
        (jnp.dot(flat_input, w_value, preferred_element_type=jnp.float32) + bias_value)
        .astype(jnp.bfloat16)
        .reshape(heads_shape)
    )
    mixed_heads = lax.map(attend_forward, (query_rows, key_rows, value_rows, segment_id))
    mixed_low = mixed_heads.reshape(token_count, D).astype(jnp.bfloat16)
    branch = jnp.dot(mixed_low, w_output, preferred_element_type=jnp.float32) + bias_output
    residual_one = flat_input.astype(jnp.float32) + branch
    normed = layer_norm(residual_one, gain_one, shift_one)
    normed_low = normed.astype(jnp.bfloat16)
    inner_sum = jnp.dot(normed_low, w_inner, preferred_element_type=jnp.float32) + bias_inner
    active_low = gelu_exact(inner_sum).astype(jnp.bfloat16)
    outer_sum = jnp.dot(active_low, w_outer, preferred_element_type=jnp.float32) + bias_outer
    residual_two = normed + outer_sum
    result = layer_norm(residual_two, gain_two, shift_two)
    result_rows = result.reshape(row_count, seq_len, D)
    leaders = jnp.take_along_axis(result_rows, span_starts[:, :, None], axis=1).reshape(-1, D)
    partner = swapped(leaders.astype(jnp.bfloat16), "pair", 0).astype(jnp.float32)
    pair_logits = (
        jnp.dot(leaders, partner.T, precision=HIGHEST, preferred_element_type=jnp.float32)
        * CLS_SCALE
    )
    pair_probs = jax.nn.softmax(pair_logits, axis=-1)
    targets = (
        pairing.reshape(-1)[:, None] == jnp.arange(leaders.shape[0], dtype=jnp.int32)[None, :]
    ).astype(jnp.float32)
    grad_pair = CLS_WEIGHT * CLS_SCALE * (pair_probs - targets)
    grad_leaders = jnp.dot(
        grad_pair, partner, precision=HIGHEST, preferred_element_type=jnp.float32
    )
    grad_partner = jnp.dot(
        grad_pair.T, leaders, precision=HIGHEST, preferred_element_type=jnp.float32
    )
    returned = swapped(grad_partner.astype(jnp.bfloat16), "pair", 0).astype(jnp.float32)
    grad_leaders = grad_leaders + returned
    valid_mask = (segment_id < SEGS).astype(jnp.float32)
    grad_result = cotangent[0].astype(jnp.float32) * valid_mask[:, :, None]
    row_index = jnp.arange(row_count, dtype=jnp.int32)[:, None]
    grad_result = grad_result.at[row_index, span_starts].add(
        grad_leaders.reshape(row_count, SEGS, D)
    )
    grad_result = grad_result.reshape(token_count, D)
    primal_two, norm_two_back = jax.vjp(layer_norm, residual_two, gain_two, shift_two)
    grad_residual_two, grad_gain_two, grad_shift_two = norm_two_back(grad_result)
    grad_outer = grad_residual_two.astype(jnp.bfloat16)
    grad_bias_outer = jnp.sum(grad_outer, axis=0, dtype=jnp.float32)
    grad_w_outer = jnp.einsum(
        "tf,td->fd", active_low, grad_outer, preferred_element_type=jnp.float32
    )
    grad_active = jnp.einsum("td,fd->tf", grad_outer, w_outer, preferred_element_type=jnp.float32)
    primal_gelu, gelu_back = jax.vjp(gelu_exact, inner_sum)
    grad_inner = gelu_back(grad_active)[0].astype(jnp.bfloat16)
    grad_bias_inner = jnp.sum(grad_inner, axis=0, dtype=jnp.float32)
    grad_w_inner = jnp.einsum(
        "td,tf->df", normed_low, grad_inner, preferred_element_type=jnp.float32
    )
    grad_normed = grad_residual_two + jnp.einsum(
        "tf,df->td", grad_inner, w_inner, preferred_element_type=jnp.float32
    )
    primal_one, norm_one_back = jax.vjp(layer_norm, residual_one, gain_one, shift_one)
    grad_residual_one, grad_gain_one, grad_shift_one = norm_one_back(grad_normed)
    grad_branch = grad_residual_one.astype(jnp.bfloat16)
    grad_bias_output = jnp.sum(grad_branch, axis=0, dtype=jnp.float32)
    grad_w_output = jnp.einsum(
        "td,te->de", mixed_low, grad_branch, preferred_element_type=jnp.float32
    )
    grad_mixed = (
        jnp.einsum("te,de->td", grad_branch, w_output, preferred_element_type=jnp.float32)
        .astype(jnp.bfloat16)
        .reshape(heads_shape)
    )
    grad_query, grad_key, grad_value = lax.map(
        attend_backward, (query_rows, key_rows, value_rows, segment_id, grad_mixed)
    )
    grad_query = grad_query.reshape(token_count, D).astype(jnp.bfloat16)
    grad_key = grad_key.reshape(token_count, D).astype(jnp.bfloat16)
    grad_value = grad_value.reshape(token_count, D).astype(jnp.bfloat16)
    grad_bias_query = jnp.sum(grad_query, axis=0, dtype=jnp.float32)
    grad_bias_value = jnp.sum(grad_value, axis=0, dtype=jnp.float32)
    grad_w_query = jnp.einsum(
        "td,te->de", flat_input, grad_query, preferred_element_type=jnp.float32
    )
    grad_w_key = jnp.einsum("td,te->de", flat_input, grad_key, preferred_element_type=jnp.float32)
    grad_w_value = jnp.einsum(
        "td,te->de", flat_input, grad_value, preferred_element_type=jnp.float32
    )
    grad_inputs = grad_residual_one + jnp.einsum(
        "te,de->td", grad_query, w_query, preferred_element_type=jnp.float32
    )
    grad_inputs = grad_inputs + jnp.einsum(
        "te,de->td", grad_key, w_key, preferred_element_type=jnp.float32
    )
    grad_inputs = grad_inputs + jnp.einsum(
        "te,de->td", grad_value, w_value, preferred_element_type=jnp.float32
    )
    local_vector = (
        jnp.concatenate(
            [
                grad_gain_one,
                grad_shift_one,
                grad_gain_two,
                grad_shift_two,
                grad_bias_query,
                grad_bias_value,
                grad_bias_output,
                grad_bias_outer,
                grad_bias_inner,
            ]
        )
        * grad_scale
    )
    vector_grad = lax.psum(local_vector, ("pair", "dp"))
    grad_blocks = (
        disassemble(
            (grad_w_query, grad_w_key, grad_w_value, grad_w_output, grad_w_inner, grad_w_outer),
            block_side,
        )
        * grad_scale
    )
    slot_total = master.shape[0] * data_count
    dealt_grad = (
        jnp.zeros((slot_total, block_side, block_side), jnp.float32).at[owner_slot].set(grad_blocks)
    )
    owned_grad = lax.psum_scatter(dealt_grad, "dp", scatter_dimension=0, tiled=True)
    owned_grad = lax.psum(owned_grad.astype(jnp.bfloat16), "pair").astype(jnp.float32)
    new_master, new_first, new_second = soap_update(
        owned_grad, master, first_moment, second_moment, left_basis, right_basis
    )
    new_vector, vector_one, vector_two = adam_update(
        vector_grad, vector_master, vector_first, vector_second
    )
    return (
        result_rows.astype(jnp.bfloat16).reshape(inputs.shape),
        grad_inputs.reshape(inputs.shape),
        owned_grad,
        new_master,
        new_first,
        new_second,
        vector_grad,
        jnp.stack([new_vector, vector_one, vector_two], axis=0),
    )


def solution(mesh):
    placed = (
        P("pair", "dp", None, None),
        P("pair", "dp", None, None),
        P("pair", "dp", None),
        P("pair", "dp"),
        P("pair", "dp", None),
        P(),
        P("dp", None, None),
        P("dp", None, None),
        P("dp", None, None),
        P("dp", None, None),
        P("dp", None, None),
        P(),
        P(),
        P(),
    )
    return jax.shard_map(
        per_device,
        mesh=mesh,
        in_specs=placed,
        out_specs=(
            P("pair", "dp", None, None),
            P("pair", "dp", None, None),
            P("dp", None, None),
            P("dp", None, None),
            P("dp", None, None),
            P("dp", None, None),
            P(),
            P(),
        ),
        check_vma=False,
    )
```

profile of v0, /device:TPU:17, one launch (start us, length us, event | category | flops | bytes accessed | tf_op | source)
XLA Modules:
  0.0 1471.8 jit_solution(17176279958069419117)
XLA Ops:
  14.8 167.3 %all-gather.2.cloned.1.call-done = bf16[112,256,256]{2,1,0:T(8,128)(2,1)} async-done(((bf16[7,256,256]{2,1,0:T(8,128)(2,1)}), bf16[112,256,256]{2,1,0:T(8,128)(2,1)}) %all-gather.2.cloned.1.call-update) | async-done | bytes 14680080 | tf_op jit(solution)/shard_map/all_gather | solution.py:177
  182.1 12.7 gather_fusion
  194.8 7.6 broadcast_select_fusion
  202.5 5.0 copy-done.1
  209.4 8.5 fusion.171
  231.0 4.3 reshape.370
  235.3 3.0 copy.149
  243.2 3.8 reshape.373
  251.3 36.5 %while.24 = (s32[]{:T(128)}, bf16[2,512,12,64]{1,3,2,0:T(8,128)(2,1)}, bf16[2,512,12,64]{1,3,2,0:T(8,128)(2,1)S(1)}, s32[2,512]{1,0:T(2,128)S(1)}, bf16[2,512,12...) while((s32[]{:T(128)}, bf16[2,512,12,64]{1,3,2,0:T(8,128)(2,1)}, ...), condition=%wide.region_5.6_spmd, body=%wide.region_2.5_spmd.sunk | while | flops 824443392 | bytes 29687888 | solution.py:221
  252.2 10.5 fusion.244
  262.7 6.7 bitcast_dynamic-update-slice_fusion.8
  270.3 10.5 fusion.244
  280.9 6.7 bitcast_dynamic-update-slice_fusion.8
  287.8 3.6 copy.151
  297.8 3.0 copy.153
  300.8 5.4 copy.192
  306.2 8.6 copy.154
  314.8 6.1 copy.193
  321.0 35.1 %multiply_convert_fusion = (bf16[1024,3072]{1,0:T(8,128)(2,1)S(1)}, f32[1024,3072]{1,0:T(8,128)}, f32[1024,3072]{1,0:T(8,128)}) fusion(f32[3072]{0:T(1024)S(1)} %copy-done.65, bf16[768,3072]{1,0:T(8,128)(2,1)S(1)} %bitcast.340, f32[1024,768]{1,0:T(8,128)S(1)} %copy-done.6, f32[768]{0:T(1024)S(1)} %copy-done.50, f32[768]{0:T(1024)S(1)} %copy-done.49, ...), kind=kOutput, calls=%fused_computation.93 | convolution fusion | flops 5043388416 | bytes 39348224 | tf_op jit(solution)/shard_map/dot_general | solution.py:227
  356.2 5.4 fusion.175
  374.3 4.5 fusion.111
  381.5 17.4 %convert_reduce_fusion = (f32[3072]{0:T(1024)}, bf16[1024,3072]{1,0:T(8,128)(2,1)}) fusion(f32[1024,3072]{1,0:T(8,128)} %get-tuple-element.243, bf16[1024,768]{1,0:T(8,128)(2,1)S(1)} %get-tuple-element.231, bf16[3072,768]{0,1:T(8,128)(2,1)} %bitcast.342, f32[1024,3072]{1,0:T(8,128)} %get-tuple-element.268, f32[3072]{0:T(1024)S(1)} %copy-done.65), kind=kOutput, calls=%fused_computation.91 | convolution fusion | flops 4885312512 | bytes 37773312 | tf_op jit(solution)/shard_map/td,fd->tf/dot_general | solution.py:266
  398.9 10.5 multiply_reduce_fusion.1
  409.4 8.5 fusion.144
  418.0 10.3 fusion.180
  447.0 128.6 %while.25 = (s32[]{:T(128)}, bf16[2,512,12,64]{1,3,2,0:T(8,128)(2,1)}, bf16[2,512,12,64]{1,3,2,0:T(8,128)(2,1)}, bf16[2,512,12,64]{1,3,2,0:T(8,128)(2,1)}, bf16[...) while((s32[]{:T(128)}, ...), condition=%wide.region_21.22_spmd, body=%wide.region_17.21_spmd.sunk | while | flops 2082747904 | bytes 149875824 | solution.py:288
  448.2 10.6 fusion.256
  458.7 7.5 fusion.255
  466.2 18.7 %bitcast_dynamic-update-slice_fusion.10 = bf16[2,512,12,64]{1,3,2,0:T(8,128)(2,1)} fusion(bf16[2,512,12,64]{1,3,2,0:T(8,128)(2,1)} %get-tuple-element.411, s32[]{:T(128)} %get-tuple-element.409, f32[12,512,512]{1,2,0:T(8,128)} %fusion.255, pred[512,512]{0,1:T(8,128)(4,1)} %broadcast_compare_fusion.5, ...), kind=kOutput, calls=%fused_computation.50.clone.1 | convolution fusion | flops 427825664 | bytes 53019648 | tf_op jit(solution)/shard_map/while/body/eval_jaxpr/hij,ihd->jhd/dot_general | solution.py:151
  485.0 7.8 bitcast_dynamic-update-slice_fusion.11
  492.7 18.7 %bitcast_dynamic-update-slice_fusion.9 = bf16[2,512,12,64]{1,3,2,0:T(8,128)(2,1)} fusion(bf16[2,512,12,64]{1,3,2,0:T(8,128)(2,1)} %get-tuple-element.410, s32[]{:T(128)} %get-tuple-element.409, f32[12,512,512]{1,2,0:T(8,128)} %fusion.255, pred[512,512]{0,1:T(8,128)(4,1)} %broadcast_compare_fusion.5, ...), kind=kOutput, calls=%fused_computation.51.clone.1 | convolution fusion | flops 427825664 | bytes 53019648 | tf_op jit(solution)/shard_map/while/body/eval_jaxpr/hij,jhd->ihd/dot_general | solution.py:148
  512.4 10.6 fusion.256
  522.9 7.5 fusion.255
  530.4 18.8 %bitcast_dynamic-update-slice_fusion.10 = bf16[2,512,12,64]{1,3,2,0:T(8,128)(2,1)} fusion(bf16[2,512,12,64]{1,3,2,0:T(8,128)(2,1)} %get-tuple-element.411, s32[]{:T(128)} %get-tuple-element.409, f32[12,512,512]{1,2,0:T(8,128)} %fusion.255, pred[512,512]{0,1:T(8,128)(4,1)} %broadcast_compare_fusion.5, ...), kind=kOutput, calls=%fused_computation.50.clone.1 | convolution fusion | flops 427825664 | bytes 53019648 | tf_op jit(solution)/shard_map/while/body/eval_jaxpr/hij,ihd->jhd/dot_general | solution.py:151
  549.2 7.8 bitcast_dynamic-update-slice_fusion.11
  557.0 18.7 %bitcast_dynamic-update-slice_fusion.9 = bf16[2,512,12,64]{1,3,2,0:T(8,128)(2,1)} fusion(bf16[2,512,12,64]{1,3,2,0:T(8,128)(2,1)} %get-tuple-element.410, s32[]{:T(128)} %get-tuple-element.409, f32[12,512,512]{1,2,0:T(8,128)} %fusion.255, pred[512,512]{0,1:T(8,128)(4,1)} %broadcast_compare_fusion.5, ...), kind=kOutput, calls=%fused_computation.51.clone.1 | convolution fusion | flops 427825664 | bytes 53019648 | tf_op jit(solution)/shard_map/while/body/eval_jaxpr/hij,jhd->ihd/dot_general | solution.py:148
  575.7 12.4 reshape.392
  588.1 13.8 copy.170
  607.9 3.1 copy.163
  610.9 4.7 reshape.385
  625.9 3.0 copy.165
  628.9 4.6 reshape.387
  633.5 3.8 copy.166
  643.3 3.0 copy.167
  646.4 4.6 reshape.389
  650.9 3.7 copy.168
  657.2 12.0 reshape.394
  669.2 12.3 copy.172
  681.5 3.4 constant_dynamic-update-slice_fusion.4
  687.2 3.2 fusion.179
  692.1 4.7 constant_dynamic-update-slice_fusion.1
  696.7 8.3 constant_dynamic-update-slice_fusion
  705.1 20.0 %broadcast_multiply_fusion = f32[108,256,256]{2,1,0:T(8,128)} fusion(f32[108,256,256]{2,1,0:T(8,128)} %constant_dynamic-update-slice_fusion), kind=kLoop, calls=%fused_computation.88 | loop fusion | flops 7077888 | bytes 56623104 | tf_op jit(solution)/shard_map/mul | solution.py:330
  725.0 13.4 broadcast_in_dim.136
  738.4 51.9 %scatter_fusion.1 = f32[112,256,256]{2,1,0:T(8,128)} fusion(f32[112,256,256]{2,1,0:T(8,128)} %broadcast_in_dim.136, s32[108]{0:T(128)S(1)} %copy-done.71, f32[108,256,256]{2,1,0:T(8,128)} %broadcast_multiply_fusion), kind=kCustom, calls=%fused_computation.3 | custom fusion | bytes 84935088 | tf_op jit(solution)/shard_map/scatter | solution.py:338
  790.3 29.6 %copy.173 = f32[112,256,256]{1,2,0:T(8,128)} copy(f32[112,256,256]{2,1,0:T(8,128)} %scatter_fusion.1) | data formatting | bytes 58720256 | tf_op jit(solution)/shard_map/scatter | solution.py:338
  824.3 78.3 %psum.15 = f32[9216]{0:T(1024)S(1)} all-reduce(f32[9216]{0:T(1024)S(1)} %broadcast_multiply_fusion.1), channel_id=1, replica_groups=mesh['pair'=2,'dp'=16] {'pair','dp'}, use_global_device_ids=true, to_apply=%region_34.35 | all-reduce | flops 9216 | bytes 73728 | tf_op jit(solution)/shard_map/psum | solution.py:328
  902.7 3.3 fusion.177
  908.8 3.6 add_add_fusion.2
  912.4 508.2 %reduce-scatter.2.cloned.1.call-done = f32[7,256,256]{1,2,0:T(8,128)} async-done(((f32[112,256,256]{1,2,0:T(8,128)}), f32[7,256,256]{1,2,0:T(8,128)}) %reduce-scatter.2.cloned.1.call-update) | async-done | bytes 1835024 | tf_op jit(solution)/shard_map/reduce_scatter | solution.py:340
  1424.0 26.6 %all-reduce.2.cloned.1.call-done = bf16[7,256,256]{1,2,0:T(8,128)(2,1)} async-done(((bf16[7,256,256]{1,2,0:T(8,128)(2,1)}), bf16[7,256,256]{1,2,0:T(8,128)(2,1)}) %all-reduce.2.cloned.1.call-update) | async-done | bytes 917520 | tf_op jit(solution)/shard_map/psum | solution.py:341
  1450.5 3.6 fusion.181
  1456.5 3.2 fusion.114
  1459.8 3.4 multiply_subtract_fusion
  (304 shorter events, 118.5 us)
Async XLA Ops:
  7.2 1446.9 %copy-start = (f32[7,256,256]{2,1,0:T(8,128)S(1)}, f32[7,256,256]{2,1,0:T(8,128)}, u32[]{:S(2)}) copy-start(f32[7,256,256]{2,1,0:T(8,128)} %param.28) | copy-start | bytes 5505028
  7.2 3.2 copy-start.44
  7.2 5.1 copy-start.82
  7.2 5.7 copy-start.83
  7.2 174.9 %all-gather.2.cloned.1.call-start = ((), (), s32[]{:S(2)}) async-start(), calls=%async_computation.1 | async-start | bytes 15597568 | tf_op jit(solution)/shard_map/all_gather | solution.py:177
  9.9 1410.7 %reduce-scatter.2.cloned.1.call-start = ((), (), s32[]{:S(2)}) async-start(), calls=%async_computation.2 | async-start | bytes 31195136 | tf_op jit(solution)/shard_map/reduce_scatter | solution.py:340
  202.5 5.0 copy-start.1
  287.7 4.1 copy-start.10
  287.7 4.1 copy-start.46
  287.7 4.1 copy-start.23
  291.8 3.7 copy-start.33
  293.2 4.6 slice-start.3
  293.8 3.9 slice-start.4
  306.2 14.7 %slice-start.5 = ((s8[4718592]{0:T(1024)(128)(4,1)}), s8[524288]{0:T(1024)(128)(4,1)S(1)}, s32[]{:S(2)}) async-start(s8[4718592]{0:T(1024)(128)(4,1)} %bitcast.338), calls=%async_computation.9 | async-start | bytes 1048576
  314.8 6.2 copy-start.6
  314.8 6.2 slice-start.6
  314.8 6.2 copy-start.49
  314.8 6.2 copy-start.50
  314.8 6.2 copy-start.65
  320.9 35.3 %copy-start.26 = (bf16[96,8,12,256]{3,1,2,0:T(8,128)(2,1)}, bf16[96,8,12,256]{3,1,2,0:T(8,128)(2,1)S(1)}, u32[]{:S(2)}) copy-start(bf16[96,8,12,256]{3,1,2,0:T(8,128)(2,1)S(1)} %copy.193) | copy-start | bytes 14155780
  321.0 35.2 %copy-start.66 = (f32[768]{0:T(1024)S(1)}, f32[768]{0:T(1024)}, u32[]{:S(2)}) copy-start(f32[768]{0:T(1024)} %get-tuple-element.256) | copy-start | bytes 9220
  356.2 5.4 copy-start.84
  361.6 3.5 copy-start.3
  362.3 4.1 copy-start.74
  362.3 6.7 copy-start.73
  362.3 7.3 copy-start.38
  362.3 7.3 copy-start.62
  365.1 6.6 copy-start.72
  366.5 2.2 collective-permute-start
  369.2 2.6 collective-permute-start.1
  374.3 4.5 copy-start.2
  374.3 4.7 copy-start.4
  381.5 17.4 %copy-start.7 = (f32[1024,768]{1,0:T(8,128)S(1)}, f32[1024,768]{1,0:T(8,128)}, u32[]{:S(2)}) copy-start(f32[1024,768]{1,0:T(8,128)} %copy-done.5) | copy-start | bytes 9437188
  398.9 10.5 copy-start.15
  418.0 10.3 copy-start.55
  429.8 3.7 copy-start.43
  443.1 4.0 copy-start.11
  443.1 4.0 copy-start.47
  588.1 13.8 copy-start.12
  601.9 3.2 copy-start.79
  619.8 3.2 copy-start.80
  633.5 3.8 copy-start.13
  637.3 3.2 copy-start.81
  681.4 3.4 copy-start.14
  681.5 10.6 slice-start
  684.9 7.2 slice-start.1
  687.2 4.9 slice-start.2
  725.0 13.4 copy-start.71
  819.9 630.6 %all-reduce.2.cloned.1.call-start = ((), (), s32[]{:S(2)}) async-start(), calls=%async_computation.3 | async-start | bytes 1835008 | tf_op jit(solution)/shard_map/psum | solution.py:341
  820.0 4.2 copy-start.68
  820.0 4.2 copy-start.67
  820.0 4.2 copy-start.63
  820.0 4.3 copy-start.61
  820.0 4.3 copy-start.60
  820.0 4.3 copy-start.64
  902.7 5.0 copy-start.48
  902.7 3.4 copy-start.37
  902.7 3.4 copy-start.41
  1450.5 3.6 copy-start.29
  1450.5 3.6 copy-start.30
  1456.5 3.3 copy-start.31
  1456.5 3.3 copy-start.32
  1456.5 3.2 copy-start.16
  1459.8 3.4 copy-start.27
  (33 other events, 61.4 us)
Sparse Core Ops, SparseCore 0:
  11.4 170.6 all-gather.1
  820.0 600.6 reduce-scatter.1
  1423.6 26.8 all-reduce.1
where the time goes:
time: 1480 us; the launch traced here: 1470 us
  waiting for transfers between devices  703 us (48%)
  local copies, waits for them, and re-layouts  319 us (22%)
  matrix products  292 us (20%)
  blocking collectives  78.3 us (5%)
  other arithmetic  61.1 us (4%)
  between operations  15.5 us (1%)
    reduce_scatter x1, waiting for transfers between devices, per_device(): lax.psum_scatter(dealt_grad, 'dp', scatter_dimension=0, tiled=True)  508 us
    all_gather x1, waiting for transfers between devices, per_device(): lax.all_gather(master.astype(jnp.bfloat16), 'dp', axis=0, tiled=True)  167 us
    scatter x2, local copies, waits for them, and re-layouts, per_device(): jnp.zeros((slot_total, block_side, block_side), jnp.float32).at[owner_slot]  81.5 us
    psum x1, blocking collectives, per_device(): vector_grad = lax.psum(local_vector, ('pair', 'dp'))  78.3 us
    unnamed x208, local copies, waits for them, and re-layouts  48.8 us
    sub x4, matrix products, attend(): return (jax.nn.softmax(scores, axis=-1), allowed, factor)  42.2 us
    reshape x5, local copies, waits for them, and re-layouts, untiled(): matrix.reshape(count_rows, block_side, count_cols, block_side)  38.2 us
    dot_general x2, matrix products, attend_backward(): jnp.einsum('hij,ihd->jhd', grad_logits, query_row, preferred_element_type...  37.5 us
  transfers between devices with their start and end apart: 5, of which 4 were waited for; matrix products, arithmetic and copies ran while one was open for 1% of the time, Pallas kernels for 0%

commit v1 on v0

--- a/solution.py
+++ b/solution.py
@@ -1,8 +1,11 @@
+import functools
 import math
 
 import jax
 import jax.numpy as jnp
 from jax import lax
+from jax.experimental import pallas as pl
+from jax.experimental.pallas import tpu as pltpu
 from jax.sharding import PartitionSpec as P
 
 D = 768
@@ -116,42 +119,78 @@
     return (weight - LR_VECTOR * direction, moment_one, moment_two)
 
 
-def attend(query_row, key_row, segment_row):
-    allowed = segment_row[:, None] == segment_row[None, :]
-    logits = jnp.einsum("ihd,jhd->hij", query_row, key_row, preferred_element_type=jnp.float32)
-    factor = 1.0 / math.sqrt(query_row.shape[-1])
-    scores = jnp.where(allowed[None], logits * factor, -1e30)
-    return (jax.nn.softmax(scores, axis=-1), allowed, factor)
-
-
-def attend_forward(record):
-    query_row, key_row, value_row, segment_row = record
-    attn_probs, allowed, factor = attend(query_row, key_row, segment_row)
-    return jnp.einsum(
-        "hij,jhd->ihd",
-        attn_probs.astype(jnp.bfloat16),
-        value_row,
-        preferred_element_type=jnp.float32,
-    )
-
-
-def attend_backward(record):
-    query_row, key_row, value_row, segment_row, grad_row = record
-    attn_probs, allowed, factor = attend(query_row, key_row, segment_row)
-    probs_low = attn_probs.astype(jnp.bfloat16)
-    grad_probs = jnp.einsum("ihd,jhd->hij", grad_row, value_row, preferred_element_type=jnp.float32)
-    grad_value = jnp.einsum("hij,ihd->jhd", probs_low, grad_row, preferred_element_type=jnp.float32)
-    grad_scores = attn_probs * (
-        grad_probs - jnp.sum(attn_probs * grad_probs, axis=-1, keepdims=True)
-    )
-    grad_logits = jnp.where(allowed[None], grad_scores * factor, 0.0).astype(jnp.bfloat16)
-    grad_query = jnp.einsum(
-        "hij,jhd->ihd", grad_logits, key_row, preferred_element_type=jnp.float32
-    )
-    grad_key = jnp.einsum(
-        "hij,ihd->jhd", grad_logits, query_row, preferred_element_type=jnp.float32
-    )
-    return (grad_query, grad_key, grad_value)
+def scores_of(left, right):
+    return lax.dot_general(
+        left, right, (((1,), (1,)), ((), ())), preferred_element_type=jnp.float32
+    )
+
+
+def attend_forward_body(head_dim, seg_col, seg_row, q_ref, k_ref, v_ref, o_ref):
+    allowed = seg_col[0] == seg_row[0]
+    factor = 1.0 / math.sqrt(head_dim)
+    for start in range(0, q_ref.shape[1], head_dim):
+        lanes = slice(start, start + head_dim)
+        scores = scores_of(q_ref[:, lanes], k_ref[:, lanes])
+        scores = jnp.where(allowed, scores * factor, -1e30)
+        top = jnp.max(scores, axis=1, keepdims=True)
+        weights = jnp.exp(scores - top)
+        total = jnp.sum(weights, axis=1, keepdims=True)
+        probs = (weights * (1.0 / total)).astype(jnp.bfloat16)
+        mixed = jnp.dot(probs, v_ref[:, lanes], preferred_element_type=jnp.float32)
+        o_ref[:, lanes] = mixed.astype(o_ref.dtype)
+
+
+def attend_backward_body(
+    head_dim, seg_col, seg_row, q_ref, k_ref, v_ref, g_ref, dq_ref, dk_ref, dv_ref
+):
+    allowed = seg_col[0] == seg_row[0]
+    factor = 1.0 / math.sqrt(head_dim)
+    for start in range(0, q_ref.shape[1], head_dim):
+        lanes = slice(start, start + head_dim)
+        query, key = q_ref[:, lanes], k_ref[:, lanes]
+        value, grad = v_ref[:, lanes], g_ref[:, lanes]
+        scores = jnp.where(allowed, scores_of(key, query) * factor, -1e30)
+        top = jnp.max(scores, axis=0, keepdims=True)
+        weights = jnp.exp(scores - top)
+        total = jnp.sum(weights, axis=0, keepdims=True)
+        probs = weights * (1.0 / total)
+        dv = jnp.dot(probs.astype(jnp.bfloat16), grad, preferred_element_type=jnp.float32)
+        dv_ref[:, lanes] = dv.astype(dv_ref.dtype)
+        grad_probs = scores_of(value, grad)
+        inner = jnp.sum(probs * grad_probs, axis=0, keepdims=True)
+        grad_scores = probs * (grad_probs - inner)
+        grad_logits = jnp.where(allowed, grad_scores * factor, 0.0).astype(jnp.bfloat16)
+        dk = jnp.dot(grad_logits, query, preferred_element_type=jnp.float32)
+        dk_ref[:, lanes] = dk.astype(dk_ref.dtype)
+        dq = lax.dot_general(
+            grad_logits, key, (((0,), (0,)), ((), ())), preferred_element_type=jnp.float32
+        )
+        dq_ref[:, lanes] = dq.astype(dq_ref.dtype)
+
+
+def attention_call(body, count_out, segment_id, arrays):
+    rows, seq_len = segment_id.shape
+    width = arrays[0].shape[1]
+    lanes = 2 * (D // HEADS)
+    tile = pl.BlockSpec((seq_len, lanes), lambda r, h: (r, h))
+    shape = jax.ShapeDtypeStruct(arrays[0].shape, jnp.bfloat16)
+    flops = 2 * rows * seq_len * seq_len * width * (2 if count_out == 1 else 5)
+    return pl.pallas_call(
+        functools.partial(body, D // HEADS),
+        grid=(rows, width // lanes),
+        in_specs=[
+            pl.BlockSpec((1, seq_len, 1), lambda r, h: (r, 0, 0)),
+            pl.BlockSpec((1, 1, seq_len), lambda r, h: (r, 0, 0)),
+        ]
+        + [tile] * len(arrays),
+        out_specs=[tile] * count_out,
+        out_shape=[shape] * count_out,
+        cost_estimate=pl.CostEstimate(
+            flops=flops,
+            bytes_accessed=2 * arrays[0].size * (len(arrays) + count_out),
+            transcendentals=rows * HEADS * seq_len * seq_len,
+        ),
+    )(segment_id[:, :, None], segment_id[:, None, :], *arrays)
 
 
 def per_device(
@@ -174,9 +213,14 @@
     data_count = lax.axis_size("dp")
     grad_scale = 1.0 / (pair_count * data_count)
     block_side = master.shape[-1]
-    gathered = lax.all_gather(master.astype(jnp.bfloat16), "dp", axis=0, tiled=True)
+    half = block_side // pair_count
+    core = lax.axis_index("pair")
+    own_half = lax.dynamic_slice_in_dim(master, core * half, half, axis=1).astype(jnp.bfloat16)
+    gathered = lax.all_gather(own_half, ("dp", "pair"), axis=0)
+    gathered = gathered.reshape(data_count, pair_count, -1, half, block_side)
+    gathered = gathered.transpose(0, 2, 1, 3, 4).reshape(-1, block_side, block_side)
     w_query, w_key, w_value, w_output, w_inner, w_outer = assemble(
-        jnp.take(gathered, owner_slot, axis=0)
+        gathered.at[owner_slot].get(mode="promise_in_bounds", unique_indices=True)
     )
     (
         gain_one,
@@ -192,7 +236,6 @@
     row_count = inputs.shape[1]
     seq_len = inputs.shape[2]
     token_count = row_count * seq_len
-    heads_shape = (row_count, seq_len, HEADS, D // HEADS)
     flat_input = inputs.reshape(token_count, D)
     span_rows = span_lengths[0]
     pad_rows = pad_lengths[0]
@@ -206,20 +249,18 @@
     query_rows = (
         (jnp.dot(flat_input, w_query, preferred_element_type=jnp.float32) + bias_query)
         .astype(jnp.bfloat16)
-        .reshape(heads_shape)
     )
     key_rows = (
         jnp.dot(flat_input, w_key, preferred_element_type=jnp.float32)
         .astype(jnp.bfloat16)
-        .reshape(heads_shape)
     )
     value_rows = (
         (jnp.dot(flat_input, w_value, preferred_element_type=jnp.float32) + bias_value)
         .astype(jnp.bfloat16)
-        .reshape(heads_shape)
-    )
-    mixed_heads = lax.map(attend_forward, (query_rows, key_rows, value_rows, segment_id))
-    mixed_low = mixed_heads.reshape(token_count, D).astype(jnp.bfloat16)
+    )
+    (mixed_low,) = attention_call(
+        attend_forward_body, 1, segment_id, (query_rows, key_rows, value_rows)
+    )
     branch = jnp.dot(mixed_low, w_output, preferred_element_type=jnp.float32) + bias_output
     residual_one = flat_input.astype(jnp.float32) + branch
     normed = layer_norm(residual_one, gain_one, shift_one)
@@ -283,14 +324,10 @@
     grad_mixed = (
         jnp.einsum("te,de->td", grad_branch, w_output, preferred_element_type=jnp.float32)
         .astype(jnp.bfloat16)
-        .reshape(heads_shape)
-    )
-    grad_query, grad_key, grad_value = lax.map(
-        attend_backward, (query_rows, key_rows, value_rows, segment_id, grad_mixed)
-    )
-    grad_query = grad_query.reshape(token_count, D).astype(jnp.bfloat16)
-    grad_key = grad_key.reshape(token_count, D).astype(jnp.bfloat16)
-    grad_value = grad_value.reshape(token_count, D).astype(jnp.bfloat16)
+    )
+    grad_query, grad_key, grad_value = attention_call(
+        attend_backward_body, 3, segment_id, (query_rows, key_rows, value_rows, grad_mixed)
+    )
     grad_bias_query = jnp.sum(grad_query, axis=0, dtype=jnp.float32)
     grad_bias_value = jnp.sum(grad_value, axis=0, dtype=jnp.float32)
     grad_w_query = jnp.einsum(
@@ -326,19 +363,28 @@
         * grad_scale
     )
     vector_grad = lax.psum(local_vector, ("pair", "dp"))
-    grad_blocks = (
-        disassemble(
-            (grad_w_query, grad_w_key, grad_w_value, grad_w_output, grad_w_inner, grad_w_outer),
-            block_side,
-        )
-        * grad_scale
+    grad_blocks = disassemble(
+        tuple(
+            (matrix * grad_scale).astype(jnp.bfloat16)
+            for matrix in (
+                grad_w_query, grad_w_key, grad_w_value, grad_w_output, grad_w_inner, grad_w_outer
+            )
+        ),
+        block_side,
     )
     slot_total = master.shape[0] * data_count
-    dealt_grad = (
-        jnp.zeros((slot_total, block_side, block_side), jnp.float32).at[owner_slot].set(grad_blocks)
-    )
-    owned_grad = lax.psum_scatter(dealt_grad, "dp", scatter_dimension=0, tiled=True)
-    owned_grad = lax.psum(owned_grad.astype(jnp.bfloat16), "pair").astype(jnp.float32)
+    block_of = (
+        jnp.full((slot_total,), owner_slot.shape[0], jnp.int32)
+        .at[owner_slot]
+        .set(jnp.arange(owner_slot.shape[0], dtype=jnp.int32))
+    )
+    padded = jnp.concatenate(
+        [grad_blocks, jnp.zeros((1, block_side, block_side), jnp.bfloat16)], axis=0
+    )
+    dealt_grad = padded.at[block_of].get(mode="promise_in_bounds")
+    own_grad = lax.psum_scatter(dealt_grad, "pair", scatter_dimension=1, tiled=True)
+    own_grad = lax.psum_scatter(own_grad, "dp", scatter_dimension=0, tiled=True)
+    owned_grad = lax.all_gather(own_grad, "pair", axis=1, tiled=True).astype(jnp.float32)
     new_master, new_first, new_second = soap_update(
         owned_grad, master, first_moment, second_moment, left_basis, right_basis
     )

time: 1480 us -> 730 us (0.49)
  waiting for transfers between devices: 703 us -> 216 us
  matrix products: 292 us -> 130 us
  local copies, waits for them, and re-layouts: 319 us -> 208 us
  Pallas kernels: 0 us -> 70.6 us
  other arithmetic: 61.1 us -> 27.9 us
  blocking collectives: 78.3 us -> 53 us
    reduce_scatter x1, waiting for transfers between devices: 508 us -> 94.6 us  [per_device(): own_grad = lax.psum_scatter(own_grad, 'dp', scatter_dimension=0, tiled=True)]
    dot_general x10 -> x0, matrix products: 119 us -> none  [the longest x2 37.5 us: attend_backward(): jnp.einsum('hij,ihd->jhd', grad_logits, query_row, preferred_element_type...]
    scatter x2 -> x1, local copies, waits for them, and re-layouts: 81.5 us -> 0.91 us  [per_device(): block_of = jnp.full((slot_total,), owner_slot.shape[0], jnp.int32).at[own...]
    all_gather x1, waiting for transfers between devices: 167 us -> 96.3 us  [per_device(): gathered = lax.all_gather(own_half, ('dp', 'pair'), axis=0)]
    pallas_call x0 -> x2, Pallas kernels: none -> 70.6 us  [attention_call(): pl.pallas_call(functools.partial(body, D // HEADS), grid=(rows, width //...]
    sub x4 -> x0, matrix products: 42.2 us -> none  [attend(): return (jax.nn.softmax(scores, axis=-1), allowed, factor)]
    psum x1, blocking collectives: 78.3 us -> 50 us  [per_device(): vector_grad = lax.psum(local_vector, ('pair', 'dp'))]
    psum x1 -> x0, waiting for transfers between devices: 26.6 us -> none  [per_device(): lax.psum(owned_grad.astype(jnp.bfloat16), 'pair').astype(jnp.float32)]
  transfers between devices with their start and end apart: 5 -> 5, of which waited for: 4 -> 4; matrix products, arithmetic and copies ran while one was open for 1% -> 4% of each run, Pallas kernels for 0% -> 0%
where the time goes in v1:
time: 730 us; the launch traced here: 722 us
  waiting for transfers between devices  216 us (30%)
  local copies, waits for them, and re-layouts  208 us (28%)
  matrix products  130 us (18%)
  Pallas kernels  70.6 us (10%)
  blocking collectives  53 us (7%)
  other arithmetic  27.9 us (4%)
  between operations  15.1 us (2%)
    all_gather x1, waiting for transfers between devices, per_device(): gathered = lax.all_gather(own_half, ('dp', 'pair'), axis=0)  96.3 us
    reduce_scatter x1, waiting for transfers between devices, per_device(): own_grad = lax.psum_scatter(own_grad, 'dp', scatter_dimension=0, tiled=True)  94.6 us
    pallas_call x2, Pallas kernels, attention_call(): pl.pallas_call(functools.partial(body, D // HEADS), grid=(rows, width //...  70.6 us
    unnamed x150, local copies, waits for them, and re-layouts  67.5 us
    psum x1, blocking collectives, per_device(): vector_grad = lax.psum(local_vector, ('pair', 'dp'))  50 us
    dot_general x1, matrix products, per_device(): jnp.dot(normed_low, w_inner, preferred_element_type=jnp.float32)  35.3 us
    reshape x6, local copies, waits for them, and re-layouts, untiled(): matrix.reshape(count_rows, block_side, count_cols, block_side)  30.6 us
    unnamed x4, waiting for transfers between devices  24.4 us
  transfers between devices with their start and end apart: 5, of which 4 were waited for; matrix products, arithmetic and copies ran while one was open for 4% of the time, Pallas kernels for 0%

profile of v1, /device:TPU:17, one launch (start us, length us, event | category | flops | bytes accessed | tf_op | source)
XLA Modules:
  0.0 722.2 jit_solution(17753165092663317131)
XLA Ops:
  7.2 2.1 dynamic-slice_convert_fusion
  20.5 96.3 %all-gather.3.cloned.1.call-done = bf16[224,128,256]{2,1,0:T(8,128)(2,1)} async-done(((bf16[7,128,256]{2,1,0:T(8,128)(2,1)}), bf16[224,128,256]{2,1,0:T(8,128)(2,1)}) %all-gather.3.cloned.1.call-update) | async-done | bytes 14680080 | tf_op jit(solution)/shard_map/all_gather | solution.py:219
  116.9 13.5 %copy.130 = bf16[16,7,2,128,256]{4,3,2,1,0:T(8,128)(2,1)} copy(bf16[16,7,2,128,256]{4,3,1,2,0:T(8,128)(2,1)} %bitcast.179) | data formatting | bytes 29360128 | tf_op jit(solution)/shard_map/transpose | solution.py:221
  130.4 13.2 %gather_fusion = bf16[108,256,256]{2,1,0:T(8,128)(2,1)} fusion(bf16[112,256,256]{2,1,0:T(8,128)(2,1)} %bitcast.165, s32[1024]{0:T(1024)S(1)} %get-tuple-element.95), kind=kCustom, calls=%fused_computation | custom fusion | bytes 28311984 | tf_op jit(solution)/shard_map/gather | solution.py:223
  143.6 4.2 fusion.54
  147.9 7.0 fusion.53
  163.2 3.0 copy.138
  166.2 5.6 copy.168
  171.8 8.3 %copy.139 = bf16[12,3,256,256]{2,0,3,1:T(8,128)(2,1)} copy(bf16[12,3,256,256]{3,2,1,0:T(8,128)(2,1)} %bitcast.177) | data formatting | bytes 9437184 | tf_op jit(solution)/shard_map/reshape | solution.py:53
  180.1 8.2 %copy.169 = bf16[96,8,12,256]{3,1,2,0:T(8,128)(2,1)} copy(bf16[96,8,12,256]{3,2,1,0:T(8,128)(2,1)} %bitcast.168) | data formatting | bytes 9437184
  188.3 2.5 fusion.15.k_ref
  190.8 2.5 fusion.17.v_ref
  193.4 2.5 fusion.16.q_ref
  195.9 34.5 %shard_map.197 = bf16[1024,768]{1,0:T(8,128)(2,1)} custom-call(s32[2,512,1]{2,1,0:T(8,128)} %fusion.24.seg_col, s32[2,1,512]{2,1,0:T(1,128)} %compare_select_fusion.seg_row, bf16[1024,768]{1,0:T(8,128)(2,1)} %fusion.16.q_ref, bf16[1024,768]{1,0:T(8,128)(2,1)} %fusion.15.k_ref, bf16[1024,768]{1,0:T(8,128)(2,1)} %fusion.17.v_ref), custom_call_target="tpu_custom_call" | custom-call | flops 1610612736 | bytes 6291456 | tf_op jit(solution)/shard_map/pallas_call | solution.py:178
  230.4 3.6 fusion.56
  234.6 35.3 %multiply_convert_fusion = (bf16[1024,3072]{1,0:T(8,128)(2,1)S(1)}, f32[1024,3072]{1,0:T(8,128)}, f32[1024,3072]{1,0:T(8,128)}) fusion(f32[3072]{0:T(1024)S(1)} %slice.59, bf16[768,3072]{1,0:T(8,128)(2,1)S(1)} %bitcast.202, f32[1024,768]{1,0:T(8,128)S(1)} %get-tuple-element.85, f32[768]{0:T(1024)S(1)} %get-tuple-element.76, f32[768]{0:T(1024)S(1)} %get-tuple-element.77, ...), kind=kOutput, calls=%fused_computation.9 | convolution fusion | flops 5043388416 | bytes 39348224 | tf_op jit(solution)/shard_map/dot_general | solution.py:268
  269.9 5.5 fusion.57
  276.2 2.8 fusion.51
  282.5 2.1 convert_multiply_fusion
  284.8 2.2 scatter_fusion
  287.1 3.9 fusion.6
  291.8 2.0 fusion.50
  294.1 6.9 multiply_convert_fusion.1
  301.0 17.4 %convert_reduce_fusion = (f32[3072]{0:T(1024)}, bf16[1024,3072]{1,0:T(8,128)(2,1)}) fusion(f32[1024,3072]{1,0:T(8,128)} %get-tuple-element.65, bf16[1024,768]{1,0:T(8,128)(2,1)S(1)} %get-tuple-element.55, bf16[3072,768]{0,1:T(8,128)(2,1)} %bitcast.203, f32[1024,3072]{1,0:T(8,128)} %get-tuple-element.86, f32[3072]{0:T(1024)S(1)} %slice.59), kind=kOutput, calls=%fused_computation.7 | convolution fusion | flops 4885312512 | bytes 37773312 | tf_op jit(solution)/shard_map/td,fd->tf/dot_general | solution.py:307
  318.4 10.3 %multiply_reduce_fusion = (f32[768]{0:T(1024)}, f32[1024]{0:T(1024)S(1)}, f32[768]{0:T(1024)}, f32[1024,768]{1,0:T(8,128)S(1)}) fusion(f32[1024,768]{1,0:T(8,128)S(1)} %copy-done.7, f32[1024]{0:T(1024)S(1)} %fusion.33, f32[1024]{0:T(1024)S(1)} %broadcast_multiply_fusion.2, f32[768]{0:T(1024)S(1)} %get-tuple-element.77, ...), kind=kOutput, calls=%fused_computation.35 | convolution fusion | flops 4839699456 | bytes 20472832 | tf_op jit(solution)/shard_map/tf,df->td/dot_general | solution.py:314
  328.8 7.9 %multiply_convert_fusion.2 = bf16[768,3072]{1,0:T(8,128)(2,1)} fusion(bf16[1024,3072]{1,0:T(8,128)(2,1)S(1)} %copy-done.50, f32[1024,768]{1,0:T(8,128)S(1)} %copy-done.7, f32[768]{0:T(1024)S(1)} %get-tuple-element.76, f32[768]{0:T(1024)S(1)} %get-tuple-element.77, f32[1024]{0:T(1024)S(1)} %fusion.33, f32[1024]{0:T(1024)S(1)} %broadcast_multiply_fusion.2), kind=kOutput, calls=%fused_computation.24 | convolution fusion | flops 4840488960 | bytes 14170112 | tf_op jit(solution)/shard_map/td,tf->df/dot_general | solution.py:311
  338.8 2.2 copy-done.51
  340.9 2.5 multiply_convert_fusion.3
  343.4 2.6 convolution_convert_fusion.1.g_ref
  346.0 6.7 copy.148
  352.7 9.1 %reshape.367 = bf16[3,256,12,256]{3,2,1,0:T(8,128)(2,1)} reshape(bf16[768,3072]{1,0:T(8,128)(2,1)} %multiply_convert_fusion.2) | data formatting | bytes 9437184 | tf_op jit(solution)/shard_map/reshape | solution.py:63
  361.9 6.8 copy.147
  368.7 9.1 %reshape.369 = bf16[12,256,3,256]{1,0,3,2:T(8,128)(2,1)} reshape(bf16[3072,768]{0,1:T(8,128)(2,1)} %copy.148) | data formatting | bytes 9437184 | tf_op jit(solution)/shard_map/reshape | solution.py:63
  377.8 9.0 %copy.149 = bf16[12,3,256,256]{3,2,1,0:T(8,128)(2,1)} copy(bf16[12,3,256,256]{2,0,3,1:T(8,128)(2,1)} %bitcast.170) | data formatting | bytes 9437184 | tf_op jit(solution)/shard_map/transpose | solution.py:64
  386.9 2.3 reshape.365
  390.4 36.1 %shard_map.198 = (bf16[1024,768]{1,0:T(8,128)(2,1)}, bf16[1024,768]{1,0:T(8,128)(2,1)}, bf16[1024,768]{1,0:T(8,128)(2,1)}) custom-call(s32[2,512,1]{2,1,0:T(8,128)} %fusion.24.seg_col, s32[2,1,512]{2,1,0:T(1,128)} %compare_select_fusion.seg_row, bf16[1024,768]{1,0:T(8,128)(2,1)} %fusion.16.q_ref, bf16[1024,768]{1,0:T(8,128)(2,1)} %fusion.15.k_ref, ...), custom_call_target="tpu_custom_call" | custom-call | flops 4026531840 | bytes 11010048 | tf_op jit(solution)/shard_map/pallas_call | solution.py:178
  426.6 3.3 fusion.19
  429.9 1.7 copy.142
  431.5 2.3 reshape.361
  435.1 3.3 fusion.18
  439.9 3.8 reshape.359
  443.7 2.6 copy.141
  446.3 3.9 fusion.20
  450.1 2.4 copy.144
  452.5 3.8 reshape.363
  456.3 1.7 copy.145
  462.5 2.7 constant_dynamic-update-slice_fusion.1
  466.5 2.5 constant_dynamic-update-slice_fusion
  469.6 13.0 %gather_fusion.1 = bf16[112,256,256]{2,1,0:T(8,128)(2,1)} fusion(bf16[109,256,256]{2,1,0:T(8,128)(2,1)} %broadcast_dynamic-update-slice_fusion, s32[1024]{0:T(1024)} %get-tuple-element.94), kind=kCustom, calls=%fused_computation.1 | custom fusion | bytes 29360576 | tf_op jit(solution)/shard_map/gather | solution.py:384
  482.6 13.6 %copy.170 = bf16[32,8,112,256]{3,1,2,0:T(8,128)(2,1)} copy(bf16[32,8,112,256]{3,1,0,2:T(8,128)(2,1)} %bitcast.164) | data formatting | bytes 29360128
  496.3 24.4 %reduce-scatter.7.cloned.1.call-done = bf16[128,28672]{1,0:T(8,128)(2,1)} async-done(((bf16[256,28672]{1,0:T(8,128)(2,1)}), bf16[128,28672]{1,0:T(8,128)(2,1)}) %reduce-scatter.7.cloned.1.call-update) | async-done | bytes 7340048
  520.7 8.1 %copy.171 = bf16[16,8,112,256]{3,2,1,0:T(8,128)(2,1)} copy(bf16[16,8,112,256]{3,1,2,0:T(8,128)(2,1)} %bitcast.180) | data formatting | bytes 14680064
  528.7 11.1 %copy.162 = bf16[112,128,256]{1,2,0:T(8,128)(2,1)} copy(bf16[112,128,256]{2,0,1:T(8,128)(2,1)} %bitcast.166) | data formatting | bytes 14680064
  539.9 2.2 reduce_sum.198
  542.3 1.7 convert_reduce_fusion.4
  544.3 50.0 %psum.7 = f32[9216]{0:T(1024)S(1)} all-reduce(f32[9216]{0:T(1024)S(1)} %broadcast_multiply_fusion), channel_id=1, replica_groups=mesh['pair'=2,'dp'=16] {'pair','dp'}, use_global_device_ids=true, to_apply=%region_25.26 | all-reduce | flops 9216 | bytes 73728 | tf_op jit(solution)/shard_map/psum | solution.py:365
  594.3 3.3 fusion.60
  600.0 3.1 add_add_fusion.2
  603.8 94.6 %reduce-scatter.5.cloned.1.call-done = bf16[7,128,256]{1,2,0:T(8,128)(2,1)} async-done(((bf16[112,128,256]{1,2,0:T(8,128)(2,1)}), bf16[7,128,256]{1,2,0:T(8,128)(2,1)}) %reduce-scatter.5.cloned.1.call-update) | async-done | bytes 458768 | tf_op jit(solution)/shard_map/reduce_scatter | solution.py:386
  698.5 3.0 all_gather.11
  703.1 3.3 fusion.61
  706.5 2.3 multiply_add_fusion.2
  708.8 2.9 fusion.9
  711.8 3.4 multiply_subtract_fusion
  (212 shorter events, 42.9 us)
Async XLA Ops:
  7.2 699.3 %copy-start = (f32[7,256,256]{2,1,0:T(8,128)S(1)}, f32[7,256,256]{2,1,0:T(8,128)}, u32[]{:S(2)}) copy-start(f32[7,256,256]{2,1,0:T(8,128)} %param.24) | copy-start | bytes 5505028
  7.2 109.7 %all-gather.3.cloned.1.call-start = ((), (), s32[]{:S(2)}) async-start(), calls=%async_computation.3 | async-start | bytes 15138816 | tf_op jit(solution)/shard_map/all_gather | solution.py:219
  9.4 511.3 %reduce-scatter.7.cloned.1.call-start = ((), (), s32[]{:S(2)}) async-start(), calls=%async_computation.4 | async-start | bytes 22020096
  13.9 116.5 %copy-start.32 = (s32[2,512]{1,0:T(2,128)}, s32[2,512]{1,0:T(2,128)S(1)}, u32[]{:S(2)}) copy-start(s32[2,512]{1,0:T(2,128)S(1)} %fusion.28) | copy-start | bytes 12292
  16.9 113.5 %copy-start.42 = (s32[2]{0:T(128)}, s32[2]{0:T(128)S(1)}, u32[]{:S(2)}) copy-start(s32[2]{0:T(128)S(1)} %subtract_bitcast_fusion) | copy-start | bytes 28
  156.2 34.7 %copy-start.10 = (bf16[96,8,3,256]{3,1,2,0:T(8,128)(2,1)}, bf16[96,8,3,256]{3,1,2,0:T(8,128)(2,1)S(1)}, u32[]{:S(2)}) copy-start(bf16[96,8,3,256]{3,1,2,0:T(8,128)(2,1)S(1)} %copy.166) | copy-start | bytes 3538948
  156.2 2.3 copy-start.12
  180.1 8.2 %copy-start.25 = (bf16[96,8,3,256]{3,1,2,0:T(8,128)(2,1)S(1)}, bf16[96,8,3,256]{3,1,2,0:T(8,128)(2,1)}, u32[]{:S(2)}) copy-start(bf16[96,8,3,256]{3,1,2,0:T(8,128)(2,1)} %copy.165) | copy-start | bytes 3538948
  180.1 8.2 %copy-start.49 = (bf16[1,2,512,768]{3,2,1,0:T(8,128)(2,1)S(1)}, bf16[1,2,512,768]{3,2,1,0:T(8,128)(2,1)}, u32[]{:S(2)}) copy-start(bf16[1,2,512,768]{3,2,1,0:T(8,128)(2,1)} %param.14) | copy-start | bytes 4718596
  190.8 2.5 copy-start.26
  195.9 34.5 %copy-start.28 = (bf16[96,8,3,256]{3,1,2,0:T(8,128)(2,1)S(1)}, bf16[96,8,3,256]{3,1,2,0:T(8,128)(2,1)}, u32[]{:S(2)}) copy-start(bf16[96,8,3,256]{3,1,2,0:T(8,128)(2,1)} %copy.167) | copy-start | bytes 3538948
  230.4 4.2 slice-start.4
  230.4 4.2 slice-start.5
  230.4 39.5 %slice-start.6 = ((s8[4718592]{0:T(1024)(128)(4,1)}), s8[4194304]{0:T(1024)(128)(4,1)S(1)}, s32[]{:S(2)}) async-start(s8[4718592]{0:T(1024)(128)(4,1)} %bitcast.204), calls=%async_computation.11 | async-start | bytes 8388608
  234.0 35.9 %copy-start.6 = (f32[1024,768]{1,0:T(8,128)}, f32[1024,768]{1,0:T(8,128)S(1)}, u32[]{:S(2)}) copy-start(f32[1024,768]{1,0:T(8,128)S(1)} %get-tuple-element.85) | copy-start | bytes 9437188
  234.6 35.3 %copy-start.35 = (f32[1024]{0:T(1024)}, f32[1024]{0:T(1024)S(1)}, u32[]{:S(2)}) copy-start(f32[1024]{0:T(1024)S(1)} %multiply_reduce_fusion.4) | copy-start | bytes 12292
  234.6 35.3 %slice-start.7 = ((s8[4718592]{0:T(1024)(128)(4,1)}), s8[524288]{0:T(1024)(128)(4,1)S(1)}, s32[]{:S(2)}) async-start(s8[4718592]{0:T(1024)(128)(4,1)} %bitcast.204), calls=%async_computation.12 | async-start | bytes 1048576
  269.9 5.5 copy-start.52
  275.4 3.6 copy-start.2
  276.2 2.8 copy-start.39
  276.2 4.2 copy-start.48
  276.2 4.5 copy-start.33
  276.2 4.5 copy-start.43
  276.2 5.7 copy-start.47
  276.2 6.2 copy-start.24
  279.0 5.5 copy-start.46
  280.5 1.2 collective-permute-start
  282.2 2.5 collective-permute-start.1
  287.1 4.0 copy-start.1
  287.1 4.7 copy-start.3
  291.0 3.1 slice-start.8
  291.8 2.3 slice-start.9
  301.0 17.4 %copy-start.7 = (f32[1024,768]{1,0:T(8,128)S(1)}, f32[1024,768]{1,0:T(8,128)}, u32[]{:S(2)}) copy-start(f32[1024,768]{1,0:T(8,128)} %copy-done.6) | copy-start | bytes 9437188
  318.4 10.3 %copy-start.50 = (bf16[1024,3072]{1,0:T(8,128)(2,1)S(1)}, bf16[1024,3072]{1,0:T(8,128)(2,1)}, u32[]{:S(2)}) copy-start(bf16[1024,3072]{1,0:T(8,128)(2,1)} %get-tuple-element.93) | copy-start | bytes 18874372
  328.8 7.9 %copy-start.36 = (f32[1024]{0:T(1024)S(1)}, f32[1024]{0:T(1024)}, u32[]{:S(2)}) copy-start(f32[1024]{0:T(1024)} %copy-done.35) | copy-start | bytes 12292
  338.4 5.0 copy-start.4
  338.4 2.5 copy-start.51
  340.9 2.5 copy-start.29
  439.9 6.4 copy-start.8
  452.5 5.5 copy-start.16
  452.5 10.0 %slice-start = ((s8[4718592]{0:T(1024)(128)(4,1)}), s8[524288]{0:T(1024)(128)(4,1)S(1)}, s32[]{:S(2)}) async-start(s8[4718592]{0:T(1024)(128)(4,1)} %bitcast.171), calls=%async_computation.5 | async-start | bytes 1048576
  456.3 2.8 copy-start.15
  458.0 3.4 copy-start.14
  458.0 4.5 slice-start.1
  462.5 3.9 slice-start.2
  462.5 4.0 slice-start.3
  496.2 202.2 %reduce-scatter.5.cloned.1.call-start = ((), (), s32[]{:S(2)}) async-start(), calls=%async_computation.2 | async-start | bytes 7798784 | tf_op jit(solution)/shard_map/reduce_scatter | solution.py:386
  539.9 2.3 copy-start.45
  539.9 2.3 copy-start.44
  539.9 4.0 copy-start.9
  539.9 4.3 copy-start.41
  594.3 4.8 copy-start.31
  594.3 3.3 copy-start.23
  594.3 3.3 copy-start.27
  597.7 1.5 copy-start.30
  597.7 1.5 copy-start.37
  597.7 1.9 copy-start.5
  597.7 2.3 copy-start.11
  703.1 3.3 copy-start.19
  703.1 3.3 copy-start.20
  706.5 2.4 copy-start.18
  708.8 3.0 copy-start.21
  708.8 3.0 copy-start.22
  708.8 3.0 copy-start.17
  (4 other events, 4.3 us)
Sparse Core Ops, SparseCore 0:
  11.4 105.3 all-gather.2
  496.4 24.2 reduce-scatter.6
  540.0 158.4 reduce-scatter.4

commit v2 on v1

--- a/solution.py
+++ b/solution.py
@@ -38,8 +38,10 @@
     return centered * lax.rsqrt(variance + NORM_EPS) * gain_vector + shift_vector
 
 
-def gelu_exact(values):
-    return jax.nn.gelu(values, approximate=False)
+def gelu_and_slope(values):
+    lower = 0.5 * (1.0 + lax.erf(values * math.sqrt(0.5)))
+    density = jnp.exp(-0.5 * values * values) * (1.0 / math.sqrt(2.0 * math.pi))
+    return values * lower, lower + values * density
 
 
 def split_vector(vector):
@@ -47,44 +49,102 @@
     return tuple(pieces) + (vector[8 * D : 8 * D + FF],)
 
 
-def tiled(stack, count_rows, count_cols):
-    block_side = stack.shape[-1]
-    return (
-        stack.reshape(count_rows, count_cols, block_side, block_side)
-        .transpose(0, 2, 1, 3)
-        .reshape(count_rows * block_side, count_cols * block_side)
-    )
-
-
-def untiled(matrix, block_side):
-    count_rows = matrix.shape[0] // block_side
-    count_cols = matrix.shape[1] // block_side
-    return (
-        matrix.reshape(count_rows, block_side, count_cols, block_side)
-        .transpose(0, 2, 1, 3)
-        .reshape(count_rows * count_cols, block_side, block_side)
-    )
-
-
-def assemble(blocks):
-    block_side = blocks.shape[-1]
-    row_tiles = D // block_side
-    wide_tiles = FF // block_side
-    square = row_tiles * row_tiles
-    wide_count = row_tiles * wide_tiles
-    mats = [
-        tiled(blocks[index * square : (index + 1) * square], row_tiles, row_tiles)
-        for index in range(4)
-    ]
-    mats.append(tiled(blocks[4 * square : 4 * square + wide_count], row_tiles, wide_tiles))
-    mats.append(
-        tiled(blocks[4 * square + wide_count : 4 * square + 2 * wide_count], wide_tiles, row_tiles)
-    )
-    return tuple(mats)
-
-
-def disassemble(mats, block_side):
-    return jnp.concatenate([untiled(matrix, block_side) for matrix in mats], axis=0)
+def matrix_shapes():
+    return ((D, D),) * 4 + ((D, FF), (FF, D))
+
+
+def tile_walk(block_side):
+    for index, (rows, cols) in enumerate(matrix_shapes()):
+        for row in range(rows // block_side):
+            for col in range(cols // block_side):
+                yield index, row, col
+
+
+def assemble_body(per_owner, halves, slot_ref, gathered_ref, *refs):
+    mats, sems = refs[:-1], refs[-1]
+    half, side = gathered_ref.shape[-2:]
+    for block, (index, row, col) in enumerate(tile_walk(side)):
+        slot = slot_ref[block]
+        owner, place = lax.div(slot, per_owner), lax.rem(slot, per_owner)
+        for part in range(halves):
+            pltpu.make_async_copy(
+                gathered_ref.at[owner * halves + part, place],
+                mats[index].at[
+                    pl.ds(row * side + part * half, half), pl.ds(col * side, side)
+                ],
+                sems.at[index],
+            ).start()
+    for index, matrix in enumerate(mats):
+        pltpu.make_async_copy(matrix, matrix, sems.at[index]).wait()
+
+
+def assemble(gathered, owner_slot, halves):
+    shapes = matrix_shapes()
+    return pl.pallas_call(
+        functools.partial(assemble_body, gathered.shape[1], halves),
+        in_specs=[
+            pl.BlockSpec(memory_space=pltpu.SMEM),
+            pl.BlockSpec(memory_space=pl.ANY),
+        ],
+        out_specs=[pl.BlockSpec(memory_space=pltpu.VMEM)] * len(shapes),
+        out_shape=[jax.ShapeDtypeStruct(shape, gathered.dtype) for shape in shapes],
+        scratch_shapes=[pltpu.SemaphoreType.DMA((len(shapes),))],
+        cost_estimate=pl.CostEstimate(
+            flops=0, bytes_accessed=4 * gathered.size, transcendentals=0
+        ),
+    )(owner_slot, gathered)
+
+
+def deal_body(side, slot_ref, zero_ref, *refs):
+    mats, (dealt_ref, used_ref, sem) = refs[:-3], refs[-3:]
+    half = dealt_ref.shape[1]
+
+    @pl.loop(0, dealt_ref.shape[0])
+    def _(slot):
+        used_ref[slot] = 0
+
+    for block, (index, row, col) in enumerate(tile_walk(side)):
+        slot = slot_ref[block]
+        used_ref[slot] = 1
+        pltpu.make_async_copy(
+            mats[index].at[pl.ds(row * half, half), pl.ds(col * side, side)],
+            dealt_ref.at[slot],
+            sem,
+        ).start()
+
+    @pl.loop(0, dealt_ref.shape[0])
+    def _(slot):
+        @pl.when(used_ref[slot] == 0)
+        def _():
+            pltpu.make_async_copy(zero_ref, dealt_ref.at[slot], sem).start()
+
+    pltpu.make_async_copy(dealt_ref, dealt_ref, sem).wait()
+
+
+def deal(mats, owner_slot, slot_total, half, side):
+    dtype = mats[0].dtype
+    return pl.pallas_call(
+        functools.partial(deal_body, side),
+        in_specs=[pl.BlockSpec(memory_space=pltpu.SMEM)]
+        + [pl.BlockSpec(memory_space=pltpu.VMEM)] * (1 + len(mats)),
+        out_specs=pl.BlockSpec(memory_space=pl.ANY),
+        out_shape=jax.ShapeDtypeStruct((slot_total, half, side), dtype),
+        scratch_shapes=[pltpu.SMEM((slot_total,), jnp.int32), pltpu.SemaphoreType.DMA],
+        cost_estimate=pl.CostEstimate(
+            flops=0, bytes_accessed=4 * slot_total * half * side, transcendentals=0
+        ),
+    )(owner_slot, jnp.zeros((half, side), dtype), *mats)
+
+
+def pair_summed(gradient, scale, block_side, core):
+    halves = lax.axis_size("pair")
+    half = block_side // halves
+    gradient = (gradient * scale).astype(jnp.bfloat16)
+    parts = gradient.reshape(-1, halves, half, gradient.shape[1])
+    sent = lax.dynamic_index_in_dim(parts, 1 - core, axis=1, keepdims=False)
+    kept = lax.dynamic_index_in_dim(parts, core, axis=1, keepdims=False)
+    total = kept.astype(jnp.float32) + swapped(sent, "pair", 0).astype(jnp.float32)
+    return total.astype(jnp.bfloat16).reshape(-1, gradient.shape[1])
 
 
 def soap_update(gradient, weight, moment_one, moment_two, left_basis, right_basis):
@@ -217,10 +277,8 @@
     core = lax.axis_index("pair")
     own_half = lax.dynamic_slice_in_dim(master, core * half, half, axis=1).astype(jnp.bfloat16)
     gathered = lax.all_gather(own_half, ("dp", "pair"), axis=0)
-    gathered = gathered.reshape(data_count, pair_count, -1, half, block_side)
-    gathered = gathered.transpose(0, 2, 1, 3, 4).reshape(-1, block_side, block_side)
     w_query, w_key, w_value, w_output, w_inner, w_outer = assemble(
-        gathered.at[owner_slot].get(mode="promise_in_bounds", unique_indices=True)
+        gathered, owner_slot, pair_count
     )
     (
         gain_one,
@@ -266,7 +324,8 @@
     normed = layer_norm(residual_one, gain_one, shift_one)
     normed_low = normed.astype(jnp.bfloat16)
     inner_sum = jnp.dot(normed_low, w_inner, preferred_element_type=jnp.float32) + bias_inner
-    active_low = gelu_exact(inner_sum).astype(jnp.bfloat16)
+    active, slope = gelu_and_slope(inner_sum)
+    active_low, slope_low = active.astype(jnp.bfloat16), slope.astype(jnp.bfloat16)
     outer_sum = jnp.dot(active_low, w_outer, preferred_element_type=jnp.float32) + bias_outer
     residual_two = normed + outer_sum
     result = layer_norm(residual_two, gain_two, shift_two)
@@ -305,8 +364,7 @@
         "tf,td->fd", active_low, grad_outer, preferred_element_type=jnp.float32
     )
     grad_active = jnp.einsum("td,fd->tf", grad_outer, w_outer, preferred_element_type=jnp.float32)
-    primal_gelu, gelu_back = jax.vjp(gelu_exact, inner_sum)
-    grad_inner = gelu_back(grad_active)[0].astype(jnp.bfloat16)
+    grad_inner = (grad_active * slope_low.astype(jnp.float32)).astype(jnp.bfloat16)
     grad_bias_inner = jnp.sum(grad_inner, axis=0, dtype=jnp.float32)
     grad_w_inner = jnp.einsum(
         "td,tf->df", normed_low, grad_inner, preferred_element_type=jnp.float32
@@ -363,26 +421,13 @@
         * grad_scale
     )
     vector_grad = lax.psum(local_vector, ("pair", "dp"))
-    grad_blocks = disassemble(
-        tuple(
-            (matrix * grad_scale).astype(jnp.bfloat16)
-            for matrix in (
-                grad_w_query, grad_w_key, grad_w_value, grad_w_output, grad_w_inner, grad_w_outer
-            )
-        ),
-        block_side,
-    )
-    slot_total = master.shape[0] * data_count
-    block_of = (
-        jnp.full((slot_total,), owner_slot.shape[0], jnp.int32)
-        .at[owner_slot]
-        .set(jnp.arange(owner_slot.shape[0], dtype=jnp.int32))
-    )
-    padded = jnp.concatenate(
-        [grad_blocks, jnp.zeros((1, block_side, block_side), jnp.bfloat16)], axis=0
-    )
-    dealt_grad = padded.at[block_of].get(mode="promise_in_bounds")
-    own_grad = lax.psum_scatter(dealt_grad, "pair", scatter_dimension=1, tiled=True)
+    grad_mats = [
+        pair_summed(matrix, grad_scale, block_side, core)
+        for matrix in (
+            grad_w_query, grad_w_key, grad_w_value, grad_w_output, grad_w_inner, grad_w_outer
+        )
+    ]
+    own_grad = deal(grad_mats, owner_slot, master.shape[0] * data_count, half, block_side)
     own_grad = lax.psum_scatter(own_grad, "dp", scatter_dimension=0, tiled=True)
     owned_grad = lax.all_gather(own_grad, "pair", axis=1, tiled=True).astype(jnp.float32)
     new_master, new_first, new_second = soap_update(

time: 730 us -> 529 us (0.72)
  local copies, waits for them, and re-layouts: 208 us -> 32.4 us
  matrix products: 130 us -> 92 us
  waiting for transfers between devices: 216 us -> 196 us
  Pallas kernels: 70.6 us -> 88.8 us
  other arithmetic: 27.9 us -> 42.4 us
    unnamed x150 -> x113, local copies, waits for them, and re-layouts: 67.5 us -> 8.31 us
    reshape x12 -> x1, local copies, waits for them, and re-layouts: 46 us -> 2.75 us  [pair_summed(): parts = gradient.reshape(-1, halves, half, gradient.shape[1])]
    transpose x7 -> x0, local copies, waits for them, and re-layouts: 36.1 us -> none  [the longest x6 22.6 us: untiled(): return matrix.reshape(count_rows, block_side, count_cols, block_side).tra...]
    gather x2 -> x0, local copies, waits for them, and re-layouts: 26.2 us -> none  [the longest x1 13.2 us: per_device(): gathered.at[owner_slot].get(mode='promise_in_bounds', unique_indices=True)]
    dot_general x1, matrix products: 35.3 us -> 9.33 us  [per_device(): jnp.dot(normed_low, w_inner, preferred_element_type=jnp.float32)]
    unnamed x4 -> x2, waiting for transfers between devices: 24.4 us -> 0.03 us
    pallas_call x0 -> x2, Pallas kernels: none -> 17.9 us  [the longest x1 11.1 us: assemble(): pl.pallas_call(functools.partial(assemble_body, gathered.shape[1], halves...]
    convert_element_type x0 -> x7, other arithmetic: none -> 17.4 us  [the longest x6 16 us: pair_summed(): return total.astype(jnp.bfloat16).reshape(-1, gradient.shape[1])]
  transfers between devices with their start and end apart: 5 -> 10, of which waited for: 4 -> 3; matrix products, arithmetic and copies ran while one was open for 4% -> 11% of each run, Pallas kernels for 0% -> 0%
where the time goes in v2:
time: 529 us; the launch traced here: 521 us
  waiting for transfers between devices  196 us (37%)
  matrix products  92 us (17%)
  Pallas kernels  88.8 us (17%)
  blocking collectives  51.7 us (10%)
  other arithmetic  42.4 us (8%)
  local copies, waits for them, and re-layouts  32.4 us (6%)
  between operations  15.2 us (3%)
    all_gather x1, waiting for transfers between devices, per_device(): gathered = lax.all_gather(own_half, ('dp', 'pair'), axis=0)  101 us
    reduce_scatter x1, waiting for transfers between devices, per_device(): own_grad = lax.psum_scatter(own_grad, 'dp', scatter_dimension=0, tiled=True)  94.5 us
    pallas_call x2, Pallas kernels, attention_call(): pl.pallas_call(functools.partial(body, D // HEADS), grid=(rows, width //...  70.9 us
    psum x1, blocking collectives, per_device(): vector_grad = lax.psum(local_vector, ('pair', 'dp'))  48.3 us
    convert_element_type x6, other arithmetic, pair_summed(): return total.astype(jnp.bfloat16).reshape(-1, gradient.shape[1])  16 us
    dot_general x1, matrix products, per_device(): jnp.einsum('td,fd->tf', grad_outer, w_outer, preferred_element_type=jnp.f...  11.8 us
    pallas_call x1, Pallas kernels, assemble(): pl.pallas_call(functools.partial(assemble_body, gathered.shape[1], halves...  11.1 us
  transfers between devices with their start and end apart: 10, of which 3 were waited for; matrix products, arithmetic and copies ran while one was open for 11% of the time, Pallas kernels for 0%

profile of v2, /device:TPU:17, one launch (start us, length us, event | category | flops | bytes accessed | tf_op | source)
XLA Modules:
  0.0 520.8 jit_solution(6566809320594139490)
XLA Ops:
  7.2 2.1 dynamic-slice_convert_fusion
  9.4 0.8 squeeze.37
  10.2 0.8 reduce_window_sum.15
  14.4 0.8 fusion.52
  15.2 0.9 fusion.26.seg_col
  16.1 100.8 %all-gather.3.cloned.1.call-done = bf16[224,128,256]{2,1,0:T(8,128)(2,1)} async-done(((bf16[7,128,256]{2,1,0:T(8,128)(2,1)}), bf16[224,128,256]{2,1,0:T(8,128)(2,1)}) %all-gather.3.cloned.1.call-update) | async-done | bytes 14680080 | tf_op jit(solution)/shard_map/all_gather | solution.py:279
  116.9 11.1 %shard_map.197 = (bf16[768,768]{1,0:T(8,128)(2,1)}, bf16[768,768]{1,0:T(8,128)(2,1)}, bf16[768,768]{1,0:T(8,128)(2,1)}, bf16[768,768]{1,0:T(8,128)(2,1)}, bf16[7...) custom-call(s32[108]{0:T(128)} %slot_ref.3, bf16[32,7,128,256]{3,2,1,0:T(8,128)(2,1)} %bitcast.156), custom_call_target="tpu_custom_call" | custom-call | bytes 29360128 | tf_op jit(solution)/shard_map/pallas_call | solution.py:83
  128.0 3.9 fusion.16.k_ref
  131.9 2.5 fusion.17.q_ref
  134.4 2.5 fusion.18.v_ref
  137.0 34.6 %shard_map.198 = bf16[1024,768]{1,0:T(8,128)(2,1)} custom-call(s32[2,512,1]{2,1,0:T(8,128)} %fusion.26.seg_col, s32[2,1,512]{2,1,0:T(1,128)} %compare_select_fusion.seg_row, bf16[1024,768]{1,0:T(8,128)(2,1)} %fusion.17.q_ref, bf16[1024,768]{1,0:T(8,128)(2,1)} %fusion.16.k_ref, bf16[1024,768]{1,0:T(8,128)(2,1)} %fusion.18.v_ref), custom_call_target="tpu_custom_call" | custom-call | flops 1610612736 | bytes 6291456 | tf_op jit(solution)/shard_map/pallas_call | solution.py:238
  171.6 3.4 fusion.53
  175.6 9.3 %multiply_convert_fusion.1 = (bf16[1024,3072]{1,0:T(8,128)(2,1)S(1)}, f32[1024,3072]{1,0:T(8,128)}) fusion(f32[3072]{0:T(1024)S(1)} %slice.36, bf16[768,3072]{1,0:T(8,128)(2,1)S(1)} %bitcast.192, f32[1024,768]{1,0:T(8,128)S(1)} %get-tuple-element.59, f32[768]{0:T(1024)S(1)} %get-tuple-element.50, f32[768]{0:T(1024)S(1)} %get-tuple-element.51, ...), kind=kOutput, calls=%fused_computation.10 | convolution fusion | flops 4854644736 | bytes 26765312 | tf_op jit(solution)/shard_map/dot_general | solution.py:326
  185.0 5.4 %fusion.54 = (f32[1024]{0:T(1024)S(1)}, f32[1024,768]{1,0:T(8,128)S(1)}) fusion(f32[768]{0:T(1024)S(1)} %get-tuple-element.48, bf16[1024,3072]{1,0:T(8,128)(2,1)S(1)} %get-tuple-element.60, bf16[3072,768]{1,0:T(8,128)(2,1)S(1)} %bitcast.196, f32[768]{0:T(1024)S(1)} %get-tuple-element.50, f32[768]{0:T(1024)S(1)} %get-tuple-element.51, ...), kind=kOutput, calls=%fused_computation.149 | convolution fusion | flops 4837342208 | bytes 17323008 | tf_op jit(solution)/shard_map/dot_general | solution.py:329
  191.0 2.8 fusion.51
  193.8 1.4 gather_fusion
  195.6 0.8 collective-permute-done
  197.2 2.1 convert_multiply_fusion
  199.6 2.4 scatter_fusion
  202.0 3.9 fusion.7
  206.7 1.6 fusion.50
  209.0 7.0 %multiply_convert_fusion.2 = bf16[3072,768]{1,0:T(8,128)(2,1)} fusion(bf16[1024,3072]{1,0:T(8,128)(2,1)S(1)} %bitcast.207, bf16[1024,768]{1,0:T(8,128)(2,1)S(1)} %get-tuple-element.35), kind=kOutput, calls=%fused_computation.12 | convolution fusion | flops 4836556800 | bytes 12582912 | tf_op jit(solution)/shard_map/tf,td->fd/dot_general | solution.py:363
  216.1 11.8 %convert_reduce_fusion = (f32[3072]{0:T(1024)S(1)}, bf16[1024,3072]{1,0:T(8,128)(2,1)S(1)}) fusion(f32[1024,3072]{1,0:T(8,128)} %get-tuple-element.61, f32[3072]{0:T(1024)S(1)} %slice.36, bf16[1024,768]{1,0:T(8,128)(2,1)S(1)} %get-tuple-element.35, bf16[3072,768]{1,0:T(8,128)(2,1)S(1)} %bitcast.198), kind=kOutput, calls=%fused_computation.8 | convolution fusion | flops 4879021056 | bytes 25190400 | tf_op jit(solution)/shard_map/td,fd->tf/dot_general | solution.py:366
  227.9 6.1 %multiply_reduce_fusion = (f32[768]{0:T(1024)S(1)}, f32[1024]{0:T(1024)S(1)}, f32[768]{0:T(1024)S(1)}, f32[1024,768]{1,0:T(8,128)S(1)}) fusion(f32[1024,768]{1,0:T(8,128)S(1)} %copy-done.7, f32[1024]{0:T(1024)S(1)} %fusion.35, f32[1024]{0:T(1024)S(1)} %broadcast_multiply_fusion.2, f32[768]{0:T(1024)S(1)} %get-tuple-element.51, ...), kind=kOutput, calls=%fused_computation.28 | convolution fusion | flops 4839699456 | bytes 20472832 | tf_op jit(solution)/shard_map/tf,df->td/dot_general | solution.py:372
  234.0 8.4 %multiply_convert_fusion.3 = bf16[768,3072]{1,0:T(8,128)(2,1)} fusion(bf16[1024,3072]{1,0:T(8,128)(2,1)S(1)} %get-tuple-element.68, f32[1024,768]{1,0:T(8,128)S(1)} %copy-done.7, f32[768]{0:T(1024)S(1)} %get-tuple-element.50, f32[768]{0:T(1024)S(1)} %get-tuple-element.51, f32[1024]{0:T(1024)S(1)} %fusion.35, f32[1024]{0:T(1024)S(1)} %broadcast_multiply_fusion.2), kind=kOutput, calls=%fused_computation.13 | convolution fusion | flops 4840488960 | bytes 14170112 | tf_op jit(solution)/shard_map/td,tf->df/dot_general | solution.py:369
  242.4 1.4 fusion.49
  243.9 1.7 copy-done.4
  246.0 2.6 convolution_convert_fusion.1.g_ref
  248.6 36.3 %shard_map.199 = (bf16[1024,768]{1,0:T(8,128)(2,1)}, bf16[1024,768]{1,0:T(8,128)(2,1)}, bf16[1024,768]{1,0:T(8,128)(2,1)}) custom-call(s32[2,512,1]{2,1,0:T(8,128)} %fusion.26.seg_col, s32[2,1,512]{2,1,0:T(1,128)} %compare_select_fusion.seg_row, bf16[1024,768]{1,0:T(8,128)(2,1)} %fusion.17.q_ref, bf16[1024,768]{1,0:T(8,128)(2,1)} %fusion.16.k_ref, ...), custom_call_target="tpu_custom_call" | custom-call | flops 4026531840 | bytes 11010048 | tf_op jit(solution)/shard_map/pallas_call | solution.py:238
  285.0 3.5 multiply_convert_fusion.6
  288.5 1.0 dynamic-slice_bitcast_fusion.3
  289.7 1.5 multiply_convert_fusion.7
  291.2 1.0 copy-done.21
  292.2 0.9 dynamic-slice_bitcast_fusion.4
  293.4 1.6 dynamic-slice_bitcast_fusion
  295.2 1.6 dynamic-slice_bitcast_fusion.1
  297.0 2.5 multiply_convert_fusion.4
  299.5 2.5 multiply_convert_fusion.5
  302.0 2.7 reshape.321
  304.8 2.0 dynamic-slice_bitcast_fusion.2
  307.0 3.8 constant_dynamic-slice_fusion.1
  310.8 3.4 copy.92
  314.2 3.6 copy.74
  318.2 2.3 fusion.21
  320.5 2.2 fusion.22
  322.7 2.0 fusion.20
  324.7 1.0 fusion.19
  325.7 4.4 fusion.5
  330.1 4.1 fusion.6
  334.8 6.8 %shard_map.200 = bf16[112,128,256]{2,1,0:T(8,128)(2,1)} custom-call(s32[108]{0:T(128)} %slot_ref.3, bf16[128,256]{1,0:T(8,128)(2,1)} %broadcast_in_dim.38.zero_ref, bf16[384,768]{1,0:T(8,128)(2,1)} %bitcast.173, bf16[384,768]{1,0:T(8,128)(2,1)} %bitcast.172, bf16[384,768]{1,0:T(8,128)(2,1)} %bitcast.174, bf16[384,768]{1,0:T(8,128)(2,1)} %bitcast.171, ...), custom_call_target="tpu_custom_call" | custom-call | bytes 14680064 | tf_op jit(solution)/shard_map/pallas_call | solution.py:126
  341.7 2.2 reduce_sum.198
  344.0 1.9 convert_reduce_fusion.3
  346.0 48.3 %psum.7 = f32[9216]{0:T(1024)S(1)} all-reduce(f32[9216]{0:T(1024)S(1)} %broadcast_multiply_fusion), channel_id=1, replica_groups=mesh['pair'=2,'dp'=16] {'pair','dp'}, use_global_device_ids=true, to_apply=%region_23.24 | all-reduce | flops 9216 | bytes 73728 | tf_op jit(solution)/shard_map/psum | solution.py:423
  394.4 3.3 fusion.57
  397.7 1.4 fusion.56
  400.0 3.1 add_add_fusion.2
  403.1 0.8 pad_maximum_fusion
  403.9 94.5 %reduce-scatter.2.cloned.1.call-done = bf16[7,128,256]{2,1,0:T(8,128)(2,1)} async-done(((bf16[112,128,256]{2,1,0:T(8,128)(2,1)}), bf16[7,128,256]{2,1,0:T(8,128)(2,1)}) %reduce-scatter.2.cloned.1.call-update) | async-done | bytes 458768 | tf_op jit(solution)/shard_map/reduce_scatter | solution.py:431
  498.4 3.4 all_gather.11
  501.8 1.4 convert_element_type.263
  503.2 1.8 fusion.58
  505.0 2.3 multiply_add_fusion.2
  507.4 2.9 fusion.10
  510.3 3.4 multiply_subtract_fusion
  (171 shorter events, 11.1 us)
Async XLA Ops:
  7.2 497.8 %copy-start = (f32[7,256,256]{2,1,0:T(8,128)S(1)}, f32[7,256,256]{2,1,0:T(8,128)}, u32[]{:S(2)}) copy-start(f32[7,256,256]{2,1,0:T(8,128)} %param.24) | copy-start | bytes 5505028
  7.2 109.7 %all-gather.3.cloned.1.call-start = ((), (), s32[]{:S(2)}) async-start(), calls=%async_computation.2 | async-start | bytes 15138816 | tf_op jit(solution)/shard_map/all_gather | solution.py:279
  9.4 489.0 %reduce-scatter.2.cloned.1.call-start = ((), (), s32[]{:S(2)}) async-start(), calls=%async_computation.1 | async-start | bytes 7798784 | tf_op jit(solution)/shard_map/reduce_scatter | solution.py:431
  116.9 11.1 %copy-start.29 = (bf16[1,2,512,768]{3,2,1,0:T(8,128)(2,1)S(1)}, bf16[1,2,512,768]{3,2,1,0:T(8,128)(2,1)}, u32[]{:S(2)}) copy-start(bf16[1,2,512,768]{3,2,1,0:T(8,128)(2,1)} %param.14) | copy-start | bytes 4718596
  128.0 3.9 copy-start.31
  131.9 2.5 copy-start.19
  171.6 4.0 slice-start.6
  171.6 4.0 slice-start.7
  175.0 9.9 %copy-start.6 = (f32[1024,768]{1,0:T(8,128)}, f32[1024,768]{1,0:T(8,128)S(1)}, u32[]{:S(2)}) copy-start(f32[1024,768]{1,0:T(8,128)S(1)} %get-tuple-element.59) | copy-start | bytes 9437188
  175.0 9.9 %slice-start.10 = ((s8[4718592]{0:T(1024)(128)(4,1)}), s8[4194304]{0:T(1024)(128)(4,1)S(1)}, s32[]{:S(2)}) async-start(s8[4718592]{0:T(1024)(128)(4,1)} %bitcast.195), calls=%async_computation.13 | async-start | bytes 8388608
  175.6 9.4 %slice-start.11 = ((s8[4718592]{0:T(1024)(128)(4,1)}), s8[524288]{0:T(1024)(128)(4,1)S(1)}, s32[]{:S(2)}) async-start(s8[4718592]{0:T(1024)(128)(4,1)} %bitcast.195), calls=%async_computation.14 | async-start | bytes 1048576
  184.9 5.5 %copy-start.35 = (bf16[1024,3072]{1,0:T(8,128)(2,1)}, bf16[1024,3072]{1,0:T(8,128)(2,1)S(1)}, u32[]{:S(2)}) copy-start(bf16[1024,3072]{1,0:T(8,128)(2,1)S(1)} %get-tuple-element.60) | copy-start | bytes 18874372
  190.4 3.4 copy-start.2
  191.0 5.7 %copy-start.28 = (s32[1,1,8]{2,1,0:T(1,128)S(1)}, s32[1,1,8]{2,1,0:T(1,128)}, u32[]{:S(2)}) copy-start(s32[1,1,8]{2,1,0:T(1,128)} %param.18) | copy-start | bytes 100
  191.0 6.2 %copy-start.18 = (bf16[1,2,512,768]{3,2,1,0:T(8,128)(2,1)S(1)}, bf16[1,2,512,768]{3,2,1,0:T(8,128)(2,1)}, u32[]{:S(2)}) copy-start(bf16[1,2,512,768]{3,2,1,0:T(8,128)(2,1)} %param.15) | copy-start | bytes 4718596
  195.2 1.2 collective-permute-start
  196.9 2.5 collective-permute-start.1
  202.0 4.0 copy-start.1
  202.0 4.7 copy-start.3
  206.0 2.7 slice-start.14
  206.7 2.3 slice-start.15
  208.3 7.7 %slice-start.12 = ((s8[4718592]{0:T(1024)(128)(4,1)}), s8[4194304]{0:T(1024)(128)(4,1)S(1)}, s32[]{:S(2)}) async-start(s8[4718592]{0:T(1024)(128)(4,1)} %bitcast.197), calls=%async_computation.15 | async-start | bytes 8388608
  209.0 7.0 %slice-start.13 = ((s8[4718592]{0:T(1024)(128)(4,1)}), s8[524288]{0:T(1024)(128)(4,1)S(1)}, s32[]{:S(2)}) async-start(s8[4718592]{0:T(1024)(128)(4,1)} %bitcast.197), calls=%async_computation.16 | async-start | bytes 1048576
  209.0 18.9 %slice-start.8 = ((s8[4718592]{0:T(1024)(128)(4,1)}), s8[4194304]{0:T(1024)(128)(4,1)S(1)}, s32[]{:S(2)}) async-start(s8[4718592]{0:T(1024)(128)(4,1)} %bitcast.193), calls=%async_computation.11 | async-start | bytes 8388608
  216.0 11.9 %copy-start.7 = (f32[1024,768]{1,0:T(8,128)S(1)}, f32[1024,768]{1,0:T(8,128)}, u32[]{:S(2)}) copy-start(f32[1024,768]{1,0:T(8,128)} %copy-done.6) | copy-start | bytes 9437188
  216.0 11.9 %slice-start.9 = ((s8[4718592]{0:T(1024)(128)(4,1)}), s8[524288]{0:T(1024)(128)(4,1)S(1)}, s32[]{:S(2)}) async-start(s8[4718592]{0:T(1024)(128)(4,1)} %bitcast.193), calls=%async_computation.12 | async-start | bytes 1048576
  243.9 1.8 copy-start.4
  243.9 2.1 copy-start.33
  285.0 4.7 copy-start.16
  285.0 4.7 copy-start.30
  285.0 8.4 %slice-start = ((s8[4718592]{0:T(1024)(128)(4,1)}), s8[4194304]{0:T(1024)(128)(4,1)S(1)}, s32[]{:S(2)}) async-start(s8[4718592]{0:T(1024)(128)(4,1)} %bitcast.160), calls=%async_computation.3 | async-start | bytes 8388608
  288.5 1.2 copy-start.22
  289.4 28.4 %collective-permute-start.3 = (bf16[3,128,768]{2,1,0:T(8,128)(2,1)}, bf16[3,128,768]{2,1,0:T(8,128)(2,1)}, u32[]{:S(2)}, u32[]{:S(2)}) collective-permute-start(bf16[3,128,768]{2,1,0:T(8,128)(2,1)} %dynamic-slice_bitcast_fusion.3), channel_id=1, source_target_pairs={{0,16},{16,0},{1,17},{17,1},{2,18},{18,2},{3,19},{19,3},{4,20},{20... | collective-permute-start | bytes 1769480 | tf_op jit(solution)/shard_map/ppermute | solution.py:31
  289.7 5.5 %slice-start.2 = ((s8[4718592]{0:T(1024)(128)(4,1)}), s8[4194304]{0:T(1024)(128)(4,1)S(1)}, s32[]{:S(2)}) async-start(s8[4718592]{0:T(1024)(128)(4,1)} %bitcast.163), calls=%async_computation.5 | async-start | bytes 8388608
  289.7 3.7 slice-start.1
  289.7 5.5 %slice-start.3 = ((s8[4718592]{0:T(1024)(128)(4,1)}), s8[524288]{0:T(1024)(128)(4,1)S(1)}, s32[]{:S(2)}) async-start(s8[4718592]{0:T(1024)(128)(4,1)} %bitcast.163), calls=%async_computation.6 | async-start | bytes 1048576
  291.2 1.0 copy-start.21
  293.1 27.4 %collective-permute-start.2 = (bf16[3,128,768]{2,1,0:T(8,128)(2,1)}, bf16[3,128,768]{2,1,0:T(8,128)(2,1)}, u32[]{:S(2)}, u32[]{:S(2)}) collective-permute-start(bf16[3,128,768]{2,1,0:T(8,128)(2,1)} %dynamic-slice_bitcast_fusion.4), channel_id=1, source_target_pairs={{0,16},{16,0},{1,17},{17,1},{2,18},{18,2},{3,19},{19,3},{4,20},{20... | collective-permute-start | bytes 1769480 | tf_op jit(solution)/shard_map/ppermute | solution.py:31
  294.9 2.1 copy-start.34
  294.9 30.8 %collective-permute-start.7 = (bf16[12,128,768]{2,1,0:T(8,128)(2,1)}, bf16[12,128,768]{2,1,0:T(8,128)(2,1)}, u32[]{:S(2)}, u32[]{:S(2)}) collective-permute-start(bf16[12,128,768]{2,1,0:T(8,128)(2,1)} %dynamic-slice_bitcast_fusion), channel_id=1, source_target_pairs={{0,16},{16,0},{1,17},{17,1},{2,18},{18,2},{3,19},{19,3},{4,20},{20... | collective-permute-start | bytes 7077896 | tf_op jit(solution)/shard_map/ppermute | solution.py:31
  296.7 2.8 copy-start.8
  296.7 33.4 %collective-permute-start.6 = (bf16[3,128,3072]{2,1,0:T(8,128)(2,1)}, bf16[3,128,3072]{2,1,0:T(8,128)(2,1)}, u32[]{:S(2)}, u32[]{:S(2)}) collective-permute-start(bf16[3,128,3072]{2,1,0:T(8,128)(2,1)} %dynamic-slice_bitcast_fusion.1), channel_id=1, source_target_pairs={{0,16},{16,0},{1,17},{17,1},{2,18},{18,2},{3,19},{19,3},{4,20},{20... | collective-permute-start | bytes 7077896 | tf_op jit(solution)/shard_map/ppermute | solution.py:31
  306.7 16.0 %collective-permute-start.4 = (bf16[3,128,768]{2,1,0:T(8,128)(2,1)}, bf16[3,128,768]{2,1,0:T(8,128)(2,1)}, u32[]{:S(2)}, u32[]{:S(2)}) collective-permute-start(bf16[3,128,768]{2,1,0:T(8,128)(2,1)} %dynamic-slice_bitcast_fusion.2), channel_id=1, source_target_pairs={{0,16},{16,0},{1,17},{17,1},{2,18},{18,2},{3,19},{19,3},{4,20},{20... | collective-permute-start | bytes 1769480 | tf_op jit(solution)/shard_map/ppermute | solution.py:31
  317.8 4.9 copy-start.23
  317.8 6.9 %collective-permute-start.5 = (bf16[3,128,768]{2,1,0:T(8,128)(2,1)S(1)}, bf16[3,128,768]{2,1,0:T(8,128)(2,1)S(1)}, u32[]{:S(2)}, u32[]{:S(2)}) collective-permute-start(bf16[3,128,768]{2,1,0:T(8,128)(2,1)S(1)} %bitcast.182), channel_id=1, source_target_pairs={{0,16},{16,0},{1,17},{17,1},{2,18},{18,2},{3,19},{19,3},{4,20},{20... | collective-permute-start | bytes 1769480 | tf_op jit(solution)/shard_map/ppermute | solution.py:31
  318.2 11.9 %slice-start.4 = ((s8[4718592]{0:T(1024)(128)(4,1)}), s8[4194304]{0:T(1024)(128)(4,1)S(1)}, s32[]{:S(2)}) async-start(s8[4718592]{0:T(1024)(128)(4,1)} %bitcast.166), calls=%async_computation.7 | async-start | bytes 8388608
  324.7 5.4 %slice-start.5 = ((s8[4718592]{0:T(1024)(128)(4,1)}), s8[524288]{0:T(1024)(128)(4,1)S(1)}, s32[]{:S(2)}) async-start(s8[4718592]{0:T(1024)(128)(4,1)} %bitcast.166), calls=%async_computation.8 | async-start | bytes 1048576
  341.6 2.4 copy-start.9
  394.3 4.9 copy-start.25
  394.3 3.3 copy-start.17
  394.3 3.3 copy-start.32
  397.7 1.5 copy-start.24
  397.7 1.5 copy-start.26
  397.7 1.5 copy-start.27
  397.7 1.9 copy-start.5
  397.7 2.3 copy-start.20
  498.4 4.8 copy-start.11
  501.8 3.2 copy-start.12
  501.8 3.2 copy-start.13
  507.3 3.0 copy-start.14
  507.4 3.0 copy-start.15
  507.4 3.0 copy-start.10
Sparse Core Ops, SparseCore 0:
  11.4 105.3 all-gather.2
  341.8 156.5 reduce-scatter.1

commit v3 on v2

--- a/solution.py
+++ b/solution.py
@@ -134,6 +134,185 @@
             flops=0, bytes_accessed=4 * slot_total * half * side, transcendentals=0
         ),
     )(owner_slot, jnp.zeros((half, side), dtype), *mats)
+
+
+MESH_IDS = pl.DeviceIdType.MESH
+
+
+def spread_body(own_ref, out_ref, send_sem, recv_sem, local_sem):
+    core, me = lax.axis_index("pair"), lax.axis_index("dp")
+    level, rest = lax.div(me, 4), lax.rem(me, 4)
+    flip_y = me + 2 - 4 * lax.div(rest, 2)
+    flip_x = me + 1 - 2 * lax.rem(rest, 2)
+    first = (1 - core) * flip_y + core * flip_x
+    second = (1 - core) * flip_x + core * flip_y
+    both = flip_x + flip_y - me
+    targets = (
+        (core, me + 4), (core, me - 4), (core, first), (core, second), (1 - core, me)
+    )
+
+    barrier = pltpu.get_barrier_semaphore()
+
+    def greet(kind):
+        pl.semaphore_signal(barrier, inc=1, device_id=targets[kind], device_id_type=MESH_IDS)
+
+    @pl.when(level < 3)
+    def _():
+        greet(0)
+
+    @pl.when(level > 0)
+    def _():
+        greet(1)
+
+    for kind in (2, 3, 4):
+        greet(kind)
+
+    pl.semaphore_wait(barrier, 3 + lax.div(level + 3, 4) + lax.div(6 - level, 4))
+
+    def link(kind, source, piece=None):
+        place = source * 2 + core
+        return pltpu.make_async_remote_copy(
+            src_ref=out_ref.at[place] if piece is None else piece,
+            dst_ref=out_ref.at[place],
+            send_sem=send_sem.at[kind, source],
+            recv_sem=recv_sem.at[kind // 4, source],
+            device_id=targets[kind],
+            device_id_type=MESH_IDS,
+        )
+
+    def walk(act):
+        def line(base, step, kinds, up=(), down=()):
+            @pl.when(level >= step)
+            def _():
+                act(base - 4 * step, kinds, up)
+
+            @pl.when(level + step <= 3)
+            def _():
+                act(base + 4 * step, kinds, down)
+
+        line(me, 1, (3, 2, 4), (0,), (1,))
+        act(first, (3, 4), ())
+        line(me, 2, (3, 2, 4), (0,), (1,))
+        line(first, 1, (3, 4))
+        line(me, 3, (3, 2, 4), (0,), (1,))
+        line(first, 2, (3, 4))
+        line(first, 3, (3, 4))
+        act(second, (4,), ())
+        line(second, 1, (4,))
+        act(both, (4,), ())
+        line(second, 2, (4,))
+        line(both, 1, (4,))
+        line(second, 3, (4,))
+        line(both, 2, (4,))
+        line(both, 3, (4,))
+
+    def guarded(kind, run):
+        if kind == 0:
+            pl.when(level < 3)(run)
+        elif kind == 1:
+            pl.when(level > 0)(run)
+        else:
+            run()
+
+    def go(source, kinds, further):
+        link(0, source).wait_recv()
+        for kind in further + kinds:
+            guarded(kind, lambda kind=kind: link(kind, source).start())
+
+    def drain(source, kinds, further):
+        for kind in further + kinds:
+            guarded(kind, lambda kind=kind: link(kind, source).wait_send())
+
+    for kind in range(5):
+        guarded(kind, lambda kind=kind: link(kind, me, own_ref).start())
+    local = pltpu.make_async_copy(own_ref, out_ref.at[me * 2 + core], local_sem)
+    local.start()
+    walk(go)
+    for kind in range(5):
+        guarded(kind, lambda kind=kind: link(kind, me, own_ref).wait_send())
+    walk(drain)
+
+    @pl.loop(0, 16)
+    def _(source):
+        pltpu.make_async_remote_copy(
+            src_ref=own_ref,
+            dst_ref=out_ref.at[source * 2 + 1 - core],
+            send_sem=send_sem.at[4, source],
+            recv_sem=recv_sem.at[1, source],
+            device_id=targets[4],
+            device_id_type=MESH_IDS,
+        ).wait_recv()
+
+    local.wait()
+
+
+def spread(own, data_count, pair_count):
+    if (data_count, pair_count) != (16, 2):
+        return lax.all_gather(own, ("dp", "pair"), axis=0)
+    return pl.pallas_call(
+        spread_body,
+        in_specs=[pl.BlockSpec(memory_space=pl.ANY)],
+        out_specs=pl.BlockSpec(memory_space=pl.ANY),
+        out_shape=jax.ShapeDtypeStruct((32,) + own.shape, own.dtype),
+        scratch_shapes=[
+            pltpu.SemaphoreType.DMA((5, 16)),
+            pltpu.SemaphoreType.DMA((2, 16)),
+            pltpu.SemaphoreType.DMA,
+        ],
+        compiler_params=pltpu.CompilerParams(collective_id=1, has_side_effects=True),
+    )(own)
+
+
+def vector_body(rounds, part_ref, total_ref, held, landed, send_sem, recv_sem):
+    core, me = lax.axis_index("pair"), lax.axis_index("dp")
+    partners = [(1 - core, me)]
+    for step in range(rounds - 1):
+        bit = 2**step
+        partners.append((core, me + bit - 2 * bit * lax.rem(lax.div(me, bit), 2)))
+    barrier = pltpu.get_barrier_semaphore()
+    for partner in partners:
+        pl.semaphore_signal(barrier, inc=1, device_id=partner, device_id_type=MESH_IDS)
+    pl.semaphore_wait(barrier, rounds)
+    for step, partner in enumerate(partners):
+        source = part_ref if step == 0 else held.at[step - 1]
+        copy = pltpu.make_async_remote_copy(
+            src_ref=source,
+            dst_ref=landed.at[step],
+            send_sem=send_sem.at[step],
+            recv_sem=recv_sem.at[step],
+            device_id=partner,
+            device_id_type=MESH_IDS,
+        )
+        copy.start()
+        copy.wait()
+        total = source[...] + landed[step]
+        if step < rounds - 1:
+            held[step] = total
+        else:
+            total_ref[...] = total
+
+
+def vector_total(part, data_count, pair_count):
+    rounds = data_count.bit_length()
+    if pair_count != 2 or 2 ** (rounds - 1) != data_count:
+        return lax.psum(part, ("pair", "dp"))
+    shape = (part.shape[0] // 128, 128)
+    return pl.pallas_call(
+        functools.partial(vector_body, rounds),
+        in_specs=[pl.BlockSpec(memory_space=pltpu.VMEM)],
+        out_specs=pl.BlockSpec(memory_space=pltpu.VMEM),
+        out_shape=jax.ShapeDtypeStruct(shape, part.dtype),
+        scratch_shapes=[
+            pltpu.VMEM((rounds,) + shape, part.dtype),
+            pltpu.VMEM((rounds,) + shape, part.dtype),
+            pltpu.SemaphoreType.DMA((rounds,)),
+            pltpu.SemaphoreType.DMA((rounds,)),
+        ],
+        compiler_params=pltpu.CompilerParams(collective_id=0, has_side_effects=True),
+        cost_estimate=pl.CostEstimate(
+            flops=part.size * rounds, bytes_accessed=8 * part.size * rounds, transcendentals=0
+        ),
+    )(part.reshape(shape)).reshape(-1)
 
 
 def pair_summed(gradient, scale, block_side, core):
@@ -276,7 +455,7 @@
     half = block_side // pair_count
     core = lax.axis_index("pair")
     own_half = lax.dynamic_slice_in_dim(master, core * half, half, axis=1).astype(jnp.bfloat16)
-    gathered = lax.all_gather(own_half, ("dp", "pair"), axis=0)
+    gathered = spread(own_half, data_count, pair_count)
     w_query, w_key, w_value, w_output, w_inner, w_outer = assemble(
         gathered, owner_slot, pair_count
     )
@@ -420,7 +599,6 @@
         )
         * grad_scale
     )
-    vector_grad = lax.psum(local_vector, ("pair", "dp"))
     grad_mats = [
         pair_summed(matrix, grad_scale, block_side, core)
         for matrix in (
@@ -428,6 +606,8 @@
         )
     ]
     own_grad = deal(grad_mats, owner_slot, master.shape[0] * data_count, half, block_side)
+    own_grad, local_vector = lax.optimization_barrier((own_grad, local_vector))
+    vector_grad = vector_total(local_vector, data_count, pair_count)
     own_grad = lax.psum_scatter(own_grad, "dp", scatter_dimension=0, tiled=True)
     owned_grad = lax.all_gather(own_grad, "pair", axis=1, tiled=True).astype(jnp.float32)
     new_master, new_first, new_second = soap_update(

time: 529 us -> 508 us (0.960)
  the two profiles are of different devices: /device:TPU:17 before, /device:TPU:11 now
where the time goes in v3:
time: 508 us; the launch traced here: 499 us
  Pallas kernels  173 us (34%)
  waiting for transfers between devices  132 us (26%)
  matrix products  94 us (19%)
  other arithmetic  44.1 us (9%)
  local copies, waits for them, and re-layouts  35.4 us (7%)
  between operations  15.3 us (3%)
    reduce_scatter x1, waiting for transfers between devices, per_device(): own_grad = lax.psum_scatter(own_grad, 'dp', scatter_dimension=0, tiled=True)  131 us
    pallas_call x2, Pallas kernels, attention_call(): pl.pallas_call(functools.partial(body, D // HEADS), grid=(rows, width //...  70.8 us
    pallas_call x1, Pallas kernels, spread(): pl.pallas_call(spread_body, in_specs=[pl.BlockSpec(memory_space=pl.ANY)],...  66.3 us
    pallas_call x1, Pallas kernels, vector_total(): pl.pallas_call(functools.partial(vector_body, rounds), in_specs=[pl.Block...  17.9 us
    convert_element_type x6, other arithmetic, pair_summed(): return total.astype(jnp.bfloat16).reshape(-1, gradient.shape[1])  15.9 us
    dot_general x1, matrix products, per_device(): jnp.einsum('td,fd->tf', grad_outer, w_outer, preferred_element_type=jnp.f...  12.3 us
    unnamed x118, local copies, waits for them, and re-layouts  11.4 us
    pallas_call x1, Pallas kernels, assemble(): pl.pallas_call(functools.partial(assemble_body, gathered.shape[1], halves...  11.1 us
  transfers between devices with their start and end apart: 9, of which 2 were waited for; matrix products, arithmetic and copies ran while one was open for 10% of the time, Pallas kernels for 4%

profile of v3, /device:TPU:11, one launch (start us, length us, event | category | flops | bytes accessed | tf_op | source)
XLA Modules:
  0.0 499.5 jit_solution(3644487028780638679)
XLA Ops:
  7.2 0.9 squeeze.37
  8.1 0.8 reduce_window_sum.15
  10.4 0.8 fusion.52
  13.1 0.9 fusion.26.seg_col
  14.0 2.0 dynamic-slice_convert_fusion.own_ref
  16.0 66.3 %shard_map.197.gathered_ref = bf16[32,7,128,256]{3,2,1,0:T(8,128)(2,1)} custom-call(bf16[7,128,256]{2,1,0:T(8,128)(2,1)} %dynamic-slice_convert_fusion.own_ref), custom_call_target="tpu_custom_call" | custom-call | tf_op jit(solution)/shard_map/pallas_call | solution.py:252
  82.3 11.1 %shard_map.198 = (bf16[768,768]{1,0:T(8,128)(2,1)}, bf16[768,768]{1,0:T(8,128)(2,1)}, bf16[768,768]{1,0:T(8,128)(2,1)}, bf16[768,768]{1,0:T(8,128)(2,1)}, bf16[7...) custom-call(s32[108]{0:T(128)} %slot_ref.3, bf16[32,7,128,256]{3,2,1,0:T(8,128)(2,1)} %shard_map.197.gathered_ref), custom_call_target="tpu_custom_call" | custom-call | bytes 29360128 | tf_op jit(solution)/shard_map/pallas_call | solution.py:83
  93.4 3.9 fusion.16.k_ref
  97.3 2.5 fusion.17.q_ref
  99.9 2.5 fusion.18.v_ref
  102.4 34.4 %shard_map.199 = bf16[1024,768]{1,0:T(8,128)(2,1)} custom-call(s32[2,512,1]{2,1,0:T(8,128)} %fusion.26.seg_col, s32[2,1,512]{2,1,0:T(1,128)} %compare_select_fusion.seg_row, bf16[1024,768]{1,0:T(8,128)(2,1)} %fusion.17.q_ref, bf16[1024,768]{1,0:T(8,128)(2,1)} %fusion.16.k_ref, bf16[1024,768]{1,0:T(8,128)(2,1)} %fusion.18.v_ref), custom_call_target="tpu_custom_call" | custom-call | flops 1610612736 | bytes 6291456 | tf_op jit(solution)/shard_map/pallas_call | solution.py:417
  136.8 3.4 fusion.53
  140.8 9.5 %multiply_convert_fusion.1 = (bf16[1024,3072]{1,0:T(8,128)(2,1)S(1)}, f32[1024,3072]{1,0:T(8,128)}) fusion(f32[3072]{0:T(1024)S(1)} %slice.36, bf16[768,3072]{1,0:T(8,128)(2,1)S(1)} %bitcast.195, f32[1024,768]{1,0:T(8,128)S(1)} %get-tuple-element.63, f32[768]{0:T(1024)S(1)} %get-tuple-element.54, f32[768]{0:T(1024)S(1)} %get-tuple-element.55, ...), kind=kOutput, calls=%fused_computation.10 | convolution fusion | flops 4854644736 | bytes 26765312 | tf_op jit(solution)/shard_map/dot_general | solution.py:505
  150.4 5.4 %fusion.54 = (f32[1024]{0:T(1024)S(1)}, f32[1024,768]{1,0:T(8,128)S(1)}) fusion(f32[768]{0:T(1024)S(1)} %get-tuple-element.52, bf16[1024,3072]{1,0:T(8,128)(2,1)S(1)} %get-tuple-element.64, bf16[3072,768]{1,0:T(8,128)(2,1)S(1)} %bitcast.199, f32[768]{0:T(1024)S(1)} %get-tuple-element.54, f32[768]{0:T(1024)S(1)} %get-tuple-element.55, ...), kind=kOutput, calls=%fused_computation.149 | convolution fusion | flops 4837342208 | bytes 17323008 | tf_op jit(solution)/shard_map/dot_general | solution.py:508
  156.5 2.8 fusion.51
  159.3 1.4 gather_fusion
  162.1 0.8 convolution_convert_fusion.2
  163.3 2.1 convert_multiply_fusion
  165.7 2.2 scatter_fusion
  167.9 3.9 fusion.7
  172.6 1.6 fusion.50
  174.9 7.0 %multiply_convert_fusion.2 = bf16[3072,768]{1,0:T(8,128)(2,1)} fusion(bf16[1024,3072]{1,0:T(8,128)(2,1)S(1)} %bitcast.210, bf16[1024,768]{1,0:T(8,128)(2,1)S(1)} %get-tuple-element.39), kind=kOutput, calls=%fused_computation.12 | convolution fusion | flops 4836556800 | bytes 12582912 | tf_op jit(solution)/shard_map/tf,td->fd/dot_general | solution.py:542
  181.9 12.3 %convert_reduce_fusion = (f32[3072]{0:T(1024)S(1)}, bf16[1024,3072]{1,0:T(8,128)(2,1)S(1)}) fusion(f32[1024,3072]{1,0:T(8,128)} %get-tuple-element.65, f32[3072]{0:T(1024)S(1)} %slice.36, bf16[1024,768]{1,0:T(8,128)(2,1)S(1)} %get-tuple-element.39, bf16[3072,768]{1,0:T(8,128)(2,1)S(1)} %bitcast.201), kind=kOutput, calls=%fused_computation.8 | convolution fusion | flops 4879021056 | bytes 25190400 | tf_op jit(solution)/shard_map/td,fd->tf/dot_general | solution.py:545
  194.3 7.6 %multiply_reduce_fusion = (f32[768]{0:T(1024)S(1)}, f32[1024]{0:T(1024)S(1)}, f32[768]{0:T(1024)S(1)}, f32[1024,768]{1,0:T(8,128)}) fusion(f32[1024,768]{1,0:T(8,128)S(1)} %copy-done.7, f32[1024]{0:T(1024)S(1)} %fusion.35, f32[1024]{0:T(1024)S(1)} %broadcast_multiply_fusion.2, f32[768]{0:T(1024)S(1)} %get-tuple-element.55, ...), kind=kOutput, calls=%fused_computation.28 | convolution fusion | flops 4839699456 | bytes 20472832 | tf_op jit(solution)/shard_map/tf,df->td/dot_general | solution.py:551
  201.9 8.0 %multiply_convert_fusion.3 = bf16[768,3072]{1,0:T(8,128)(2,1)} fusion(bf16[1024,3072]{1,0:T(8,128)(2,1)S(1)} %get-tuple-element.72, f32[1024,768]{1,0:T(8,128)S(1)} %copy-done.7, f32[768]{0:T(1024)S(1)} %get-tuple-element.54, f32[768]{0:T(1024)S(1)} %get-tuple-element.55, f32[1024]{0:T(1024)S(1)} %fusion.35, f32[1024]{0:T(1024)S(1)} %broadcast_multiply_fusion.2), kind=kOutput, calls=%fused_computation.13 | convolution fusion | flops 4840488960 | bytes 14170112 | tf_op jit(solution)/shard_map/td,tf->df/dot_general | solution.py:548
  209.9 2.1 reduce_sum.198
  212.0 3.5 fusion.49
  215.6 1.6 copy-done.4
  217.7 2.6 convolution_convert_fusion.1.g_ref
  220.4 36.4 %shard_map.200 = (bf16[1024,768]{1,0:T(8,128)(2,1)}, bf16[1024,768]{1,0:T(8,128)(2,1)}, bf16[1024,768]{1,0:T(8,128)(2,1)}) custom-call(s32[2,512,1]{2,1,0:T(8,128)} %fusion.26.seg_col, s32[2,1,512]{2,1,0:T(1,128)} %compare_select_fusion.seg_row, bf16[1024,768]{1,0:T(8,128)(2,1)} %fusion.17.q_ref, bf16[1024,768]{1,0:T(8,128)(2,1)} %fusion.16.k_ref, ...), custom_call_target="tpu_custom_call" | custom-call | flops 4026531840 | bytes 11010048 | tf_op jit(solution)/shard_map/pallas_call | solution.py:417
  256.7 3.5 multiply_convert_fusion.7
  260.8 1.3 copy-done.30
  262.5 1.5 multiply_convert_fusion.6
  264.0 0.9 dynamic-slice_bitcast_fusion.3
  265.1 0.9 dynamic-slice_bitcast_fusion.4
  266.3 1.6 dynamic-slice_bitcast_fusion.1
  267.9 1.6 dynamic-slice_bitcast_fusion
  270.7 2.5 multiply_convert_fusion.4
  273.2 2.5 multiply_convert_fusion.5
  275.7 3.0 reshape.327
  278.7 1.9 dynamic-slice_bitcast_fusion.2
  280.8 3.9 constant_dynamic-slice_fusion.1
  284.7 3.4 copy.75
  288.1 3.4 copy.57
  291.9 2.3 fusion.21
  294.3 2.2 fusion.22
  296.5 2.0 fusion.20
  298.5 1.0 fusion.19
  299.4 4.4 fusion.5
  303.9 4.0 fusion.6
  308.5 6.8 %shard_map.201 = bf16[112,128,256]{2,1,0:T(8,128)(2,1)} custom-call(s32[108]{0:T(128)} %slot_ref.3, bf16[128,256]{1,0:T(8,128)(2,1)} %broadcast_in_dim.38.zero_ref, bf16[384,768]{1,0:T(8,128)(2,1)} %bitcast.174, bf16[384,768]{1,0:T(8,128)(2,1)} %bitcast.173, bf16[384,768]{1,0:T(8,128)(2,1)} %bitcast.175, bf16[384,768]{1,0:T(8,128)(2,1)} %bitcast.172, ...), custom_call_target="tpu_custom_call" | custom-call | bytes 14680064 | tf_op jit(solution)/shard_map/pallas_call | solution.py:126
  315.3 1.2 copy-done.33
  316.5 3.0 fusion.57
  319.6 1.4 fusion.56
  322.2 3.1 add_add_fusion.2
  325.3 17.9 %shard_map.202 = f32[72,128]{1,0:T(8,128)} custom-call(f32[72,128]{1,0:T(8,128)} %bitcast.185), custom_call_target="tpu_custom_call" | custom-call | flops 46080 | bytes 368640 | tf_op jit(solution)/shard_map/pallas_call | solution.py:300
  343.3 0.8 divide_subtract_fusion
  344.9 131.1 %reduce-scatter.2.cloned.1.call-done = bf16[7,128,256]{2,1,0:T(8,128)(2,1)} async-done(((bf16[112,128,256]{2,1,0:T(8,128)(2,1)}), bf16[7,128,256]{2,1,0:T(8,128)(2,1)}) %reduce-scatter.2.cloned.1.call-update) | async-done | bytes 458768 | tf_op jit(solution)/shard_map/reduce_scatter | solution.py:611
  475.9 3.7 all_gather.3
  479.6 1.4 convert_element_type.268
  481.0 1.8 fusion.58
  482.8 2.3 multiply_add_fusion.2
  485.2 2.9 fusion.10
  488.2 3.4 multiply_subtract_fusion
  (174 shorter events, 15.2 us)
Async XLA Ops:
  7.2 475.6 %copy-start = (f32[7,256,256]{2,1,0:T(8,128)S(1)}, f32[7,256,256]{2,1,0:T(8,128)}, u32[]{:S(2)}) copy-start(f32[7,256,256]{2,1,0:T(8,128)} %param.24) | copy-start | bytes 5505028
  7.2 468.8 %reduce-scatter.2.cloned.1.call-start = ((), (), s32[]{:S(2)}) async-start(), calls=%async_computation.1 | async-start | bytes 7798784 | tf_op jit(solution)/shard_map/reduce_scatter | solution.py:611
  82.3 11.1 %copy-start.29 = (bf16[1,2,512,768]{3,2,1,0:T(8,128)(2,1)S(1)}, bf16[1,2,512,768]{3,2,1,0:T(8,128)(2,1)}, u32[]{:S(2)}) copy-start(bf16[1,2,512,768]{3,2,1,0:T(8,128)(2,1)} %param.14) | copy-start | bytes 4718596
  93.4 3.9 copy-start.31
  97.3 2.5 copy-start.19
  136.8 4.0 slice-start.6
  136.8 4.0 slice-start.7
  140.2 10.1 %copy-start.6 = (f32[1024,768]{1,0:T(8,128)}, f32[1024,768]{1,0:T(8,128)S(1)}, u32[]{:S(2)}) copy-start(f32[1024,768]{1,0:T(8,128)S(1)} %get-tuple-element.63) | copy-start | bytes 9437188
  140.3 10.1 %slice-start.10 = ((s8[4718592]{0:T(1024)(128)(4,1)}), s8[4194304]{0:T(1024)(128)(4,1)S(1)}, s32[]{:S(2)}) async-start(s8[4718592]{0:T(1024)(128)(4,1)} %bitcast.198), calls=%async_computation.12 | async-start | bytes 8388608
  140.8 9.6 %slice-start.11 = ((s8[4718592]{0:T(1024)(128)(4,1)}), s8[524288]{0:T(1024)(128)(4,1)S(1)}, s32[]{:S(2)}) async-start(s8[4718592]{0:T(1024)(128)(4,1)} %bitcast.198), calls=%async_computation.13 | async-start | bytes 1048576
  150.4 5.5 %copy-start.37 = (bf16[1024,3072]{1,0:T(8,128)(2,1)}, bf16[1024,3072]{1,0:T(8,128)(2,1)S(1)}, u32[]{:S(2)}) copy-start(bf16[1024,3072]{1,0:T(8,128)(2,1)S(1)} %get-tuple-element.64) | copy-start | bytes 18874372
  155.9 3.4 copy-start.2
  156.4 5.7 %copy-start.28 = (s32[1,1,8]{2,1,0:T(1,128)S(1)}, s32[1,1,8]{2,1,0:T(1,128)}, u32[]{:S(2)}) copy-start(s32[1,1,8]{2,1,0:T(1,128)} %param.18) | copy-start | bytes 100
  156.5 6.8 %copy-start.18 = (bf16[1,2,512,768]{3,2,1,0:T(8,128)(2,1)S(1)}, bf16[1,2,512,768]{3,2,1,0:T(8,128)(2,1)}, u32[]{:S(2)}) copy-start(bf16[1,2,512,768]{3,2,1,0:T(8,128)(2,1)} %param.15) | copy-start | bytes 4718596
  160.7 1.2 collective-permute-start
  163.0 2.5 collective-permute-start.1
  167.9 4.0 copy-start.1
  167.9 4.7 copy-start.3
  171.8 2.7 slice-start.14
  172.6 2.3 slice-start.15
  174.2 7.7 %slice-start.12 = ((s8[4718592]{0:T(1024)(128)(4,1)}), s8[4194304]{0:T(1024)(128)(4,1)S(1)}, s32[]{:S(2)}) async-start(s8[4718592]{0:T(1024)(128)(4,1)} %bitcast.200), calls=%async_computation.14 | async-start | bytes 8388608
  174.9 7.0 %slice-start.13 = ((s8[4718592]{0:T(1024)(128)(4,1)}), s8[524288]{0:T(1024)(128)(4,1)S(1)}, s32[]{:S(2)}) async-start(s8[4718592]{0:T(1024)(128)(4,1)} %bitcast.200), calls=%async_computation.15 | async-start | bytes 1048576
  174.9 19.3 %slice-start.8 = ((s8[4718592]{0:T(1024)(128)(4,1)}), s8[4194304]{0:T(1024)(128)(4,1)S(1)}, s32[]{:S(2)}) async-start(s8[4718592]{0:T(1024)(128)(4,1)} %bitcast.196), calls=%async_computation.10 | async-start | bytes 8388608
  181.9 12.3 %copy-start.7 = (f32[1024,768]{1,0:T(8,128)S(1)}, f32[1024,768]{1,0:T(8,128)}, u32[]{:S(2)}) copy-start(f32[1024,768]{1,0:T(8,128)} %copy-done.6) | copy-start | bytes 9437188
  181.9 12.3 %slice-start.9 = ((s8[4718592]{0:T(1024)(128)(4,1)}), s8[524288]{0:T(1024)(128)(4,1)S(1)}, s32[]{:S(2)}) async-start(s8[4718592]{0:T(1024)(128)(4,1)} %bitcast.196), calls=%async_computation.11 | async-start | bytes 1048576
  215.6 1.7 copy-start.4
  215.6 2.1 copy-start.34
  256.7 3.5 copy-start.8
  256.7 3.5 copy-start.16
  260.2 4.9 copy-start.21
  260.2 1.8 copy-start.30
  260.2 2.3 copy-start.35
  260.3 6.0 %slice-start.2 = ((s8[4718592]{0:T(1024)(128)(4,1)}), s8[4194304]{0:T(1024)(128)(4,1)S(1)}, s32[]{:S(2)}) async-start(s8[4718592]{0:T(1024)(128)(4,1)} %bitcast.164), calls=%async_computation.4 | async-start | bytes 8388608
  260.8 7.1 %slice-start = ((s8[4718592]{0:T(1024)(128)(4,1)}), s8[4194304]{0:T(1024)(128)(4,1)S(1)}, s32[]{:S(2)}) async-start(s8[4718592]{0:T(1024)(128)(4,1)} %bitcast.161), calls=%async_computation.2 | async-start | bytes 8388608
  262.5 3.7 slice-start.3
  262.5 5.4 %slice-start.1 = ((s8[4718592]{0:T(1024)(128)(4,1)}), s8[524288]{0:T(1024)(128)(4,1)S(1)}, s32[]{:S(2)}) async-start(s8[4718592]{0:T(1024)(128)(4,1)} %bitcast.161), calls=%async_computation.3 | async-start | bytes 1048576
  264.0 1.9 copy-start.22
  264.9 26.6 %collective-permute-start.3 = (bf16[3,128,768]{2,1,0:T(8,128)(2,1)}, bf16[3,128,768]{2,1,0:T(8,128)(2,1)}, u32[]{:S(2)}, u32[]{:S(2)}) collective-permute-start(bf16[3,128,768]{2,1,0:T(8,128)(2,1)} %dynamic-slice_bitcast_fusion.3), channel_id=1, source_target_pairs={{0,16},{16,0},{1,17},{17,1},{2,18},{18,2},{3,19},{19,3},{4,20},{20... | collective-permute-start | bytes 1769480 | tf_op jit(solution)/shard_map/ppermute | solution.py:31
  265.9 28.3 %collective-permute-start.2 = (bf16[3,128,768]{2,1,0:T(8,128)(2,1)}, bf16[3,128,768]{2,1,0:T(8,128)(2,1)}, u32[]{:S(2)}, u32[]{:S(2)}) collective-permute-start(bf16[3,128,768]{2,1,0:T(8,128)(2,1)} %dynamic-slice_bitcast_fusion.4), channel_id=1, source_target_pairs={{0,16},{16,0},{1,17},{17,1},{2,18},{18,2},{3,19},{19,3},{4,20},{20... | collective-permute-start | bytes 1769480 | tf_op jit(solution)/shard_map/ppermute | solution.py:31
  267.9 2.9 copy-start.36
  269.5 29.9 %collective-permute-start.7 = (bf16[12,128,768]{2,1,0:T(8,128)(2,1)}, bf16[12,128,768]{2,1,0:T(8,128)(2,1)}, u32[]{:S(2)}, u32[]{:S(2)}) collective-permute-start(bf16[12,128,768]{2,1,0:T(8,128)(2,1)} %dynamic-slice_bitcast_fusion), channel_id=1, source_target_pairs={{0,16},{16,0},{1,17},{17,1},{2,18},{18,2},{3,19},{19,3},{4,20},{20... | collective-permute-start | bytes 7077896 | tf_op jit(solution)/shard_map/ppermute | solution.py:31
  269.7 34.2 %collective-permute-start.6 = (bf16[3,128,3072]{2,1,0:T(8,128)(2,1)}, bf16[3,128,3072]{2,1,0:T(8,128)(2,1)}, u32[]{:S(2)}, u32[]{:S(2)}) collective-permute-start(bf16[3,128,3072]{2,1,0:T(8,128)(2,1)} %dynamic-slice_bitcast_fusion.1), channel_id=1, source_target_pairs={{0,16},{16,0},{1,17},{17,1},{2,18},{18,2},{3,19},{19,3},{4,20},{20... | collective-permute-start | bytes 7077896 | tf_op jit(solution)/shard_map/ppermute | solution.py:31
  280.6 15.8 %collective-permute-start.4 = (bf16[3,128,768]{2,1,0:T(8,128)(2,1)}, bf16[3,128,768]{2,1,0:T(8,128)(2,1)}, u32[]{:S(2)}, u32[]{:S(2)}) collective-permute-start(bf16[3,128,768]{2,1,0:T(8,128)(2,1)} %dynamic-slice_bitcast_fusion.2), channel_id=1, source_target_pairs={{0,16},{16,0},{1,17},{17,1},{2,18},{18,2},{3,19},{19,3},{4,20},{20... | collective-permute-start | bytes 1769480 | tf_op jit(solution)/shard_map/ppermute | solution.py:31
  291.5 5.0 copy-start.23
  291.5 7.0 %collective-permute-start.5 = (bf16[3,128,768]{2,1,0:T(8,128)(2,1)S(1)}, bf16[3,128,768]{2,1,0:T(8,128)(2,1)S(1)}, u32[]{:S(2)}, u32[]{:S(2)}) collective-permute-start(bf16[3,128,768]{2,1,0:T(8,128)(2,1)S(1)} %bitcast.183), channel_id=1, source_target_pairs={{0,16},{16,0},{1,17},{17,1},{2,18},{18,2},{3,19},{19,3},{4,20},{20... | collective-permute-start | bytes 1769480 | tf_op jit(solution)/shard_map/ppermute | solution.py:31
  291.9 12.0 %slice-start.4 = ((s8[4718592]{0:T(1024)(128)(4,1)}), s8[4194304]{0:T(1024)(128)(4,1)S(1)}, s32[]{:S(2)}) async-start(s8[4718592]{0:T(1024)(128)(4,1)} %bitcast.167), calls=%async_computation.6 | async-start | bytes 8388608
  298.5 5.4 %slice-start.5 = ((s8[4718592]{0:T(1024)(128)(4,1)}), s8[524288]{0:T(1024)(128)(4,1)S(1)}, s32[]{:S(2)}) async-start(s8[4718592]{0:T(1024)(128)(4,1)} %bitcast.167), calls=%async_computation.7 | async-start | bytes 1048576
  315.3 1.3 copy-start.33
  316.5 3.0 copy-start.17
  316.5 3.0 copy-start.32
  319.5 1.9 copy-start.5
  319.5 2.3 copy-start.9
  319.5 2.7 copy-start.20
  322.2 21.0 %copy-start.25 = (f32[9216]{0:T(1024)S(1)}, f32[9216]{0:T(1024)}, u32[]{:S(2)}) copy-start(f32[9216]{0:T(1024)} %param.25) | copy-start | bytes 110596
  322.2 21.0 %copy-start.26 = (f32[9216]{0:T(1024)S(1)}, f32[9216]{0:T(1024)}, u32[]{:S(2)}) copy-start(f32[9216]{0:T(1024)} %param.26) | copy-start | bytes 110596
  322.2 21.0 %copy-start.27 = (f32[9216]{0:T(1024)S(1)}, f32[9216]{0:T(1024)}, u32[]{:S(2)}) copy-start(f32[9216]{0:T(1024)} %param.27) | copy-start | bytes 110596
  475.9 5.1 %copy-start.11 = (f32[7,256,256]{2,1,0:T(8,128)S(1)}, f32[7,256,256]{2,1,0:T(8,128)}, u32[]{:S(2)}) copy-start(f32[7,256,256]{2,1,0:T(8,128)} %param.23) | copy-start | bytes 5505028
  479.6 3.2 copy-start.12
  479.6 3.2 copy-start.13
  485.2 3.0 copy-start.14
  485.2 3.0 copy-start.15
  485.2 3.0 copy-start.10
  488.1 3.4 copy-start.24
Sparse Core Ops, SparseCore 0:
  315.4 160.4 reduce-scatter.1

commit v4 on v3

--- a/solution.py
+++ b/solution.py
@@ -261,6 +261,166 @@
         ],
         compiler_params=pltpu.CompilerParams(collective_id=1, has_side_effects=True),
     )(own)
+
+
+def fold_body(own_ref, out_ref, land, send_sem, recv_sem):
+    core, me = lax.axis_index("pair"), lax.axis_index("dp")
+    level, rest = lax.div(me, 4), lax.rem(me, 4)
+    flip_y = me + 2 - 4 * lax.div(rest, 2)
+    flip_x = me + 1 - 2 * lax.rem(rest, 2)
+    first = (1 - core) * flip_y + core * flip_x
+    second = (1 - core) * flip_x + core * flip_y
+    both = flip_x + flip_y - me
+    targets = ((core, second), (core, second), (core, first), (core, me + 4), (core, me - 4))
+    barrier = pltpu.get_barrier_semaphore()
+
+    def greet(kind):
+        pl.semaphore_signal(barrier, inc=1, device_id=targets[kind], device_id_type=MESH_IDS)
+
+    @pl.when(level < 3)
+    def _():
+        greet(3)
+
+    @pl.when(level > 0)
+    def _():
+        greet(4)
+
+    greet(0)
+    greet(2)
+    pl.semaphore_wait(barrier, 2 + lax.div(level + 3, 4) + lax.div(6 - level, 4))
+
+    def link(kind, place, source):
+        return pltpu.make_async_remote_copy(
+            src_ref=source,
+            dst_ref=land.at[kind, place],
+            send_sem=send_sem.at[kind, place],
+            recv_sem=recv_sem.at[kind, place],
+            device_id=targets[kind],
+            device_id_type=MESH_IDS,
+        )
+
+    def landed(kind, place):
+        link(kind, place, land.at[kind, place]).wait_recv()
+
+    def levels(step, act):
+        if step == 0:
+            act(level, 0)
+            return
+
+        @pl.when(level >= step)
+        def _():
+            act(level - step, -1)
+
+        @pl.when(level + step <= 3)
+        def _():
+            act(level + step, 1)
+
+    def column(base, place):
+        return base + 4 * (place - level)
+
+    def total(piece, place, kinds, store):
+        @pl.loop(0, own_ref.shape[1])
+        def _(row):
+            value = own_ref[piece, row].astype(jnp.float32)
+            for kind in kinds:
+                value = value + land[kind, place, row].astype(jnp.float32)
+            store(row, value.astype(land.dtype))
+
+    def send_second(kind, base):
+        def act(place, side):
+            link(kind, place, own_ref.at[column(base, place)]).start()
+
+        return act
+
+    def send_first(place, side):
+        landed(1, place)
+
+        def store(row, value):
+            land[1, place, row] = value
+
+        total(column(first, place), place, (1,), store)
+        link(2, place, land.at[1, place]).start()
+
+    def send_along(place, side):
+        landed(0, place)
+        landed(2, place)
+        kind = 3 if side > 0 else 4
+        ends = level == (0 if side > 0 else 3)
+
+        def store(row, value):
+            land[0, place, row] = value
+
+        @pl.when(ends)
+        def _():
+            total(column(me, place), place, (0, 2), store)
+
+        @pl.when(jnp.logical_not(ends))
+        def _():
+            landed(kind, place)
+            total(column(me, place), place, (0, 2, kind), store)
+
+        link(kind, place, land.at[0, place]).start()
+
+    for step, kind in ((3, 1), (2, 1), (3, 0), (1, 1), (2, 0), (0, 1), (1, 0), (0, 0)):
+        levels(step, send_second(kind, both if kind else second))
+    levels(3, send_first)
+    levels(2, send_first)
+    levels(3, send_along)
+    levels(1, send_first)
+    levels(2, send_along)
+    levels(0, send_first)
+    levels(1, send_along)
+
+    def keep(row, value):
+        out_ref[row] = value
+
+    landed(0, level)
+    landed(2, level)
+
+    @pl.when(level == 0)
+    def _():
+        landed(4, level)
+        total(me, level, (0, 2, 4), keep)
+
+    @pl.when(level == 3)
+    def _():
+        landed(3, level)
+        total(me, level, (0, 2, 3), keep)
+
+    @pl.when(jnp.logical_and(level > 0, level < 3))
+    def _():
+        landed(3, level)
+        landed(4, level)
+        total(me, level, (0, 2, 3, 4), keep)
+
+    for step in range(4):
+        for kind in range(3):
+            levels(step, lambda place, side, kind=kind: link(kind, place, land.at[0, 0]).wait_send())
+        if step:
+            levels(
+                step,
+                lambda place, side: link(
+                    3 if side > 0 else 4, place, land.at[0, 0]
+                ).wait_send(),
+            )
+
+
+def fold(dealt, data_count, pair_count):
+    if (data_count, pair_count) != (16, 2):
+        return lax.psum_scatter(dealt, "dp", scatter_dimension=0, tiled=True)
+    pieces = dealt.reshape((16, dealt.shape[0] // 16) + dealt.shape[1:])
+    return pl.pallas_call(
+        fold_body,
+        in_specs=[pl.BlockSpec(memory_space=pltpu.VMEM)],
+        out_specs=pl.BlockSpec(memory_space=pltpu.VMEM),
+        out_shape=jax.ShapeDtypeStruct(pieces.shape[1:], dealt.dtype),
+        scratch_shapes=[
+            pltpu.VMEM((5, 4) + pieces.shape[1:], dealt.dtype),
+            pltpu.SemaphoreType.DMA((5, 4)),
+            pltpu.SemaphoreType.DMA((5, 4)),
+        ],
+        compiler_params=pltpu.CompilerParams(collective_id=2, has_side_effects=True),
+    )(pieces)
 
 
 def vector_body(rounds, part_ref, total_ref, held, landed, send_sem, recv_sem):
@@ -606,9 +766,8 @@
         )
     ]
     own_grad = deal(grad_mats, owner_slot, master.shape[0] * data_count, half, block_side)
-    own_grad, local_vector = lax.optimization_barrier((own_grad, local_vector))
     vector_grad = vector_total(local_vector, data_count, pair_count)
-    own_grad = lax.psum_scatter(own_grad, "dp", scatter_dimension=0, tiled=True)
+    own_grad = fold(own_grad, data_count, pair_count)
     owned_grad = lax.all_gather(own_grad, "pair", axis=1, tiled=True).astype(jnp.float32)
     new_master, new_first, new_second = soap_update(
         owned_grad, master, first_moment, second_moment, left_basis, right_basis

time: 508 us -> 441 us (0.87)
  the two profiles are of different devices: /device:TPU:11 before, /device:TPU:17 now
where the time goes in v4:
time: 441 us; the launch traced here: 432 us
  Pallas kernels  241 us (55%)
  matrix products  96.6 us (22%)
  other arithmetic  41.3 us (9%)
  local copies, waits for them, and re-layouts  40.4 us (9%)
  blocking collectives  5.14 us (1%)
  starting transfers between devices  4.79 us (1%)
    pallas_call x1, Pallas kernels, fold(): pl.pallas_call(fold_body, in_specs=[pl.BlockSpec(memory_space=pltpu.VMEM)...  71.6 us
    pallas_call x2, Pallas kernels, attention_call(): pl.pallas_call(functools.partial(body, D // HEADS), grid=(rows, width //...  70.7 us
    pallas_call x1, Pallas kernels, spread(): pl.pallas_call(spread_body, in_specs=[pl.BlockSpec(memory_space=pl.ANY)],...  66.8 us
    convert_element_type x6, other arithmetic, pair_summed(): return total.astype(jnp.bfloat16).reshape(-1, gradient.shape[1])  16 us
    pallas_call x1, Pallas kernels, vector_total(): pl.pallas_call(functools.partial(vector_body, rounds), in_specs=[pl.Block...  13.7 us
    squeeze x5, local copies, waits for them, and re-layouts, pair_summed(): sent = lax.dynamic_index_in_dim(parts, 1 - core, axis=1, keepdims=False)  12.6 us
    dot_general x1, matrix products, per_device(): jnp.einsum('td,fd->tf', grad_outer, w_outer, preferred_element_type=jnp.f...  12.4 us
    pallas_call x1, Pallas kernels, assemble(): pl.pallas_call(functools.partial(assemble_body, gathered.shape[1], halves...  11.2 us
  transfers between devices with their start and end apart: 8, of which 1 were waited for; matrix products, arithmetic and copies ran while one was open for 11% of the time, Pallas kernels for 0%

profile of v4, /device:TPU:17, one launch (start us, length us, event | category | flops | bytes accessed | tf_op | source)
XLA Modules:
  0.0 431.9 jit_solution(9136550723277032931)
XLA Ops:
  0.7 0.9 squeeze.37
  1.5 0.8 reduce_window_sum.15
  6.5 0.9 fusion.26.seg_col
  7.4 2.0 dynamic-slice_convert_fusion.own_ref
  9.4 66.8 %shard_map.197.gathered_ref = bf16[32,7,128,256]{3,2,1,0:T(8,128)(2,1)} custom-call(bf16[7,128,256]{2,1,0:T(8,128)(2,1)} %dynamic-slice_convert_fusion.own_ref), custom_call_target="tpu_custom_call" | custom-call | tf_op jit(solution)/shard_map/pallas_call | solution.py:252
  76.2 11.2 %shard_map.198 = (bf16[768,768]{1,0:T(8,128)(2,1)}, bf16[768,768]{1,0:T(8,128)(2,1)}, bf16[768,768]{1,0:T(8,128)(2,1)}, bf16[768,768]{1,0:T(8,128)(2,1)}, bf16[7...) custom-call(s32[108]{0:T(128)} %slot_ref.3, bf16[32,7,128,256]{3,2,1,0:T(8,128)(2,1)} %shard_map.197.gathered_ref), custom_call_target="tpu_custom_call" | custom-call | bytes 29360128 | tf_op jit(solution)/shard_map/pallas_call | solution.py:83
  87.4 3.9 fusion.16.k_ref
  91.3 2.5 fusion.17.q_ref
  93.9 2.5 fusion.18.v_ref
  96.4 34.4 %shard_map.199 = bf16[1024,768]{1,0:T(8,128)(2,1)} custom-call(s32[2,512,1]{2,1,0:T(8,128)} %fusion.26.seg_col, s32[2,1,512]{2,1,0:T(1,128)} %compare_select_fusion.seg_row, bf16[1024,768]{1,0:T(8,128)(2,1)} %fusion.17.q_ref, bf16[1024,768]{1,0:T(8,128)(2,1)} %fusion.16.k_ref, bf16[1024,768]{1,0:T(8,128)(2,1)} %fusion.18.v_ref), custom_call_target="tpu_custom_call" | custom-call | flops 1610612736 | bytes 6291456 | tf_op jit(solution)/shard_map/pallas_call | solution.py:577
  130.8 3.4 fusion.53
  134.8 9.5 %multiply_convert_fusion.1 = (bf16[1024,3072]{1,0:T(8,128)(2,1)S(1)}, f32[1024,3072]{1,0:T(8,128)}) fusion(f32[3072]{0:T(1024)S(1)} %slice.36, bf16[768,3072]{1,0:T(8,128)(2,1)S(1)} %bitcast.193, f32[1024,768]{1,0:T(8,128)S(1)} %get-tuple-element.59, f32[768]{0:T(1024)S(1)} %get-tuple-element.50, f32[768]{0:T(1024)S(1)} %get-tuple-element.51, ...), kind=kOutput, calls=%fused_computation.10 | convolution fusion | flops 4854644736 | bytes 26765312 | tf_op jit(solution)/shard_map/dot_general | solution.py:665
  144.4 5.4 %fusion.54 = (f32[1024]{0:T(1024)S(1)}, f32[1024,768]{1,0:T(8,128)S(1)}) fusion(f32[768]{0:T(1024)S(1)} %get-tuple-element.48, bf16[1024,3072]{1,0:T(8,128)(2,1)S(1)} %get-tuple-element.60, bf16[3072,768]{1,0:T(8,128)(2,1)S(1)} %bitcast.197, f32[768]{0:T(1024)S(1)} %get-tuple-element.50, f32[768]{0:T(1024)S(1)} %get-tuple-element.51, ...), kind=kOutput, calls=%fused_computation.149 | convolution fusion | flops 4837342208 | bytes 17323008 | tf_op jit(solution)/shard_map/dot_general | solution.py:668
  150.5 2.8 fusion.51
  153.3 1.4 gather_fusion
  154.9 0.9 collective-permute-done
  157.1 2.1 convert_multiply_fusion
  159.5 2.2 scatter_fusion
  161.8 3.9 fusion.7
  166.4 1.6 fusion.50
  168.7 7.0 %multiply_convert_fusion.2 = bf16[3072,768]{1,0:T(8,128)(2,1)} fusion(bf16[1024,3072]{1,0:T(8,128)(2,1)S(1)} %bitcast.208, bf16[1024,768]{1,0:T(8,128)(2,1)S(1)} %get-tuple-element.35), kind=kOutput, calls=%fused_computation.12 | convolution fusion | flops 4836556800 | bytes 12582912 | tf_op jit(solution)/shard_map/tf,td->fd/dot_general | solution.py:702
  175.8 12.4 %convert_reduce_fusion = (f32[3072]{0:T(1024)S(1)}, bf16[1024,3072]{1,0:T(8,128)(2,1)S(1)}) fusion(f32[1024,3072]{1,0:T(8,128)} %get-tuple-element.61, f32[3072]{0:T(1024)S(1)} %slice.36, bf16[1024,768]{1,0:T(8,128)(2,1)S(1)} %get-tuple-element.35, bf16[3072,768]{1,0:T(8,128)(2,1)S(1)} %bitcast.199), kind=kOutput, calls=%fused_computation.8 | convolution fusion | flops 4879021056 | bytes 25190400 | tf_op jit(solution)/shard_map/td,fd->tf/dot_general | solution.py:705
  188.2 6.1 %multiply_reduce_fusion = (f32[768]{0:T(1024)S(1)}, f32[1024]{0:T(1024)S(1)}, f32[768]{0:T(1024)S(1)}, f32[1024,768]{1,0:T(8,128)S(1)}) fusion(f32[1024,768]{1,0:T(8,128)S(1)} %copy-done.7, f32[1024]{0:T(1024)S(1)} %fusion.35, f32[1024]{0:T(1024)S(1)} %broadcast_multiply_fusion.1, f32[768]{0:T(1024)S(1)} %get-tuple-element.51, ...), kind=kOutput, calls=%fused_computation.28 | convolution fusion | flops 4839699456 | bytes 20472832 | tf_op jit(solution)/shard_map/tf,df->td/dot_general | solution.py:711
  194.2 8.0 %multiply_convert_fusion.3 = bf16[768,3072]{1,0:T(8,128)(2,1)} fusion(bf16[1024,3072]{1,0:T(8,128)(2,1)S(1)} %get-tuple-element.68, f32[1024,768]{1,0:T(8,128)S(1)} %copy-done.7, f32[768]{0:T(1024)S(1)} %get-tuple-element.50, f32[768]{0:T(1024)S(1)} %get-tuple-element.51, f32[1024]{0:T(1024)S(1)} %fusion.35, f32[1024]{0:T(1024)S(1)} %broadcast_multiply_fusion.1), kind=kOutput, calls=%fused_computation.13 | convolution fusion | flops 4840488960 | bytes 14170112 | tf_op jit(solution)/shard_map/td,tf->df/dot_general | solution.py:708
  202.3 1.4 fusion.49
  203.8 1.6 copy-done.4
  205.7 1.1 copy-done.19
  206.9 2.6 convolution_convert_fusion.1.g_ref
  209.4 36.4 %shard_map.200 = (bf16[1024,768]{1,0:T(8,128)(2,1)}, bf16[1024,768]{1,0:T(8,128)(2,1)}, bf16[1024,768]{1,0:T(8,128)(2,1)}) custom-call(s32[2,512,1]{2,1,0:T(8,128)} %fusion.26.seg_col, s32[2,1,512]{2,1,0:T(1,128)} %compare_select_fusion.seg_row, bf16[1024,768]{1,0:T(8,128)(2,1)} %fusion.17.q_ref, bf16[1024,768]{1,0:T(8,128)(2,1)} %fusion.16.k_ref, ...), custom_call_target="tpu_custom_call" | custom-call | flops 4026531840 | bytes 11010048 | tf_op jit(solution)/shard_map/pallas_call | solution.py:577
  245.8 4.5 %multiply_convert_fusion.7 = bf16[768,768]{0,1:T(8,128)(2,1)} fusion(bf16[1024,768]{1,0:T(8,128)(2,1)} %get-tuple-element.23, bf16[1024,768]{1,0:T(8,128)(2,1)} %bitcast.200), kind=kOutput, calls=%fused_computation.50 | convolution fusion | flops 1209139200 | bytes 4325376 | tf_op jit(solution)/shard_map/td,te->de/dot_general | solution.py:730
  250.8 0.9 copy-done.30
  251.7 2.5 multiply_convert_fusion.5
  254.2 2.1 reduce_sum.198
  257.1 4.5 %multiply_convert_fusion.6 = bf16[768,768]{0,1:T(8,128)(2,1)} fusion(bf16[1024,768]{1,0:T(8,128)(2,1)} %get-tuple-element.24, bf16[1024,768]{1,0:T(8,128)(2,1)} %bitcast.201), kind=kOutput, calls=%fused_computation.49 | convolution fusion | flops 1209139200 | bytes 4325376 | tf_op jit(solution)/shard_map/td,te->de/dot_general | solution.py:733
  261.6 3.1 fusion.57
  264.7 13.7 %shard_map.203 = f32[72,128]{1,0:T(8,128)} custom-call(f32[72,128]{1,0:T(8,128)} %multiply_bitcast_fusion.part_ref), custom_call_target="tpu_custom_call" | custom-call | flops 46080 | bytes 368640 | tf_op jit(solution)/shard_map/pallas_call | solution.py:460
  278.4 1.9 dynamic-slice_bitcast_fusion.3
  280.3 3.3 collective-permute-start.3
  283.6 2.0 dynamic-slice_bitcast_fusion.2
  285.6 1.9 dynamic-slice_bitcast_fusion.4
  288.1 3.3 dynamic-slice_bitcast_fusion.1
  291.4 3.5 dynamic-slice_bitcast_fusion
  296.2 1.4 fusion.56
  298.1 1.0 copy-done.9
  299.3 3.1 add_add_fusion.2
  302.4 2.5 multiply_convert_fusion.4
  304.9 3.0 reshape.331
  307.9 3.9 constant_dynamic-slice_fusion.1
  311.7 3.4 copy.75
  315.1 3.4 copy.57
  318.6 2.3 fusion.21
  321.0 2.2 fusion.22
  323.2 2.0 fusion.20
  325.2 1.0 fusion.19
  326.2 4.5 %fusion.5 = bf16[12,128,768]{2,1,0:T(8,128)(2,1)} fusion(bf16[12,128,768]{2,1,0:T(8,128)(2,1)} %collective-permute-done.7, bf16[12,2,128,768]{3,2,1,0:T(8,128)(2,1)} %bitcast.164, s32[]{:T(128)S(6)} %select_n.79), kind=kLoop, calls=%fused_computation.17 | loop fusion | flops 4718592 | bytes 7077892 | tf_op jit(solution)/shard_map/convert_element_type | solution.py:486
  330.7 4.0 fusion.6
  335.4 6.8 %shard_map.201 = bf16[112,128,256]{2,1,0:T(8,128)(2,1)} custom-call(s32[108]{0:T(128)} %slot_ref.3, bf16[128,256]{1,0:T(8,128)(2,1)} %broadcast_in_dim.38.zero_ref, bf16[384,768]{1,0:T(8,128)(2,1)} %bitcast.173, bf16[384,768]{1,0:T(8,128)(2,1)} %bitcast.172, bf16[384,768]{1,0:T(8,128)(2,1)} %bitcast.174, bf16[384,768]{1,0:T(8,128)(2,1)} %bitcast.171, ...), custom_call_target="tpu_custom_call" | custom-call | bytes 14680064 | tf_op jit(solution)/shard_map/pallas_call | solution.py:126
  342.2 71.6 %shard_map.202 = bf16[7,128,256]{2,1,0:T(8,128)(2,1)} custom-call(bf16[16,7,128,256]{3,2,1,0:T(8,128)(2,1)} %bitcast.160), custom_call_target="tpu_custom_call" | custom-call | tf_op jit(solution)/shard_map/pallas_call | solution.py:412
  413.8 5.1 %all_gather.3 = bf16[7,256,256]{2,1,0:T(8,128)(2,1)S(1)} all-gather(bf16[7,128,256]{2,1,0:T(8,128)(2,1)} %shard_map.202), channel_id=1, replica_groups=mesh['pair'=2,'dp'=16] {'pair'}, dimensions={1}, use_global_device_ids=true | all-gather | bytes 1376256 | tf_op jit(solution)/shard_map/all_gather | solution.py:771
  418.9 1.4 convert_element_type.263
  420.3 1.8 fusion.58
  422.2 2.3 multiply_add_fusion.2
  424.5 2.9 fusion.10
  427.5 3.4 multiply_subtract_fusion
  (162 shorter events, 14.0 us)
Async XLA Ops:
  0.6 421.5 %copy-start = (f32[7,256,256]{2,1,0:T(8,128)S(1)}, f32[7,256,256]{2,1,0:T(8,128)}, u32[]{:S(2)}) copy-start(f32[7,256,256]{2,1,0:T(8,128)} %param.24) | copy-start | bytes 5505028
  76.2 11.2 %copy-start.29 = (bf16[1,2,512,768]{3,2,1,0:T(8,128)(2,1)S(1)}, bf16[1,2,512,768]{3,2,1,0:T(8,128)(2,1)}, u32[]{:S(2)}) copy-start(bf16[1,2,512,768]{3,2,1,0:T(8,128)(2,1)} %param.14) | copy-start | bytes 4718596
  87.4 3.9 copy-start.31
  91.3 2.5 copy-start.21
  130.8 4.0 slice-start.2
  130.8 4.0 slice-start.3
  134.2 10.1 %copy-start.6 = (f32[1024,768]{1,0:T(8,128)}, f32[1024,768]{1,0:T(8,128)S(1)}, u32[]{:S(2)}) copy-start(f32[1024,768]{1,0:T(8,128)S(1)} %get-tuple-element.59) | copy-start | bytes 9437188
  134.3 10.1 %slice-start.6 = ((s8[4718592]{0:T(1024)(128)(4,1)}), s8[4194304]{0:T(1024)(128)(4,1)S(1)}, s32[]{:S(2)}) async-start(s8[4718592]{0:T(1024)(128)(4,1)} %bitcast.196), calls=%async_computation.6 | async-start | bytes 8388608
  134.8 9.6 %slice-start.7 = ((s8[4718592]{0:T(1024)(128)(4,1)}), s8[524288]{0:T(1024)(128)(4,1)S(1)}, s32[]{:S(2)}) async-start(s8[4718592]{0:T(1024)(128)(4,1)} %bitcast.196), calls=%async_computation.7 | async-start | bytes 1048576
  144.4 5.5 %copy-start.37 = (bf16[1024,3072]{1,0:T(8,128)(2,1)}, bf16[1024,3072]{1,0:T(8,128)(2,1)S(1)}, u32[]{:S(2)}) copy-start(bf16[1024,3072]{1,0:T(8,128)(2,1)S(1)} %get-tuple-element.60) | copy-start | bytes 18874372
  149.9 3.4 copy-start.2
  150.4 5.7 %copy-start.28 = (s32[1,1,8]{2,1,0:T(1,128)S(1)}, s32[1,1,8]{2,1,0:T(1,128)}, u32[]{:S(2)}) copy-start(s32[1,1,8]{2,1,0:T(1,128)} %param.18) | copy-start | bytes 100
  150.5 6.7 %copy-start.18 = (bf16[1,2,512,768]{3,2,1,0:T(8,128)(2,1)S(1)}, bf16[1,2,512,768]{3,2,1,0:T(8,128)(2,1)}, u32[]{:S(2)}) copy-start(bf16[1,2,512,768]{3,2,1,0:T(8,128)(2,1)} %param.15) | copy-start | bytes 4718596
  154.7 1.2 collective-permute-start
  157.0 2.3 collective-permute-start.1
  161.7 4.0 copy-start.1
  161.7 4.7 %copy-start.3 = (f32[1024,768]{1,0:T(8,128)S(1)}, f32[1024,768]{1,0:T(8,128)}, u32[]{:S(2)}) copy-start(f32[1024,768]{1,0:T(8,128)} %copy-done.2) | copy-start | bytes 9437188
  165.7 2.7 slice-start.10
  166.4 2.3 slice-start.11
  168.0 7.7 %slice-start.8 = ((s8[4718592]{0:T(1024)(128)(4,1)}), s8[4194304]{0:T(1024)(128)(4,1)S(1)}, s32[]{:S(2)}) async-start(s8[4718592]{0:T(1024)(128)(4,1)} %bitcast.198), calls=%async_computation.8 | async-start | bytes 8388608
  168.7 7.0 %slice-start.9 = ((s8[4718592]{0:T(1024)(128)(4,1)}), s8[524288]{0:T(1024)(128)(4,1)S(1)}, s32[]{:S(2)}) async-start(s8[4718592]{0:T(1024)(128)(4,1)} %bitcast.198), calls=%async_computation.9 | async-start | bytes 1048576
  168.7 19.4 %slice-start.4 = ((s8[4718592]{0:T(1024)(128)(4,1)}), s8[4194304]{0:T(1024)(128)(4,1)S(1)}, s32[]{:S(2)}) async-start(s8[4718592]{0:T(1024)(128)(4,1)} %bitcast.194), calls=%async_computation.4 | async-start | bytes 8388608
  175.7 12.4 %copy-start.7 = (f32[1024,768]{1,0:T(8,128)S(1)}, f32[1024,768]{1,0:T(8,128)}, u32[]{:S(2)}) copy-start(f32[1024,768]{1,0:T(8,128)} %copy-done.6) | copy-start | bytes 9437188
  175.7 12.4 %slice-start.5 = ((s8[4718592]{0:T(1024)(128)(4,1)}), s8[524288]{0:T(1024)(128)(4,1)S(1)}, s32[]{:S(2)}) async-start(s8[4718592]{0:T(1024)(128)(4,1)} %bitcast.194), calls=%async_computation.5 | async-start | bytes 1048576
  203.7 1.6 copy-start.4
  203.7 3.1 copy-start.34
  205.7 1.2 copy-start.19
  245.8 4.5 %copy-start.8 = (bf16[1024,768]{1,0:T(8,128)(2,1)S(1)}, bf16[1024,768]{1,0:T(8,128)(2,1)}, u32[]{:S(2)}) copy-start(bf16[1024,768]{1,0:T(8,128)(2,1)} %get-tuple-element.25) | copy-start | bytes 4718596
  245.8 4.5 %copy-start.16 = (bf16[1024,768]{1,0:T(8,128)(2,1)S(1)}, bf16[1024,768]{1,0:T(8,128)(2,1)}, u32[]{:S(2)}) copy-start(bf16[1024,768]{1,0:T(8,128)(2,1)} %get-tuple-element.23) | copy-start | bytes 4718596
  250.3 1.4 copy-start.30
  257.1 4.5 %copy-start.33 = (bf16[768,768]{1,0:T(8,128)(2,1)S(1)}, bf16[768,768]{1,0:T(8,128)(2,1)}, u32[]{:S(2)}) copy-start(bf16[768,768]{1,0:T(8,128)(2,1)} %get-tuple-element.18) | copy-start | bytes 3538948
  257.1 4.5 %copy-start.35 = (bf16[1024,768]{1,0:T(8,128)(2,1)S(1)}, bf16[1024,768]{1,0:T(8,128)(2,1)}, u32[]{:S(2)}) copy-start(bf16[1024,768]{1,0:T(8,128)(2,1)} %get-tuple-element.24) | copy-start | bytes 4718596
  280.3 38.3 %collective-permute-start.3 = (bf16[3,128,768]{2,1,0:T(8,128)(2,1)}, bf16[3,128,768]{2,1,0:T(8,128)(2,1)}, u32[]{:S(2)}, u32[]{:S(2)}) collective-permute-start(bf16[3,128,768]{2,1,0:T(8,128)(2,1)} %dynamic-slice_bitcast_fusion.3), channel_id=1, source_target_pairs={{0,16},{16,0},{1,17},{17,1},{2,18},{18,2},{3,19},{19,3},{4,20},{20... | collective-permute-start | bytes 1769480 | tf_op jit(solution)/shard_map/ppermute | solution.py:31
  287.5 33.5 %collective-permute-start.2 = (bf16[3,128,768]{2,1,0:T(8,128)(2,1)}, bf16[3,128,768]{2,1,0:T(8,128)(2,1)}, u32[]{:S(2)}, u32[]{:S(2)}) collective-permute-start(bf16[3,128,768]{2,1,0:T(8,128)(2,1)} %dynamic-slice_bitcast_fusion.4), channel_id=1, source_target_pairs={{0,16},{16,0},{1,17},{17,1},{2,18},{18,2},{3,19},{19,3},{4,20},{20... | collective-permute-start | bytes 1769480 | tf_op jit(solution)/shard_map/ppermute | solution.py:31
  287.6 35.6 %collective-permute-start.4 = (bf16[3,128,768]{2,1,0:T(8,128)(2,1)}, bf16[3,128,768]{2,1,0:T(8,128)(2,1)}, u32[]{:S(2)}, u32[]{:S(2)}) collective-permute-start(bf16[3,128,768]{2,1,0:T(8,128)(2,1)} %dynamic-slice_bitcast_fusion.2), channel_id=1, source_target_pairs={{0,16},{16,0},{1,17},{17,1},{2,18},{18,2},{3,19},{19,3},{4,20},{20... | collective-permute-start | bytes 1769480 | tf_op jit(solution)/shard_map/ppermute | solution.py:31
  291.4 4.0 copy-start.24
  291.4 4.0 copy-start.25
  291.4 4.0 copy-start.26
  291.4 4.0 copy-start.27
  291.4 4.8 %copy-start.17 = (bf16[1024,768]{1,0:T(8,128)(2,1)S(1)}, bf16[1024,768]{1,0:T(8,128)(2,1)}, u32[]{:S(2)}) copy-start(bf16[1024,768]{1,0:T(8,128)(2,1)} %get-tuple-element.23) | copy-start | bytes 4718596
  291.4 4.8 %copy-start.32 = (bf16[768,768]{1,0:T(8,128)(2,1)S(1)}, bf16[768,768]{1,0:T(8,128)(2,1)}, u32[]{:S(2)}) copy-start(bf16[768,768]{1,0:T(8,128)(2,1)} %get-tuple-element.17) | copy-start | bytes 3538948
  294.9 31.3 %collective-permute-start.7 = (bf16[12,128,768]{2,1,0:T(8,128)(2,1)}, bf16[12,128,768]{2,1,0:T(8,128)(2,1)}, u32[]{:S(2)}, u32[]{:S(2)}) collective-permute-start(bf16[12,128,768]{2,1,0:T(8,128)(2,1)} %dynamic-slice_bitcast_fusion), channel_id=1, source_target_pairs={{0,16},{16,0},{1,17},{17,1},{2,18},{18,2},{3,19},{19,3},{4,20},{20... | collective-permute-start | bytes 7077896 | tf_op jit(solution)/shard_map/ppermute | solution.py:31
  294.9 35.8 %collective-permute-start.6 = (bf16[3,128,3072]{2,1,0:T(8,128)(2,1)}, bf16[3,128,3072]{2,1,0:T(8,128)(2,1)}, u32[]{:S(2)}, u32[]{:S(2)}) collective-permute-start(bf16[3,128,3072]{2,1,0:T(8,128)(2,1)} %dynamic-slice_bitcast_fusion.1), channel_id=1, source_target_pairs={{0,16},{16,0},{1,17},{17,1},{2,18},{18,2},{3,19},{19,3},{4,20},{20... | collective-permute-start | bytes 7077896 | tf_op jit(solution)/shard_map/ppermute | solution.py:31
  296.2 1.9 copy-start.5
  296.2 2.8 copy-start.9
  296.2 3.1 copy-start.22
  299.3 3.1 copy-start.20
  299.3 3.1 copy-start.36
  318.5 4.7 %copy-start.23 = (bf16[768,768]{0,1:T(8,128)(2,1)S(1)}, bf16[768,768]{0,1:T(8,128)(2,1)}, u32[]{:S(2)}) copy-start(bf16[768,768]{0,1:T(8,128)(2,1)} %multiply_convert_fusion.5) | copy-start | bytes 3538948
  318.6 6.7 %collective-permute-start.5 = (bf16[3,128,768]{2,1,0:T(8,128)(2,1)S(1)}, bf16[3,128,768]{2,1,0:T(8,128)(2,1)S(1)}, u32[]{:S(2)}, u32[]{:S(2)}) collective-permute-start(bf16[3,128,768]{2,1,0:T(8,128)(2,1)S(1)} %bitcast.182), channel_id=1, source_target_pairs={{0,16},{16,0},{1,17},{17,1},{2,18},{18,2},{3,19},{19,3},{4,20},{20... | collective-permute-start | bytes 1769480 | tf_op jit(solution)/shard_map/ppermute | solution.py:31
  318.6 12.0 %slice-start = ((s8[4718592]{0:T(1024)(128)(4,1)}), s8[4194304]{0:T(1024)(128)(4,1)S(1)}, s32[]{:S(2)}) async-start(s8[4718592]{0:T(1024)(128)(4,1)} %bitcast.166), calls=%async_computation | async-start | bytes 8388608
  325.2 5.5 %slice-start.1 = ((s8[4718592]{0:T(1024)(128)(4,1)}), s8[524288]{0:T(1024)(128)(4,1)S(1)}, s32[]{:S(2)}) async-start(s8[4718592]{0:T(1024)(128)(4,1)} %bitcast.166), calls=%async_computation.1 | async-start | bytes 1048576
  413.8 6.6 %copy-start.11 = (f32[7,256,256]{2,1,0:T(8,128)S(1)}, f32[7,256,256]{2,1,0:T(8,128)}, u32[]{:S(2)}) copy-start(f32[7,256,256]{2,1,0:T(8,128)} %param.23) | copy-start | bytes 5505028
  418.9 3.2 copy-start.12
  418.9 3.2 copy-start.13
  424.5 3.0 copy-start.14
  424.5 3.0 copy-start.15
  424.5 3.0 copy-start.10

commit v5 on v4

--- a/solution.py
+++ b/solution.py
@@ -421,6 +421,64 @@
         ],
         compiler_params=pltpu.CompilerParams(collective_id=2, has_side_effects=True),
     )(pieces)
+
+
+def pair_body(half, count, *refs):
+    mats, outs, lands = refs[:count], refs[count : 2 * count], refs[2 * count : 3 * count]
+    send_sem, recv_sem, own_sem = refs[3 * count :]
+    core, me = lax.axis_index("pair"), lax.axis_index("dp")
+    target = (1 - core, me)
+    barrier = pltpu.get_barrier_semaphore()
+    pl.semaphore_signal(barrier, inc=1, device_id=target, device_id_type=MESH_IDS)
+    pl.semaphore_wait(barrier, 1)
+    stripes = []
+    for index in range(count):
+        for row in range(outs[index].shape[0] // half):
+            number = len(stripes)
+            here = pl.ds(row * half, half)
+
+            def rows_of(part, row=row):
+                return pl.ds(pl.multiple_of((2 * row + part) * half, half), half)
+
+            remote = pltpu.make_async_remote_copy(
+                src_ref=mats[index].at[rows_of(1 - core)],
+                dst_ref=lands[index].at[here],
+                send_sem=send_sem.at[number],
+                recv_sem=recv_sem.at[number],
+                device_id=target,
+                device_id_type=MESH_IDS,
+            )
+            remote.start()
+            own = pltpu.make_async_copy(
+                mats[index].at[rows_of(core)], outs[index].at[here], own_sem.at[number]
+            )
+            own.start()
+            stripes.append((index, row, remote, own))
+    for index, row, remote, own in stripes:
+        own.wait()
+        remote.wait()
+        out, land = outs[index], lands[index]
+
+        @pl.loop(0, half // 16)
+        def _(step, out=out, land=land, row=row):
+            rows = pl.ds(pl.multiple_of(row * half + step * 16, 16), 16)
+            total = out[rows, :].astype(jnp.float32) + land[rows, :].astype(jnp.float32)
+            out[rows, :] = total.astype(out.dtype)
+
+
+def pair_summed(mats, half):
+    count = len(mats)
+    shapes = [(matrix.shape[0] // 2, matrix.shape[1]) for matrix in mats]
+    stripes = sum(shape[0] // half for shape in shapes)
+    return pl.pallas_call(
+        functools.partial(pair_body, half, count),
+        in_specs=[pl.BlockSpec(memory_space=pl.ANY)] * count,
+        out_specs=[pl.BlockSpec(memory_space=pltpu.VMEM)] * count,
+        out_shape=[jax.ShapeDtypeStruct(shape, mats[0].dtype) for shape in shapes],
+        scratch_shapes=[pltpu.VMEM(shape, mats[0].dtype) for shape in shapes]
+        + [pltpu.SemaphoreType.DMA((stripes,))] * 3,
+        compiler_params=pltpu.CompilerParams(collective_id=3, has_side_effects=True),
+    )(*mats)
 
 
 def vector_body(rounds, part_ref, total_ref, held, landed, send_sem, recv_sem):
@@ -475,17 +533,6 @@
     )(part.reshape(shape)).reshape(-1)
 
 
-def pair_summed(gradient, scale, block_side, core):
-    halves = lax.axis_size("pair")
-    half = block_side // halves
-    gradient = (gradient * scale).astype(jnp.bfloat16)
-    parts = gradient.reshape(-1, halves, half, gradient.shape[1])
-    sent = lax.dynamic_index_in_dim(parts, 1 - core, axis=1, keepdims=False)
-    kept = lax.dynamic_index_in_dim(parts, core, axis=1, keepdims=False)
-    total = kept.astype(jnp.float32) + swapped(sent, "pair", 0).astype(jnp.float32)
-    return total.astype(jnp.bfloat16).reshape(-1, gradient.shape[1])
-
-
 def soap_update(gradient, weight, moment_one, moment_two, left_basis, right_basis):
     rotated = jnp.matmul(
         jnp.matmul(jnp.swapaxes(left_basis, -1, -2), gradient, precision=HIGHEST),
@@ -529,13 +576,15 @@
     factor = 1.0 / math.sqrt(head_dim)
     for start in range(0, q_ref.shape[1], head_dim):
         lanes = slice(start, start + head_dim)
-        scores = scores_of(q_ref[:, lanes], k_ref[:, lanes])
+        scores = scores_of(k_ref[:, lanes], q_ref[:, lanes])
         scores = jnp.where(allowed, scores * factor, -1e30)
-        top = jnp.max(scores, axis=1, keepdims=True)
+        top = jnp.max(scores, axis=0, keepdims=True)
         weights = jnp.exp(scores - top)
-        total = jnp.sum(weights, axis=1, keepdims=True)
+        total = jnp.sum(weights, axis=0, keepdims=True)
         probs = (weights * (1.0 / total)).astype(jnp.bfloat16)
-        mixed = jnp.dot(probs, v_ref[:, lanes], preferred_element_type=jnp.float32)
+        mixed = lax.dot_general(
+            probs, v_ref[:, lanes], (((0,), (0,)), ((), ())), preferred_element_type=jnp.float32
+        )
         o_ref[:, lanes] = mixed.astype(o_ref.dtype)
 
 
@@ -759,12 +808,15 @@
         )
         * grad_scale
     )
-    grad_mats = [
-        pair_summed(matrix, grad_scale, block_side, core)
-        for matrix in (
-            grad_w_query, grad_w_key, grad_w_value, grad_w_output, grad_w_inner, grad_w_outer
-        )
-    ]
+    grad_mats = pair_summed(
+        [
+            (matrix * grad_scale).astype(jnp.bfloat16)
+            for matrix in (
+                grad_w_query, grad_w_key, grad_w_value, grad_w_output, grad_w_inner, grad_w_outer
+            )
+        ],
+        half,
+    )
     own_grad = deal(grad_mats, owner_slot, master.shape[0] * data_count, half, block_side)
     vector_grad = vector_total(local_vector, data_count, pair_count)
     own_grad = fold(own_grad, data_count, pair_count)

time: 441 us -> 400 us (0.907)
  local copies, waits for them, and re-layouts: 40.4 us -> 18.2 us
  other arithmetic: 41.3 us -> 25.3 us
  starting transfers between devices: 4.79 us -> 0.34 us
    pallas_call x0 -> x1, Pallas kernels: none -> 18.1 us  [pair_summed(): pl.pallas_call(functools.partial(pair_body, half, count), in_specs=[pl.Bl...]
    convert_element_type x6 -> x0, other arithmetic: 16 us -> none  [pair_summed(): return total.astype(jnp.bfloat16).reshape(-1, gradient.shape[1])]
    pallas_call x2, Pallas kernels: 70.7 us -> 55.7 us  [attention_call(): pl.pallas_call(functools.partial(body, D // HEADS), grid=(rows, width //...]
    squeeze x5 -> x0, local copies, waits for them, and re-layouts: 12.6 us -> none  [pair_summed(): sent = lax.dynamic_index_in_dim(parts, 1 - core, axis=1, keepdims=False)]
    dynamic_slice x2 -> x0, local copies, waits for them, and re-layouts: 7.27 us -> none  [the longest x1 3.88 us: pair_summed(): kept = lax.dynamic_index_in_dim(parts, core, axis=1, keepdims=False)]
    convert_element_type x0 -> x3, local copies, waits for them, and re-layouts: none -> 7.12 us  [per_device(): (matrix * grad_scale).astype(jnp.bfloat16)]
    unnamed x110 -> x99, local copies, waits for them, and re-layouts: 10.6 us -> 4.11 us
    ppermute x8 -> x2, starting transfers between devices: 4.79 us -> 0.34 us  [swapped(): lax.ppermute(array, axis, [(i, i ^ 1 << stride) for i in range(lax.axis_s...]
  transfers between devices with their start and end apart: 8 -> 2, of which waited for: 1 -> 1; matrix products, arithmetic and copies ran while one was open for 11% -> 1% of each run, Pallas kernels for 0% -> 0%
where the time goes in v5:
time: 400 us; the launch traced here: 392 us
  Pallas kernels  244 us (61%)
  matrix products  97.1 us (24%)
  other arithmetic  25.3 us (6%)
  local copies, waits for them, and re-layouts  18.2 us (5%)
  blocking collectives  4.95 us (1%)
    pallas_call x1, Pallas kernels, fold(): pl.pallas_call(fold_body, in_specs=[pl.BlockSpec(memory_space=pltpu.VMEM)...  71.7 us
    pallas_call x1, Pallas kernels, spread(): pl.pallas_call(spread_body, in_specs=[pl.BlockSpec(memory_space=pl.ANY)],...  66.8 us
    pallas_call x2, Pallas kernels, attention_call(): pl.pallas_call(functools.partial(body, D // HEADS), grid=(rows, width //...  55.7 us
    pallas_call x1, Pallas kernels, pair_summed(): pl.pallas_call(functools.partial(pair_body, half, count), in_specs=[pl.Bl...  18.1 us
    pallas_call x1, Pallas kernels, vector_total(): pl.pallas_call(functools.partial(vector_body, rounds), in_specs=[pl.Block...  13.7 us
    dot_general x1, matrix products, per_device(): jnp.einsum('td,fd->tf', grad_outer, w_outer, preferred_element_type=jnp.f...  12 us
    pallas_call x1, Pallas kernels, assemble(): pl.pallas_call(functools.partial(assemble_body, gathered.shape[1], halves...  11.1 us
    dot_general x1, matrix products, per_device(): jnp.dot(normed_low, w_inner, preferred_element_type=jnp.float32)  9.73 us
  transfers between devices with their start and end apart: 2, of which 1 were waited for; matrix products, arithmetic and copies ran while one was open for 1% of the time, Pallas kernels for 0%

profile of v5, /device:TPU:17, one launch (start us, length us, event | category | flops | bytes accessed | tf_op | source)
XLA Modules:
  0.0 392.4 jit_solution(16583207731332450778)
XLA Ops:
  0.7 0.9 squeeze.10
  1.5 0.8 reduce_window_sum.15
  2.5 0.7 fusion.36
  3.2 0.7 slice.36
  3.9 0.8 fusion.49
  4.7 0.7 subtract_bitcast_fusion
  5.6 0.7 compare_select_fusion.seg_row
  6.5 0.9 fusion.23.seg_col
  7.4 2.0 dynamic-slice_convert_fusion.own_ref
  9.4 66.8 %shard_map.197.gathered_ref = bf16[32,7,128,256]{3,2,1,0:T(8,128)(2,1)} custom-call(bf16[7,128,256]{2,1,0:T(8,128)(2,1)} %dynamic-slice_convert_fusion.own_ref), custom_call_target="tpu_custom_call" | custom-call | tf_op jit(solution)/shard_map/pallas_call | solution.py:252
  76.2 11.1 %shard_map.198 = (bf16[768,768]{1,0:T(8,128)(2,1)}, bf16[768,768]{1,0:T(8,128)(2,1)}, bf16[768,768]{1,0:T(8,128)(2,1)}, bf16[768,768]{1,0:T(8,128)(2,1)}, bf16[7...) custom-call(s32[108]{0:T(128)} %slot_ref.3, bf16[32,7,128,256]{3,2,1,0:T(8,128)(2,1)} %shard_map.197.gathered_ref), custom_call_target="tpu_custom_call" | custom-call | bytes 29360128 | tf_op jit(solution)/shard_map/pallas_call | solution.py:83
  87.4 3.9 fusion.14.k_ref
  91.3 2.5 fusion.15.q_ref
  93.8 2.5 fusion.16.v_ref
  96.4 19.1 %shard_map.199 = bf16[1024,768]{1,0:T(8,128)(2,1)} custom-call(s32[2,512,1]{2,1,0:T(8,128)} %fusion.23.seg_col, s32[2,1,512]{2,1,0:T(1,128)} %compare_select_fusion.seg_row, bf16[1024,768]{1,0:T(8,128)(2,1)} %fusion.15.q_ref, bf16[1024,768]{1,0:T(8,128)(2,1)} %fusion.14.k_ref, bf16[1024,768]{1,0:T(8,128)(2,1)} %fusion.16.v_ref), custom_call_target="tpu_custom_call" | custom-call | flops 1610612736 | bytes 6291456 | tf_op jit(solution)/shard_map/pallas_call | solution.py:626
  115.5 3.4 fusion.50
  118.9 0.5 multiply_reduce_fusion.4
  119.5 9.7 %multiply_convert_fusion.1 = (bf16[1024,3072]{1,0:T(8,128)(2,1)S(1)}, f32[1024,3072]{1,0:T(8,128)}) fusion(f32[3072]{0:T(1024)S(1)} %slice.36, bf16[768,3072]{1,0:T(8,128)(2,1)S(1)} %bitcast.122, f32[1024,768]{1,0:T(8,128)S(1)} %get-tuple-element.69, f32[768]{0:T(1024)S(1)} %get-tuple-element.60, f32[768]{0:T(1024)S(1)} %get-tuple-element.61, ...), kind=kOutput, calls=%fused_computation.10 | convolution fusion | flops 4854644736 | bytes 26765312 | tf_op jit(solution)/shard_map/dot_general | solution.py:714
  129.3 5.5 %fusion.51 = (f32[1024]{0:T(1024)S(1)}, f32[1024,768]{1,0:T(8,128)S(1)}) fusion(f32[768]{0:T(1024)S(1)} %get-tuple-element.58, bf16[1024,3072]{1,0:T(8,128)(2,1)S(1)} %get-tuple-element.70, bf16[3072,768]{1,0:T(8,128)(2,1)S(1)} %bitcast.126, f32[768]{0:T(1024)S(1)} %get-tuple-element.60, f32[768]{0:T(1024)S(1)} %get-tuple-element.61, ...), kind=kOutput, calls=%fused_computation.133 | convolution fusion | flops 4837342208 | bytes 17323008 | tf_op jit(solution)/shard_map/dot_general | solution.py:717
  134.8 0.5 multiply_reduce_fusion.3
  135.3 2.8 fusion.48
  138.1 1.4 gather_fusion
  139.8 0.9 collective-permute-done
  141.0 0.8 convolution_convert_fusion.2
  142.0 2.1 convert_multiply_fusion
  144.4 2.2 scatter_fusion
  146.6 3.9 fusion.5
  150.6 0.7 copy-done.3
  151.3 1.6 fusion.47
  152.9 0.3 convert_reduce_fusion.1
  153.6 7.0 %multiply_convert_fusion.2.refs_5_ = bf16[3072,768]{1,0:T(8,128)(2,1)} fusion(bf16[1024,3072]{1,0:T(8,128)(2,1)S(1)} %bitcast.137, bf16[1024,768]{1,0:T(8,128)(2,1)S(1)} %get-tuple-element.47), kind=kOutput, calls=%fused_computation.12 | convolution fusion | flops 4836556800 | bytes 12582912 | tf_op jit(solution)/shard_map/tf,td->fd/dot_general | solution.py:751
  160.6 12.0 %convert_reduce_fusion = (f32[3072]{0:T(1024)S(1)}, bf16[1024,3072]{1,0:T(8,128)(2,1)S(1)}) fusion(f32[1024,3072]{1,0:T(8,128)} %get-tuple-element.71, f32[3072]{0:T(1024)S(1)} %slice.36, bf16[1024,768]{1,0:T(8,128)(2,1)S(1)} %get-tuple-element.47, bf16[3072,768]{1,0:T(8,128)(2,1)S(1)} %bitcast.128), kind=kOutput, calls=%fused_computation.8 | convolution fusion | flops 4879021056 | bytes 25190400 | tf_op jit(solution)/shard_map/td,fd->tf/dot_general | solution.py:754
  172.7 6.1 %multiply_reduce_fusion = (f32[768]{0:T(1024)S(1)}, f32[1024]{0:T(1024)S(1)}, f32[768]{0:T(1024)S(1)}, f32[1024,768]{1,0:T(8,128)S(1)}) fusion(f32[1024,768]{1,0:T(8,128)S(1)} %copy-done.7, f32[1024]{0:T(1024)S(1)} %fusion.32, f32[1024]{0:T(1024)S(1)} %broadcast_multiply_fusion.1, f32[768]{0:T(1024)S(1)} %get-tuple-element.61, ...), kind=kOutput, calls=%fused_computation.24 | convolution fusion | flops 4839699456 | bytes 20472832 | tf_op jit(solution)/shard_map/tf,df->td/dot_general | solution.py:760
  178.7 8.0 %multiply_convert_fusion.3.refs_4_ = bf16[768,3072]{1,0:T(8,128)(2,1)} fusion(bf16[1024,3072]{1,0:T(8,128)(2,1)S(1)} %get-tuple-element.78, f32[1024,768]{1,0:T(8,128)S(1)} %copy-done.7, f32[768]{0:T(1024)S(1)} %get-tuple-element.60, f32[768]{0:T(1024)S(1)} %get-tuple-element.61, f32[1024]{0:T(1024)S(1)} %fusion.32, f32[1024]{0:T(1024)S(1)} %broadcast_multiply_fusion.1), kind=kOutput, calls=%fused_computation.13 | convolution fusion | flops 4840488960 | bytes 14170112 | tf_op jit(solution)/shard_map/td,tf->df/dot_general | solution.py:757
  186.7 1.4 fusion.46
  188.6 2.2 copy-done.33
  190.7 2.6 multiply_convert_fusion.4.refs_3_
  193.3 2.6 convolution_convert_fusion.1.g_ref
  195.9 36.6 %shard_map.200 = (bf16[1024,768]{1,0:T(8,128)(2,1)}, bf16[1024,768]{1,0:T(8,128)(2,1)}, bf16[1024,768]{1,0:T(8,128)(2,1)}) custom-call(s32[2,512,1]{2,1,0:T(8,128)} %fusion.23.seg_col, s32[2,1,512]{2,1,0:T(1,128)} %compare_select_fusion.seg_row, bf16[1024,768]{1,0:T(8,128)(2,1)} %fusion.15.q_ref, bf16[1024,768]{1,0:T(8,128)(2,1)} %fusion.14.k_ref, ...), custom_call_target="tpu_custom_call" | custom-call | flops 4026531840 | bytes 11010048 | tf_op jit(solution)/shard_map/pallas_call | solution.py:626
  232.6 4.0 %fusion.18 = bf16[768,768]{0,1:T(8,128)(2,1)} fusion(bf16[1024,768]{1,0:T(8,128)(2,1)} %get-tuple-element.30, bf16[1024,768]{1,0:T(8,128)(2,1)S(1)} %bitcast.133), kind=kOutput, calls=%fused_computation.60 | convolution fusion | flops 1209139200 | bytes 4325376 | tf_op jit(solution)/shard_map/td,te->de/dot_general | solution.py:782
  236.6 3.1 fusion.54
  239.7 2.5 fusion.17
  242.2 0.5 convert_reduce_fusion.3
  242.7 2.5 fusion.19
  245.1 2.1 reduce_sum.198
  247.4 0.6 multiply_bitcast_fusion.part_ref
  248.0 4.8 %fusion.53 = f32[1024,768]{1,0:T(8,128)} fusion(bf16[1024,768]{1,0:T(8,128)(2,1)} %get-tuple-element.29, bf16[768,768]{1,0:T(8,128)(2,1)} %get-tuple-element.23), kind=kOutput, calls=%fused_computation.135 | convolution fusion | flops 1207959552 | bytes 5898240 | tf_op jit(solution)/shard_map/te,de->td/dot_general | solution.py:786
  252.8 13.7 %shard_map.204 = f32[72,128]{1,0:T(8,128)} custom-call(f32[72,128]{1,0:T(8,128)} %multiply_bitcast_fusion.part_ref), custom_call_target="tpu_custom_call" | custom-call | flops 46080 | bytes 368640 | tf_op jit(solution)/shard_map/pallas_call | solution.py:518
  266.5 2.4 copy.43.refs_1_
  268.9 2.4 copy.42.refs_0_
  271.3 2.4 copy.44.refs_2_
  273.6 18.1 %shard_map.201 = (bf16[384,768]{1,0:T(8,128)(2,1)}, bf16[384,768]{1,0:T(8,128)(2,1)}, bf16[384,768]{1,0:T(8,128)(2,1)}, bf16[384,768]{1,0:T(8,128)(2,1)}, bf16[3...) custom-call(bf16[768,768]{1,0:T(8,128)(2,1)} %copy.42.refs_0_, bf16[768,768]{1,0:T(8,128)(2,1)} %copy.43.refs_1_, ...), custom_call_target="tpu_custom_call" | custom-call | tf_op jit(solution)/shard_map/pallas_call | solution.py:473
  291.8 0.6 broadcast_in_dim.38.zero_ref
  292.4 6.8 %shard_map.202 = bf16[112,128,256]{2,1,0:T(8,128)(2,1)} custom-call(s32[108]{0:T(128)} %slot_ref.3, bf16[128,256]{1,0:T(8,128)(2,1)} %broadcast_in_dim.38.zero_ref, bf16[384,768]{1,0:T(8,128)(2,1)} %get-tuple-element.32.refs_0_, bf16[384,768]{1,0:T(8,128)(2,1)} %get-tuple-element.33.refs_1_, bf16[384,768]{1,0:T(8,128)(2,1)} %get-tuple-element.34.refs_2_, ...), custom_call_target="tpu_custom_call" | custom-call | bytes 14680064 | tf_op jit(solution)/shard_map/pallas_call | solution.py:126
  299.2 71.7 %shard_map.203 = bf16[7,128,256]{2,1,0:T(8,128)(2,1)} custom-call(bf16[16,7,128,256]{3,2,1,0:T(8,128)(2,1)} %bitcast.108), custom_call_target="tpu_custom_call" | custom-call | tf_op jit(solution)/shard_map/pallas_call | solution.py:412
  370.9 5.0 %all_gather.3 = bf16[7,256,256]{2,1,0:T(8,128)(2,1)S(1)} all-gather(bf16[7,128,256]{2,1,0:T(8,128)(2,1)} %shard_map.203), channel_id=1, replica_groups=mesh['pair'=2,'dp'=16] {'pair'}, dimensions={1}, use_global_device_ids=true | all-gather | bytes 1376256 | tf_op jit(solution)/shard_map/all_gather | solution.py:823
  375.9 1.4 convert_element_type.164
  377.3 1.7 fusion.55
  379.1 2.2 multiply_add_fusion.2
  381.4 2.8 fusion.8
  384.3 3.4 multiply_subtract_fusion
  387.7 3.1 add_add_fusion.2
  390.9 0.8 pad_maximum_fusion
  391.6 0.6 copy.67
  (128 shorter events, 2.6 us)
Async XLA Ops:
  0.6 378.4 %copy-start = (f32[7,256,256]{2,1,0:T(8,128)S(1)}, f32[7,256,256]{2,1,0:T(8,128)}, u32[]{:S(2)}) copy-start(f32[7,256,256]{2,1,0:T(8,128)} %param.24) | copy-start | bytes 5505028
  76.2 11.2 %copy-start.26 = (bf16[1,2,512,768]{3,2,1,0:T(8,128)(2,1)S(1)}, bf16[1,2,512,768]{3,2,1,0:T(8,128)(2,1)}, u32[]{:S(2)}) copy-start(bf16[1,2,512,768]{3,2,1,0:T(8,128)(2,1)} %param.14) | copy-start | bytes 4718596
  87.4 3.9 copy-start.29
  91.3 2.5 copy-start.19
  115.5 4.0 %slice-start = ((s8[4718592]{0:T(1024)(128)(4,1)}), s8[4194304]{0:T(1024)(128)(4,1)S(1)}, s32[]{:S(2)}) async-start(s8[4718592]{0:T(1024)(128)(4,1)} %bitcast.121), calls=%async_computation | async-start | bytes 8388608
  115.5 4.0 %slice-start.1 = ((s8[4718592]{0:T(1024)(128)(4,1)}), s8[524288]{0:T(1024)(128)(4,1)S(1)}, s32[]{:S(2)}) async-start(s8[4718592]{0:T(1024)(128)(4,1)} %bitcast.121), calls=%async_computation.1 | async-start | bytes 1048576
  118.9 10.4 %copy-start.6 = (f32[1024,768]{1,0:T(8,128)}, f32[1024,768]{1,0:T(8,128)S(1)}, u32[]{:S(2)}) copy-start(f32[1024,768]{1,0:T(8,128)S(1)} %get-tuple-element.69) | copy-start | bytes 9437188
  118.9 10.3 %slice-start.4 = ((s8[4718592]{0:T(1024)(128)(4,1)}), s8[4194304]{0:T(1024)(128)(4,1)S(1)}, s32[]{:S(2)}) async-start(s8[4718592]{0:T(1024)(128)(4,1)} %bitcast.125), calls=%async_computation.4 | async-start | bytes 8388608
  119.5 9.8 %slice-start.5 = ((s8[4718592]{0:T(1024)(128)(4,1)}), s8[524288]{0:T(1024)(128)(4,1)S(1)}, s32[]{:S(2)}) async-start(s8[4718592]{0:T(1024)(128)(4,1)} %bitcast.125), calls=%async_computation.5 | async-start | bytes 1048576
  129.2 5.5 %copy-start.34 = (bf16[1024,3072]{1,0:T(8,128)(2,1)}, bf16[1024,3072]{1,0:T(8,128)(2,1)S(1)}, u32[]{:S(2)}) copy-start(bf16[1024,3072]{1,0:T(8,128)(2,1)S(1)} %get-tuple-element.70) | copy-start | bytes 18874372
  134.8 3.4 copy-start.2
  135.3 5.7 %copy-start.25 = (s32[1,1,8]{2,1,0:T(1,128)S(1)}, s32[1,1,8]{2,1,0:T(1,128)}, u32[]{:S(2)}) copy-start(s32[1,1,8]{2,1,0:T(1,128)} %param.18) | copy-start | bytes 100
  135.3 6.7 %copy-start.18 = (bf16[1,2,512,768]{3,2,1,0:T(8,128)(2,1)S(1)}, bf16[1,2,512,768]{3,2,1,0:T(8,128)(2,1)}, u32[]{:S(2)}) copy-start(bf16[1,2,512,768]{3,2,1,0:T(8,128)(2,1)} %param.15) | copy-start | bytes 4718596
  139.6 1.2 collective-permute-start
  141.9 2.3 collective-permute-start.1
  146.6 4.0 %copy-start.1 = (f32[2,512,768]{2,1,0:T(8,128)S(1)}, f32[2,512,768]{2,1,0:T(8,128)}, u32[]{:S(2)}) copy-start(f32[2,512,768]{2,1,0:T(8,128)} %scatter_fusion) | copy-start | bytes 9437188
  146.6 4.7 %copy-start.3 = (f32[1024,768]{1,0:T(8,128)S(1)}, f32[1024,768]{1,0:T(8,128)}, u32[]{:S(2)}) copy-start(f32[1024,768]{1,0:T(8,128)} %copy-done.2) | copy-start | bytes 9437188
  150.5 2.7 slice-start.8
  151.3 2.3 slice-start.9
  152.9 7.7 %slice-start.6 = ((s8[4718592]{0:T(1024)(128)(4,1)}), s8[4194304]{0:T(1024)(128)(4,1)S(1)}, s32[]{:S(2)}) async-start(s8[4718592]{0:T(1024)(128)(4,1)} %bitcast.127), calls=%async_computation.6 | async-start | bytes 8388608
  153.6 7.0 %slice-start.7 = ((s8[4718592]{0:T(1024)(128)(4,1)}), s8[524288]{0:T(1024)(128)(4,1)S(1)}, s32[]{:S(2)}) async-start(s8[4718592]{0:T(1024)(128)(4,1)} %bitcast.127), calls=%async_computation.7 | async-start | bytes 1048576
  153.6 19.0 %slice-start.2 = ((s8[4718592]{0:T(1024)(128)(4,1)}), s8[4194304]{0:T(1024)(128)(4,1)S(1)}, s32[]{:S(2)}) async-start(s8[4718592]{0:T(1024)(128)(4,1)} %bitcast.123), calls=%async_computation.2 | async-start | bytes 8388608
  160.6 12.0 %copy-start.7 = (f32[1024,768]{1,0:T(8,128)S(1)}, f32[1024,768]{1,0:T(8,128)}, u32[]{:S(2)}) copy-start(f32[1024,768]{1,0:T(8,128)} %copy-done.6) | copy-start | bytes 9437188
  160.6 12.0 %slice-start.3 = ((s8[4718592]{0:T(1024)(128)(4,1)}), s8[524288]{0:T(1024)(128)(4,1)S(1)}, s32[]{:S(2)}) async-start(s8[4718592]{0:T(1024)(128)(4,1)} %bitcast.123), calls=%async_computation.3 | async-start | bytes 1048576
  188.2 5.1 %copy-start.4 = (f32[1024,768]{1,0:T(8,128)}, f32[1024,768]{1,0:T(8,128)S(1)}, u32[]{:S(2)}) copy-start(f32[1024,768]{1,0:T(8,128)S(1)} %get-tuple-element.51) | copy-start | bytes 9437188
  188.2 2.5 copy-start.33
  190.7 2.6 copy-start.31
  195.9 36.7 %copy-start.27 = (bf16[1,2,512,768]{3,2,1,0:T(8,128)(2,1)S(1)}, bf16[1,2,512,768]{3,2,1,0:T(8,128)(2,1)}, u32[]{:S(2)}) copy-start(bf16[1,2,512,768]{3,2,1,0:T(8,128)(2,1)} %param.14) | copy-start | bytes 4718596
  232.5 4.0 %copy-start.30 = (bf16[768,768]{1,0:T(8,128)(2,1)S(1)}, bf16[768,768]{1,0:T(8,128)(2,1)}, u32[]{:S(2)}) copy-start(bf16[768,768]{1,0:T(8,128)(2,1)} %get-tuple-element.24) | copy-start | bytes 3538948
  232.6 4.0 %copy-start.32 = (bf16[1024,768]{1,0:T(8,128)(2,1)S(1)}, bf16[1024,768]{1,0:T(8,128)(2,1)}, u32[]{:S(2)}) copy-start(bf16[1024,768]{1,0:T(8,128)(2,1)} %get-tuple-element.30) | copy-start | bytes 4718596
  236.6 3.1 copy-start.17
  236.6 3.1 copy-start.28
  239.7 2.5 copy-start.8
  370.9 6.4 %copy-start.12 = (f32[7,256,256]{2,1,0:T(8,128)S(1)}, f32[7,256,256]{2,1,0:T(8,128)}, u32[]{:S(2)}) copy-start(f32[7,256,256]{2,1,0:T(8,128)} %param.23) | copy-start | bytes 5505028
  375.9 3.2 copy-start.13
  375.9 3.2 copy-start.14
  381.3 2.9 copy-start.15
  381.3 2.9 copy-start.16
  381.3 2.9 copy-start.11
  381.3 6.3 %copy-start.21 = (f32[72,128]{1,0:T(8,128)S(1)}, f32[72,128]{1,0:T(8,128)}, u32[]{:S(2)}) copy-start(f32[72,128]{1,0:T(8,128)} %shard_map.204) | copy-start | bytes 110596
  381.3 6.3 %copy-start.22 = (f32[9216]{0:T(1024)S(1)}, f32[9216]{0:T(1024)}, u32[]{:S(2)}) copy-start(f32[9216]{0:T(1024)} %param.25) | copy-start | bytes 110596
  381.4 6.3 %copy-start.23 = (f32[9216]{0:T(1024)S(1)}, f32[9216]{0:T(1024)}, u32[]{:S(2)}) copy-start(f32[9216]{0:T(1024)} %param.26) | copy-start | bytes 110596
  381.4 6.3 %copy-start.24 = (f32[9216]{0:T(1024)S(1)}, f32[9216]{0:T(1024)}, u32[]{:S(2)}) copy-start(f32[9216]{0:T(1024)} %param.27) | copy-start | bytes 110596
  381.4 6.3 %copy-start.10 = (f32[1024,768]{1,0:T(8,128)S(1)}, f32[1024,768]{1,0:T(8,128)}, u32[]{:S(2)}) copy-start(f32[1024,768]{1,0:T(8,128)} %fusion.53) | copy-start | bytes 9437188
  384.2 3.5 copy-start.5
  384.2 3.5 copy-start.9
  384.3 3.5 copy-start.20
